TPU v7x, 8 devices: a whole 2x2x1 slice. The times are simulated.
8 devices in a mesh: batch: 1 (over z), dap: 8 (over y, x, core).
Axes of the slice: x: 2, y: 2, z: 1, core: 2. Of those that a mesh axis runs over, the one named last changes fastest.
Arguments:
- pair: bfloat16 [512, 512, 128], P(('batch', 'dap'))
- pair_mask: int32 [512, 512], P(('batch', 'dap'))
- ln_in: bfloat16 [2, 2, 128], replicated
- w_proj: bfloat16 [2, 128, 512], replicated
- b_proj: bfloat16 [2, 512], replicated
- w_gate: bfloat16 [2, 128, 128], replicated
- b_gate: bfloat16 [2, 128], replicated
- ln_out: bfloat16 [2, 2, 128], replicated
- w_out: bfloat16 [2, 128, 128], replicated
- b_out: bfloat16 [2, 128], replicated
Outputs:
- output: bfloat16 [512, 512, 128], P(('batch', 'dap'))
All inputs are finite; a program needn't handle non-finite values.
Results may differ from a plain program's by a relative error of at most 0.00381369.
Values are sent between devices in bfloat16 or wider.
A program may use at most 1 GiB of HBM per device.

v0:
```python
import jax
import jax.numpy as jnp
from jax import lax
from jax.sharding import PartitionSpec as P, NamedSharding

LN_EPS = 1e-5


def norm_last(values, scale, offset):
    centred = values - jnp.mean(values, axis=-1, keepdims=True)
    variance = jnp.mean(centred * centred, axis=-1, keepdims=True)
    return centred * lax.rsqrt(variance + LN_EPS) * scale.astype(jnp.float32) + offset.astype(jnp.float32)


def norm_channels(values, scale, offset):
    centred = values - jnp.mean(values, axis=-3, keepdims=True)
    variance = jnp.mean(centred * centred, axis=-3, keepdims=True)
    return (centred * lax.rsqrt(variance + LN_EPS) * scale.astype(jnp.float32)[:, None, None]
            + offset.astype(jnp.float32)[:, None, None])


def gated_side(projected, keep_mask, channels):
    return (keep_mask * jax.nn.sigmoid(projected[channels:2 * channels]) * projected[:channels]).astype(jnp.bfloat16)


def normalize_project(pair, keep_mask, ln_in, w_proj, b_proj, channels):
    normed = norm_last(pair.astype(jnp.float32), ln_in[0], ln_in[1]).astype(jnp.bfloat16)
    projected = jnp.einsum("zc,ijz->cij", w_proj, normed, preferred_element_type=jnp.float32)
    projected = projected + b_proj.astype(jnp.float32)[:, None, None]
    left = gated_side(projected[:2 * channels], keep_mask, channels)
    right = gated_side(projected[2 * channels:], keep_mask, channels)
    return normed, left, right


def finish_layer(pair, normed, tri_sum, w_gate, b_gate, ln_out, w_out, b_out):
    tri_norm = norm_channels(tri_sum, ln_out[0], ln_out[1]).astype(jnp.bfloat16)
    update = jnp.einsum("cij,cz->ijz", tri_norm, w_out, preferred_element_type=jnp.float32) + b_out.astype(jnp.float32)
    gates = jax.nn.sigmoid(jnp.einsum("ijz,zy->ijy", normed, w_gate, preferred_element_type=jnp.float32) + b_gate.astype(jnp.float32))
    return (pair.astype(jnp.float32) + gates * update).astype(jnp.bfloat16)


def solution(mesh):
    row_spec = P(("batch", "dap"), None, None)
    mask_spec = P(("batch", "dap"), None)

    def local_layers(pair, pair_mask, ln_in, w_proj, b_proj, w_gate, b_gate, ln_out, w_out, b_out):
        channels = w_out.shape[1]
        keep_mask = pair_mask.astype(jnp.float32)[None]
        normed, left, right = normalize_project(pair, keep_mask, ln_in[0], w_proj[0], b_proj[0], channels)
        right_all = lax.all_gather(right, "dap", axis=1, tiled=True)
        tri_sum = jnp.einsum("cik,cjk->cij", left, right_all, preferred_element_type=jnp.float32)
        first = finish_layer(pair, normed, tri_sum, w_gate[0], b_gate[0], ln_out[0], w_out[0], b_out[0])
        normed, left, right = normalize_project(first, keep_mask, ln_in[1], w_proj[1], b_proj[1], channels)
        left_cols = lax.all_to_all(left, "dap", 2, 1, tiled=True)
        right_all = lax.all_gather(right, "dap", axis=1, tiled=True)
        tri_sum = jnp.einsum("cki,ckj->cij", left_cols, right_all, preferred_element_type=jnp.float32)
        return finish_layer(first, normed, tri_sum, w_gate[1], b_gate[1], ln_out[1], w_out[1], b_out[1])

    return jax.shard_map(local_layers, mesh=mesh,
                         in_specs=(row_spec, mask_spec, P(), P(), P(), P(), P(), P(), P(), P()),
                         out_specs=row_spec, check_vma=False)
```

profile of v0, /device:TPU:0, one launch (start us, length us, event | category | flops | bytes accessed | tf_op | source)
XLA Modules:
  0.0 1173.9 jit_solution(4905599222372211371)
XLA Ops:
  6.6 12.0 %copy.63 = bf16[64,512,128]{1,2,0:T(8,128)(2,1)} copy(bf16[64,512,128]{2,1,0:T(8,128)(2,1)} %param.10) | data formatting | bytes 16777216 | tf_op args[0]
  30.7 31.0 %add_bitcast_fusion.1 = f32[512,64,512]{0,2,1:T(8,128)} fusion(f32[512]{0:T(512)S(1)} %bitcast.78, bf16[2,128,512]{2,1,0:T(8,128)(2,1)S(1)} %copy-done, bf16[64,512,128]{1,2,0:T(8,128)(2,1)} %copy.63, f32[128]{0:T(128)S(1)} %get-tuple-element.16, f32[128]{0:T(128)S(1)} %get-tuple-element.17, f32[64,512]{1,0:T(8,128)S(1)} %add_rsqrt_fusion.3, ...), kind=kOutput, calls=%fused_computation.5 | convolution fusion | flops 4336910336 | bytes 75893760 | tf_op jit(solution)/shard_map/zc,ijz->cij/dot_general | solution.py:28
  61.7 28.2 %fusion.28 = (bf16[128,64,512]{0,2,1:T(8,128)(2,1)}, bf16[128,64,512]{0,2,1:T(8,128)(2,1)}) fusion(f32[512,64,512]{0,2,1:T(8,128)} %add_bitcast_fusion.1, f32[64,512]{1,0:T(8,128)S(1)} %convert_element_type.153), kind=kLoop, calls=%fused_computation.41 | loop fusion | flops 50331648 | bytes 84017152 | tf_op jit(solution)/shard_map/convert_element_type | solution.py:23
  90.0 12.0 %copy.67 = bf16[128,64,512]{2,0,1:T(8,128)(2,1)} copy(bf16[128,64,512]{0,2,1:T(8,128)(2,1)} %get-tuple-element.7) | data formatting | bytes 16777216 | tf_op jit(solution)/shard_map/convert_element_type | solution.py:23
  102.3 12.7 %copy.68 = bf16[128,64,512]{2,1,0:T(8,128)(2,1)} copy(bf16[128,64,512]{0,2,1:T(8,128)(2,1)} %get-tuple-element.8) | data formatting | bytes 16777216 | tf_op jit(solution)/shard_map/convert_element_type | solution.py:23
  116.1 12.9 %fusion.45 = f32[64,512,128]{1,2,0:T(8,128)} fusion(bf16[2,128,128]{2,1,0:T(8,128)(2,1)S(1)} %copy-done.2, bf16[64,512,128]{1,2,0:T(8,128)(2,1)} %copy.63, f32[128]{0:T(128)S(1)} %get-tuple-element.16, f32[128]{0:T(128)S(1)} %get-tuple-element.17, f32[64,512]{1,0:T(8,128)S(1)} %add_rsqrt_fusion.3, f32[64,512]{1,0:T(8,128)S(1)} %broadcast_multiply_fusion.3), kind=kOutput, calls=%fused_computation.73 | convolution fusion | flops 1098907648 | bytes 25461760 | tf_op jit(solution)/shard_map/ijz,zy->ijy/dot_general | solution.py:38
  129.0 273.2 %all-gather.3.cloned.1.call-done = bf16[128,512,512]{2,0,1:T(8,128)(2,1)} async-done(((bf16[128,64,512]{2,0,1:T(8,128)(2,1)}), bf16[128,512,512]{2,0,1:T(8,128)(2,1)}) %all-gather.3.cloned.1.call-update) | async-done | bytes 67108880 | tf_op jit(solution)/shard_map/all_gather | solution.py:50
  402.2 65.6 %fusion.58 = (f32[64,512]{1,0:T(8,128)S(1)}, f32[128,64,512]{2,1,0:T(8,128)}) fusion(bf16[128,64,512]{2,1,0:T(8,128)(2,1)} %copy.68, bf16[128,512,512]{2,0,1:T(8,128)(2,1)} %all-gather.3.cloned.1.call-done), kind=kOutput, calls=%fused_computation.96 | convolution fusion | flops 4299128832 | bytes 92405760 | tf_op jit(solution)/shard_map/cik,cjk->cij/dot_general | solution.py:51
  467.8 7.9 multiply_reduce_fusion.1
  475.8 10.4 add_convert_fusion.1
  486.1 23.2 %convert_reduce_fusion = (f32[64,512]{1,0:T(8,128)S(1)}, bf16[64,512,128]{1,2,0:T(8,128)(2,1)}) fusion(f32[128]{0:T(128)S(1)} %get-tuple-element.22, bf16[128,64,512]{2,1,0:T(8,128)(2,1)} %add_convert_fusion.1, bf16[2,128,128]{2,1,0:T(8,128)(2,1)S(1)} %copy-done.12, f32[64,512,128]{1,2,0:T(8,128)} %fusion.45, f32[128]{0:T(128)S(1)} %get-tuple-element.29, ...), kind=kOutput, calls=%fused_computation.8 | convolution fusion | flops 1119846400 | bytes 42107904 | tf_op jit(solution)/shard_map/cij,cz->ijz/dot_general | solution.py:37
  515.9 31.0 %add_bitcast_fusion = f32[512,64,512]{0,2,1:T(8,128)} fusion(f32[512]{0:T(512)S(1)} %bitcast.77, bf16[2,128,512]{2,1,0:T(8,128)(2,1)S(1)} %copy-done, bf16[64,512,128]{1,2,0:T(8,128)(2,1)} %get-tuple-element.26, f32[128]{0:T(128)S(1)} %get-tuple-element.18, f32[128]{0:T(128)S(1)} %get-tuple-element.15, f32[64,512]{1,0:T(8,128)S(1)} %add_rsqrt_fusion.1, ...), kind=kOutput, calls=%fused_computation.4 | convolution fusion | flops 4336910336 | bytes 75893760 | tf_op jit(solution)/shard_map/zc,ijz->cij/dot_general | solution.py:28
  546.9 28.3 %fusion.18 = (bf16[128,64,512]{0,2,1:T(8,128)(2,1)}, bf16[128,64,512]{0,2,1:T(8,128)(2,1)}) fusion(f32[512,64,512]{0,2,1:T(8,128)} %add_bitcast_fusion, f32[64,512]{1,0:T(8,128)S(1)} %convert_element_type.153), kind=kLoop, calls=%fused_computation.27 | loop fusion | flops 50331648 | bytes 84017152 | tf_op jit(solution)/shard_map/convert_element_type | solution.py:23
  575.2 12.0 %copy.78 = bf16[128,64,512]{2,0,1:T(8,128)(2,1)} copy(bf16[128,64,512]{0,2,1:T(8,128)(2,1)} %get-tuple-element.5) | data formatting | bytes 16777216 | tf_op jit(solution)/shard_map/convert_element_type | solution.py:23
  587.2 12.1 %copy.75 = bf16[128,64,512]{0,1,2:T(8,128)(2,1)} copy(bf16[128,64,512]{0,2,1:T(8,128)(2,1)} %get-tuple-element.6) | data formatting | bytes 16777216 | tf_op jit(solution)/shard_map/convert_element_type | solution.py:23
  603.5 13.3 %fusion.48 = f32[64,512,128]{1,2,0:T(8,128)} fusion(bf16[2,128,128]{2,1,0:T(8,128)(2,1)S(1)} %copy-done.2, bf16[64,512,128]{1,2,0:T(8,128)(2,1)} %get-tuple-element.26, f32[128]{0:T(128)S(1)} %get-tuple-element.18, f32[128]{0:T(128)S(1)} %get-tuple-element.15, f32[64,512]{1,0:T(8,128)S(1)} %add_rsqrt_fusion.1, f32[64,512]{1,0:T(8,128)S(1)} %broadcast_multiply_fusion.1), kind=kOutput, calls=%fused_computation.76 | convolution fusion | flops 1098907648 | bytes 25461760 | tf_op jit(solution)/shard_map/ijz,zy->ijy/dot_general | solution.py:38
  616.7 168.0 %all-to-all-done = bf16[128,64,512]{0,1,2:T(8,128)(2,1)} async-done(((bf16[128,64,512]{0,1,2:T(8,128)(2,1)}), bf16[128,64,512]{0,1,2:T(8,128)(2,1)}, u32[]{:S(2)}, u32[]{:S(2)}) %all-to-all-start) | async-done | bytes 8388640 | tf_op jit(solution)/shard_map/all_to_all | solution.py:54
  784.7 12.0 %copy.77 = bf16[128,8,64,64]{0,3,2,1:T(8,128)(2,1)} copy(bf16[128,8,64,64]{0,2,3,1:T(8,128)(2,1)} %bitcast.25) | data formatting | bytes 16777216 | tf_op jit(solution)/shard_map/all_to_all | solution.py:54
  796.7 13.5 %copy.79 = bf16[128,512,64]{1,2,0:T(8,128)(2,1)} copy(bf16[128,512,64]{0,2,1:T(8,128)(2,1)} %bitcast.76) | data formatting | bytes 16777216 | tf_op jit(solution)/shard_map/all_to_all | solution.py:54
  810.2 164.3 %all-gather.5.cloned.1.call-done = bf16[128,512,512]{2,0,1:T(8,128)(2,1)} async-done(((bf16[128,64,512]{2,0,1:T(8,128)(2,1)}), bf16[128,512,512]{2,0,1:T(8,128)(2,1)}) %all-gather.5.cloned.1.call-update) | async-done | bytes 67108880 | tf_op jit(solution)/shard_map/all_gather | solution.py:55
  974.4 143.9 %fusion.59 = (f32[64,512]{1,0:T(8,128)S(1)}, f32[128,64,512]{2,1,0:T(8,128)}) fusion(bf16[128,512,64]{1,2,0:T(8,128)(2,1)} %copy.79, bf16[128,512,512]{2,0,1:T(8,128)(2,1)} %all-gather.5.cloned.1.call-done), kind=kOutput, calls=%fused_computation.97 | convolution fusion | flops 4299128832 | bytes 92405760 | tf_op jit(solution)/shard_map/cki,ckj->cij/dot_general | solution.py:56
  1126.4 10.4 add_convert_fusion
  1136.7 18.1 %fusion.17 = bf16[64,512,128]{1,2,0:T(8,128)(2,1)} fusion(bf16[64,512,128]{1,2,0:T(8,128)(2,1)} %get-tuple-element.26, f32[64,512,128]{1,2,0:T(8,128)} %fusion.48, bf16[128,64,512]{2,1,0:T(8,128)(2,1)} %add_convert_fusion, f32[128]{0:T(128)S(1)} %copy-done.10, f32[128]{0:T(128)S(1)} %copy-done.11, bf16[2,128,128]{2,1,0:T(8,128)(2,1)S(1)} %copy-done.12), kind=kOutput, calls=%fused_computation.25 | convolution fusion | flops 1111490560 | bytes 41976832 | tf_op jit(solution)/shard_map/cij,cz->ijz/dot_general | solution.py:37
  1154.8 11.9 %copy.83 = bf16[64,512,128]{2,1,0:T(8,128)(2,1)} copy(bf16[64,512,128]{1,2,0:T(8,128)(2,1)} %fusion.17) | data formatting | bytes 16777216 | tf_op jit(solution)/shard_map/convert_element_type | solution.py:39
  (48 shorter events, 32.2 us)
Async XLA Ops:
  6.5 24.1 %copy-start.4 = (bf16[2,2,128]{2,1,0:T(2,128)(2,1)S(1)}, bf16[2,2,128]{2,1,0:T(2,128)(2,1)}, u32[]{:S(2)}) copy-start(bf16[2,2,128]{2,1,0:T(2,128)(2,1)} %param.12) | copy-start | bytes 3076
  6.5 24.1 %copy-start.3 = (bf16[2,512]{1,0:T(2,128)(2,1)S(1)}, bf16[2,512]{1,0:T(2,128)(2,1)}, u32[]{:S(2)}) copy-start(bf16[2,512]{1,0:T(2,128)(2,1)} %param.14) | copy-start | bytes 6148
  6.5 24.1 %copy-start.1 = (s32[64,512]{1,0:T(8,128)S(1)}, s32[64,512]{1,0:T(8,128)}, u32[]{:S(2)}) copy-start(s32[64,512]{1,0:T(8,128)} %param.11) | copy-start | bytes 393220
  6.5 24.1 %copy-start = (bf16[2,128,512]{2,1,0:T(8,128)(2,1)S(1)}, bf16[2,128,512]{2,1,0:T(8,128)(2,1)}, u32[]{:S(2)}) copy-start(bf16[2,128,512]{2,1,0:T(8,128)(2,1)} %param.13) | copy-start | bytes 786436
  6.5 395.6 %all-gather.3.cloned.1.call-start = ((), (), s32[]{:S(2)}) async-start(), calls=%async_computation.1 | async-start | bytes 75497472 | tf_op jit(solution)/shard_map/all_gather | solution.py:50
  102.0 13.0 %copy-start.5 = (bf16[2,2,128]{2,1,0:T(2,128)(2,1)S(1)}, bf16[2,2,128]{2,1,0:T(2,128)(2,1)}, u32[]{:S(2)}) copy-start(bf16[2,2,128]{2,1,0:T(2,128)(2,1)} %param.17) | copy-start | bytes 3076
  102.0 13.6 %copy-start.8 = (bf16[2,128]{1,0:T(2,128)(2,1)S(1)}, bf16[2,128]{1,0:T(2,128)(2,1)}, u32[]{:S(2)}) copy-start(bf16[2,128]{1,0:T(2,128)(2,1)} %param.19) | copy-start | bytes 1540
  102.0 13.6 %copy-start.9 = (bf16[2,128]{1,0:T(2,128)(2,1)S(1)}, bf16[2,128]{1,0:T(2,128)(2,1)}, u32[]{:S(2)}) copy-start(bf16[2,128]{1,0:T(2,128)(2,1)} %param.16) | copy-start | bytes 1540
  102.0 14.1 %copy-start.2 = (bf16[2,128,128]{2,1,0:T(8,128)(2,1)S(1)}, bf16[2,128,128]{2,1,0:T(8,128)(2,1)}, u32[]{:S(2)}) copy-start(bf16[2,128,128]{2,1,0:T(8,128)(2,1)} %param.15) | copy-start | bytes 196612
  102.0 872.4 %all-gather.5.cloned.1.call-start = ((), (), s32[]{:S(2)}) async-start(), calls=%async_computation.2 | async-start | bytes 75497472 | tf_op jit(solution)/shard_map/all_gather | solution.py:55
  475.7 10.4 copy-start.12
  599.3 185.4 %all-to-all-start = ((bf16[128,64,512]{0,1,2:T(8,128)(2,1)}), bf16[128,64,512]{0,1,2:T(8,128)(2,1)}, u32[]{:S(2)}, u32[]{:S(2)}) async-start(bf16[128,64,512]{0,1,2:T(8,128)(2,1)} %copy.75), calls=%async_computation | async-start | bytes 16777216 | tf_op jit(solution)/shard_map/all_to_all | solution.py:54
  1118.3 8.0 copy-start.6
  1118.3 8.0 copy-start.7
  1126.3 10.4 copy-start.10
  1126.3 10.4 copy-start.11
Sparse Core Ops, SparseCore 0:
  102.1 300.0 all-gather.2
  587.3 387.0 all-gather.4
where the time goes:
time: 1180 us; the launch traced here: 1170 us
  waiting for transfers between devices  606 us (51%)
  matrix products  339 us (29%)
  other arithmetic  113 us (10%)
  local copies, waits for them, and re-layouts  98.1 us (8%)
  between operations  14 us (1%)
    all_gather x2, waiting for transfers between devices, local_layers(): right_all = lax.all_gather(right, 'dap', axis=1, tiled=True)  437 us
    all_to_all x1, waiting for transfers between devices, local_layers(): left_cols = lax.all_to_all(left, 'dap', 2, 1, tiled=True)  168 us
    dot_general x1, matrix products, local_layers(): jnp.einsum('cki,ckj->cij', left_cols, right_all, preferred_element_type=j...  144 us
    dot_general x1, matrix products, local_layers(): jnp.einsum('cik,cjk->cij', left, right_all, preferred_element_type=jnp.fl...  65.6 us
    dot_general x2, matrix products, normalize_project(): jnp.einsum('zc,ijz->cij', w_proj, normed, preferred_element_type=jnp.floa...  62.1 us
    convert_element_type x2, other arithmetic, gated_side(): (keep_mask * jax.nn.sigmoid(projected[channels:2 * channels]) * projected...  56.5 us
    convert_element_type x4, local copies, waits for them, and re-layouts, gated_side(): (keep_mask * jax.nn.sigmoid(projected[channels:2 * channels]) * projected...  48.7 us
    dot_general x2, matrix products, finish_layer(): jnp.einsum('cij,cz->ijz', tri_norm, w_out, preferred_element_type=jnp.flo...  41.3 us
  transfers between devices with their start and end apart: 3, of which 3 were waited for; matrix products, arithmetic and copies ran while one was open for 7% of the time, Pallas kernels for 0%

commit v1 on v0

v1 whole, which is shorter than its diff:
```python
import functools

import jax
import jax.numpy as jnp
from jax import lax
from jax.experimental import pallas as pl
from jax.experimental.pallas import tpu as pltpu
from jax.sharding import PartitionSpec as P

f32, bf16 = jnp.float32, jnp.bfloat16
LN_EPS = 1e-5
CH = 128
EXT = CH + 16
ROWS = 16
PITCH = 24
ROW_PITCH = 136
VMEM = 56 * 2**20


def norm_columns(x, scale, offset):
    mean = jnp.sum(x, axis=0, keepdims=True) * (1.0 / CH)
    centred = x - mean
    var = jnp.sum(centred * centred, axis=0, keepdims=True) * (1.0 / CH)
    return centred * lax.rsqrt(var + LN_EPS) * scale + offset


def extend(columns, row):
    n = columns.shape[1]
    first = lax.broadcasted_iota(jnp.int32, (16, n), 0) == 0
    extra = jnp.where(first, jnp.broadcast_to(row, (16, n)), 0.0).astype(bf16)
    return jnp.concatenate([columns, extra], axis=0)


def twice(ref):
    return jnp.concatenate([ref[...]] * 2, axis=1)


def store_gated(proj, store):
    for q in range(proj.shape[0] // 16):
        value, gate = proj[16 * q:16 * q + 8], proj[16 * q + 8:16 * q + 16]
        side = (jnp.tanh(gate) + 1.0) * value
        for t in range(2):
            store(q, t, side[:, 128 * t:128 * t + 128])


def project_body(z_ref, m_ref, w_ref, sc_ref, of_ref, a_ref, b_ref, zt_ref, znt_ref, scr):
    scale, offset = twice(sc_ref), twice(of_ref)

    def row(i, carry):
        zt = z_ref[i].T
        zt_ref[i] = zt
        zn = norm_columns(zt.astype(f32), scale, offset).astype(bf16)
        znt_ref[i] = zn
        m = m_ref[pl.ds(i, 1), :]
        proj = jnp.dot(w_ref[...], extend(zn * m.astype(bf16), m), preferred_element_type=f32)

        def store(q, t, tile):
            scr[t, pl.ds(8 * q * PITCH + i, 8, stride=PITCH), :] = tile

        store_gated(proj, store)
        return carry

    lax.fori_loop(0, ROWS, row, 0, unroll=8)
    for side, out in ((0, a_ref), (1, b_ref)):
        def channel(q, carry):
            for u in range(8):
                c = q * 8 + u
                start = pl.multiple_of((side * CH + c) * PITCH, 8)
                for t in range(2):
                    out[c, :, 128 * t:128 * t + 128] = scr[t, pl.ds(start, ROWS), :].astype(bf16)
            return carry

        lax.fori_loop(0, CH // 8, channel, 0)


def whole(*shape):
    return pl.BlockSpec(shape, lambda *ids: (0,) * len(shape))


def params(n=1):
    return pltpu.CompilerParams(dimension_semantics=("arbitrary",) * n, vmem_limit_bytes=VMEM)


def cost(flops, nbytes):
    return pl.CostEstimate(flops=flops, bytes_accessed=nbytes, transcendentals=0)


def project(z, m, w, scale, offset):
    rows, cols, _ = z.shape
    return pl.pallas_call(
        project_body,
        grid=(rows // ROWS, cols // 256),
        in_specs=[pl.BlockSpec((ROWS, 256, CH), lambda i, k: (i, k, 0)),
                  pl.BlockSpec((ROWS, 256), lambda i, k: (i, k)),
                  whole(4 * CH, EXT), whole(CH, CH), whole(CH, CH)],
        out_specs=[pl.BlockSpec((CH, ROWS, 256), lambda i, k: (0, i, k))] * 2
        + [pl.BlockSpec((ROWS, CH, 256), lambda i, k: (i, 0, k))] * 2,
        out_shape=[jax.ShapeDtypeStruct((CH, rows, cols), bf16)] * 2
        + [jax.ShapeDtypeStruct((rows, CH, cols), bf16)] * 2,
        scratch_shapes=[pltpu.VMEM((2, 2 * CH * PITCH, 128), f32)],
        compiler_params=params(2),
        cost_estimate=cost(rows * cols * 2**19, rows * cols * 1200),
        name="project",
    )(z, m, w, scale, offset)


def outgoing_body(n_left, n_right, h_ref, *refs):
    left = refs[:n_left]
    mine, theirs = refs[n_left:n_left + n_right], refs[n_left + n_right:n_left + 2 * n_right]
    o_ref, scr = refs[n_left + 2 * n_right:]
    at_mine, at_theirs = pl.multiple_of(64 * h_ref[0], 64), pl.multiple_of(64 - 64 * h_ref[0], 64)
    for c in range(o_ref.shape[0]):
        for s in range(n_right):
            scr[c, pl.ds(128 * s + at_mine, 64), :] = mine[s][c]
            scr[c, pl.ds(128 * s + at_theirs, 64), :] = theirs[s][c]
        a = jnp.concatenate([ref[c] for ref in left], axis=0)
        o_ref[c] = lax.dot_general(a, scr[c], (((1,), (1,)), ((), ())), preferred_element_type=f32)


def outgoing(h, left, mine, theirs):
    block = 4
    _, rows, cols = left[0].shape
    nl, nr = len(left), len(mine)
    side = pl.BlockSpec((block, rows, cols), lambda c: (c, 0, 0))
    return pl.pallas_call(
        functools.partial(outgoing_body, nl, nr),
        grid=(CH // block,),
        in_specs=[pl.BlockSpec(memory_space=pltpu.SMEM)] + [side] * (nl + 2 * nr),
        out_specs=pl.BlockSpec((block, nl * rows, nr * 2 * rows), lambda c: (c, 0, 0)),
        out_shape=jax.ShapeDtypeStruct((CH, nl * rows, nr * 2 * rows), f32),
        scratch_shapes=[pltpu.VMEM((block, nr * 2 * rows, cols), bf16)],
        compiler_params=params(),
        cost_estimate=cost(CH * nl * nr * rows * 2 * rows * cols * 4, CH * rows * (nl + 2 * nr) * cols * 4),
        name="outgoing",
    )(h, *left, *mine, *theirs)


def incoming_body(n_parts, h_ref, *refs):
    left, right = refs[:4], refs[4:4 + 4 * n_parts]
    keep_ref, send_ref, scr = refs[4 + 4 * n_parts:]
    at_mine, at_theirs = pl.multiple_of(64 * h_ref[0], 64), pl.multiple_of(64 - 64 * h_ref[0], 64)
    for c in range(keep_ref.shape[0]):
        a = jnp.concatenate([ref[c] for ref in left], axis=0)
        b = jnp.concatenate([jnp.concatenate([right[s * n_parts + p][c] for p in range(n_parts)], axis=1)
                             for s in range(4)], axis=0)
        scr[c] = lax.dot_general(a, b, (((0,), (0,)), ((), ())), preferred_element_type=f32)
        keep_ref[c] = scr[c, pl.ds(at_mine, 64), :]
        send_ref[c] = scr[c, pl.ds(at_theirs, 64), :]


def incoming(h, left, right):
    block = 4
    parts = [part for row in right for part in row]
    spec = lambda x: pl.BlockSpec((block,) + x.shape[1:], lambda c: (c, 0, 0))
    return pl.pallas_call(
        functools.partial(incoming_body, len(right[0])),
        grid=(CH // block,),
        in_specs=[pl.BlockSpec(memory_space=pltpu.SMEM)] + [spec(x) for x in left + parts],
        out_specs=[pl.BlockSpec((block, 64, 512), lambda c: (c, 0, 0))] * 2,
        out_shape=[jax.ShapeDtypeStruct((CH, 64, 512), f32)] * 2,
        scratch_shapes=[pltpu.VMEM((block, 128, 512), f32)],
        compiler_params=params(),
        cost_estimate=cost(2**32, 80 * 2**20),
        name="incoming",
    )(h, *left, *parts)


def normalize_rows(load, scr):
    for g in range(ROWS // 8):
        zero = jnp.zeros((8, 128), f32)

        def add(q, sums):
            sums = list(sums)
            for u in range(16):
                sums[u % 4] += load(q * 16 + u, g)
            return tuple(sums)

        s = lax.fori_loop(0, CH // 16, add, (zero,) * 4)
        mean = (s[0] + s[1] + s[2] + s[3]) * (1.0 / CH)

        def add_square(q, sums):
            sums = list(sums)
            for u in range(16):
                centred = load(q * 16 + u, g) - mean
                sums[u % 4] += centred * centred
            return tuple(sums)

        s = lax.fori_loop(0, CH // 16, add_square, (zero,) * 4)
        rstd = lax.rsqrt((s[0] + s[1] + s[2] + s[3]) * (1.0 / CH) + LN_EPS)

        def put(q, carry):
            for u in range(16):
                c = q * 16 + u
                scr[pl.ds(8 * g * ROW_PITCH + c, 8, stride=ROW_PITCH), :] = (load(c, g) - mean) * rstd
            return carry

        lax.fori_loop(0, CH // 16, put, 0)


def pair_of(ref, p):
    return jnp.concatenate([ref[2 * p], ref[2 * p + 1]], axis=1)


def update_pair(p, scr, zt_ref, znt_ref, wo_ref, wg_ref, scale, offset, ones):
    start = pl.multiple_of(2 * p * ROW_PITCH, 8)
    normed = jnp.concatenate([scr[pl.ds(start, CH), :], scr[pl.ds(start + ROW_PITCH, CH), :]], axis=1)
    u = (normed * scale + offset).astype(bf16)
    update = jnp.dot(wo_ref[...], extend(u, ones), preferred_element_type=f32)
    gate = jnp.dot(wg_ref[...], extend(pair_of(znt_ref, p), ones), preferred_element_type=f32)
    return (pair_of(zt_ref, p).astype(f32) + (jnp.tanh(gate) + 1.0) * update).astype(bf16)


def finish_project_body(with_left, with_pair, g_ref, o_ref, zt_ref, znt_ref, m_ref, wo_ref, wg_ref, so_ref, oo_ref,
                        w_ref, si_ref, oi_ref, *refs):
    refs = list(refs)
    b_ref = refs.pop(0)
    a_ref = refs.pop(0) if with_left else None
    z1_ref, zn1_ref = (refs.pop(0), refs.pop(0)) if with_pair else (None, None)
    scr, scr2, exts = refs
    normalize_rows(lambda c, g: o_ref[c, 8 * g:8 * g + 8, :], scr)
    scale_out, offset_out = twice(so_ref), twice(oo_ref)
    scale_in, offset_in = twice(si_ref), twice(oi_ref)
    ones = jnp.ones((1, 256), f32)

    def put(p):
        def store(q, t, tile):
            scr2[pl.ds(8 * q * PITCH + 2 * p + t, 8, stride=PITCH), :] = tile
        return store

    def pair(p, carry):
        z1 = update_pair(p, scr, zt_ref, znt_ref, wo_ref, wg_ref, scale_out, offset_out, ones)
        zn1 = norm_columns(z1.astype(f32), scale_in, offset_in).astype(bf16)
        if with_pair:
            for t in range(2):
                z1_ref[2 * p + t] = z1[:, 128 * t:128 * t + 128]
                zn1_ref[2 * p + t] = zn1[:, 128 * t:128 * t + 128]
        m = jnp.concatenate([m_ref[pl.ds(2 * p, 1), :], m_ref[pl.ds(2 * p + 1, 1), :]], axis=1)
        ext = extend(zn1 * m.astype(bf16), m)
        if with_left:
            exts[p] = ext
        store_gated(jnp.dot(w_ref[2 * CH:], ext, preferred_element_type=f32), put(p))
        return carry

    def emit(out):
        def channel(q, carry):
            for u in range(8):
                c = q * 8 + u
                out[c] = scr2[pl.ds(pl.multiple_of(c * PITCH, 8), ROWS), :].astype(bf16)
            return carry

        lax.fori_loop(0, CH // 8, channel, 0)

    lax.fori_loop(0, ROWS // 2, pair, 0, unroll=4)
    emit(b_ref)
    if with_left:
        @pl.when(pl.program_id(1) == 0)
        def _():
            def left(p, carry):
                store_gated(jnp.dot(w_ref[:2 * CH], exts[p], preferred_element_type=f32), put(p))
                return carry

            lax.fori_loop(0, ROWS // 2, left, 0, unroll=4)
            emit(a_ref)


def finish_project(chip, o, at_row, first, zt, znt, m, layer1, layer2, with_pair):
    rows = zt.shape[0]
    n = o.shape[2] // 128
    with_left = first == 0
    natural = lambda j, g: (j + first) ^ g[0]
    out_specs = [pl.BlockSpec((CH, ROWS, 128), lambda i, j, g: (0, i, j))]
    out_shape = [jax.ShapeDtypeStruct((CH, rows, n * 128), bf16)]
    if with_left:
        out_specs.append(pl.BlockSpec((CH, ROWS, 128), lambda i, j, g: (0, i, 0)))
        out_shape.append(jax.ShapeDtypeStruct((CH, rows, 128), bf16))
    if with_pair:
        out_specs += [pl.BlockSpec((ROWS, CH, 128), lambda i, j, g: (i, 0, j))] * 2
        out_shape += [jax.ShapeDtypeStruct((rows, CH, n * 128), bf16)] * 2
    positions = pl.BlockSpec((ROWS, CH, 128), lambda i, j, g: (i, 0, natural(j, g)))
    out = pl.pallas_call(
        functools.partial(finish_project_body, with_left, with_pair),
        grid_spec=pltpu.PrefetchScalarGridSpec(
            num_scalar_prefetch=1,
            grid=(rows // ROWS, n),
            in_specs=[pl.BlockSpec((CH, ROWS, 128), lambda i, j, g: (0, i + at_row // ROWS, j)),
                      positions, positions,
                      pl.BlockSpec((ROWS, 128), lambda i, j, g: (i, natural(j, g))),
                      whole(CH, EXT), whole(CH, EXT), whole(CH, CH), whole(CH, CH),
                      whole(4 * CH, EXT), whole(CH, CH), whole(CH, CH)],
            out_specs=out_specs,
            scratch_shapes=[pltpu.VMEM((ROWS * ROW_PITCH, 128), f32), pltpu.VMEM((CH * PITCH, 128), f32),
                            pltpu.VMEM((ROWS // 2, EXT, 256), bf16)],
        ),
        out_shape=out_shape,
        compiler_params=params(2),
        cost_estimate=cost(rows * n * 128 * 2**19, rows * n * 128 * 1600),
        name="finish_project",
    )(chip, o, zt, znt, m, layer1["w_out"], layer1["w_gate"], layer1["ln_out"][0], layer1["ln_out"][1],
      layer2["w_proj"], layer2["ln_in"][0], layer2["ln_in"][1])
    out = list(out)
    return (out.pop(0), out.pop(0) if with_left else None, out.pop(0) if with_pair else None,
            out.pop(0) if with_pair else None)


def finish_body(g_ref, o_ref, r_ref, zt_ref, znt_ref, wo_ref, wg_ref, so_ref, oo_ref, out_ref, scr, total):
    def add(q, carry):
        for u in range(8):
            total[q * 8 + u] = o_ref[q * 8 + u] + r_ref[q * 8 + u]
        return carry

    lax.fori_loop(0, CH // 8, add, 0)
    normalize_rows(lambda c, g: total[c, 8 * g:8 * g + 8, :], scr)
    scale, offset = twice(so_ref), twice(oo_ref)
    ones = jnp.ones((1, 256), f32)

    def pair(p, carry):
        z2 = update_pair(p, scr, zt_ref, znt_ref, wo_ref, wg_ref, scale, offset, ones).T
        for t in range(2):
            out_ref[2 * p + t] = z2[128 * t:128 * t + 128]
        return carry

    lax.fori_loop(0, ROWS // 2, pair, 0, unroll=4)


def finish(chip, o, received, zt, znt, layer2):
    _, rows, cols = o.shape
    part = pl.BlockSpec((CH, ROWS, 128), lambda i, j, g: (0, i, j))
    positions = pl.BlockSpec((ROWS, CH, 128), lambda i, j, g: (i, 0, j))
    return pl.pallas_call(
        finish_body,
        grid_spec=pltpu.PrefetchScalarGridSpec(
            num_scalar_prefetch=1,
            grid=(rows // ROWS, cols // 128),
            in_specs=[part, part, positions, positions,
                      whole(CH, EXT), whole(CH, EXT), whole(CH, CH), whole(CH, CH)],
            out_specs=pl.BlockSpec((ROWS, 128, CH), lambda i, j, g: (i, j ^ g[0], 0)),
            scratch_shapes=[pltpu.VMEM((ROWS * ROW_PITCH, 128), f32), pltpu.VMEM((CH, ROWS, 128), f32)],
        ),
        out_shape=jax.ShapeDtypeStruct((rows, cols, CH), bf16),
        compiler_params=params(2),
        cost_estimate=cost(rows * cols * 2**17, rows * cols * 1800),
        name="finish",
    )(chip, o, received, zt, znt, layer2["w_out"], layer2["w_gate"], layer2["ln_out"][0], layer2["ln_out"][1])


def with_bias(w, b):
    n = w.shape[1]
    return jnp.concatenate([w.T, b[:, None], jnp.zeros((n, EXT - CH - 1), bf16)], axis=1) * jnp.asarray(0.5, bf16)


def layer_params(ln_in, w_proj, b_proj, w_gate, b_gate, ln_out, w_out, b_out):
    lanes = lambda v: jnp.broadcast_to(v.astype(f32)[:, None], (CH, CH))
    proj = with_bias(w_proj, b_proj).reshape(2, 2, CH // 8, 8, EXT).transpose(0, 2, 1, 3, 4).reshape(4 * CH, EXT)
    gate, out = with_bias(w_gate, b_gate), with_bias(w_out, b_out)
    return {"w_proj": proj, "w_gate": gate, "w_out": out,
            "ln_in": (lanes(ln_in[0]), lanes(ln_in[1])), "ln_out": (lanes(ln_out[0]), lanes(ln_out[1]))}


def solution(mesh):
    row_spec = P(("batch", "dap"), None, None)
    mask_spec = P(("batch", "dap"), None)
    n = mesh.shape["dap"]

    def swap(x, bits):
        return lax.ppermute(x, "dap", [(i, i ^ bits) for i in range(n)])

    def local_layers(pair, pair_mask, ln_in, w_proj, b_proj, w_gate, b_gate, ln_out, w_out, b_out):
        layer1, layer2 = (layer_params(ln_in[l], w_proj[l], b_proj[l], w_gate[l], b_gate[l], ln_out[l], w_out[l],
                                       b_out[l]) for l in range(2))
        me = lax.axis_index("dap")
        chip, core = (me // 2).reshape(1).astype(jnp.int32), (me % 2).reshape(1).astype(jnp.int32)
        half = pair.shape[0] // 2

        mask = pair_mask.astype(f32)
        masks = [mask, swap(mask, 2), swap(mask, 4), swap(mask, 6)]
        pairs = [pair, swap(pair, 2), swap(pair, 4)]
        pairs.append(jnp.concatenate([swap(pairs[1][:half], 4), swap(pairs[2][half:], 2)], axis=0))

        left, mine, theirs, zt, znt = [], [], [], [], []
        b2, a2 = [[], [], [], []], []
        z1 = zn1 = None
        for s in range(4):
            a, b, t, tn = project(pairs[s], masks[s], layer1["w_proj"], *layer1["ln_in"])
            left.append(a)
            mine.append(b)
            theirs.append(swap(b, 1))
            zt.append(t)
            znt.append(tn)
        for rows, cols in RECTS:
            o = outgoing(core, [left[s] for s in rows], [mine[s] for s in cols], [theirs[s] for s in cols])
            for at, s in enumerate(rows):
                b, a, zz, zzn = finish_project(chip, o, 64 * at, cols[0], zt[s], znt[s], masks[s], layer1, layer2, s == 0)
                b2[s].append(b)
                if a is not None:
                    a2.append(a)
                if s == 0:
                    z1, zn1 = zz, zzn
        keep, send = incoming(core, a2, b2)
        return finish(chip, keep, swap(send, 1), z1, zn1, layer2)

    return jax.shard_map(local_layers, mesh=mesh,
                         in_specs=(row_spec, mask_spec, P(), P(), P(), P(), P(), P(), P(), P()),
                         out_specs=row_spec, check_vma=False)


RECTS = (((0, 1, 2, 3), (0, 1, 2, 3)),)
```

time: 1180 us -> 667 us (0.57)
  Pallas kernels: 0 us -> 402 us
  waiting for transfers between devices: 606 us -> 221 us
  matrix products: 339 us -> 0 us
  other arithmetic: 113 us -> 10.5 us
  local copies, waits for them, and re-layouts: 98.1 us -> 19.9 us
  between operations: 14 us -> 0.26 us
    all_gather x2 -> x0, waiting for transfers between devices: 437 us -> none  [local_layers(): right_all = lax.all_gather(right, 'dap', axis=1, tiled=True)]
    pallas_call x0 -> x11, Pallas kernels: none -> 402 us  [the longest x4 169 us: finish_project(): pl.pallas_call(functools.partial(finish_project_body, with_left, with_pai...]
    dot_general x8 -> x0, matrix products: 339 us -> none  [the longest x1 144 us: local_layers(): jnp.einsum('cki,ckj->cij', left_cols, right_all, preferred_element_type=j...]
    ppermute x0 -> x12, waiting for transfers between devices: none -> 221 us  [swap(): return lax.ppermute(x, 'dap', [(i, i ^ bits) for i in range(n)])]
    all_to_all x1 -> x0, waiting for transfers between devices: 168 us -> none  [local_layers(): left_cols = lax.all_to_all(left, 'dap', 2, 1, tiled=True)]
    convert_element_type x8 -> x3, other arithmetic: 78.4 us -> 2.19 us  [the longest x2 1.27 us: layer_params(): lanes = lambda v: jnp.broadcast_to(v.astype(f32)[:, None], (CH, CH))]
    convert_element_type x5 -> x0, local copies, waits for them, and re-layouts: 60.6 us -> none  [the longest x4 48.7 us: gated_side(): (keep_mask * jax.nn.sigmoid(projected[channels:2 * channels]) * projected...]
    reduce_sum x5 -> x0, other arithmetic: 34.3 us -> none  [the longest x2 15.9 us: norm_channels(): variance = jnp.mean(centred * centred, axis=-3, keepdims=True)]
  transfers between devices with their start and end apart: 3 -> 12, of which waited for: 3 -> 5; matrix products, arithmetic and copies ran while one was open for 7% -> 4% of each run, Pallas kernels for 0% -> 14%
where the time goes in v1:
time: 667 us; the launch traced here: 665 us
  Pallas kernels  402 us (60%)
  waiting for transfers between devices  221 us (33%)
  local copies, waits for them, and re-layouts  19.9 us (3%)
  starting transfers between devices  12.1 us (2%)
  other arithmetic  10.5 us (2%)
    ppermute x12, waiting for transfers between devices, swap(): return lax.ppermute(x, 'dap', [(i, i ^ bits) for i in range(n)])  221 us
    pallas_call x4, Pallas kernels, finish_project(): pl.pallas_call(functools.partial(finish_project_body, with_left, with_pai...  169 us
    pallas_call x4, Pallas kernels, project(): pl.pallas_call(project_body, grid=(rows // ROWS, cols // 256), in_specs=[...  94.5 us
    pallas_call x1, Pallas kernels, outgoing(): pl.pallas_call(functools.partial(outgoing_body, nl, nr), grid=(CH // bloc...  67.8 us
    pallas_call x1, Pallas kernels, incoming(): pl.pallas_call(functools.partial(incoming_body, len(right[0])), grid=(CH...  39.5 us
    pallas_call x1, Pallas kernels, finish(): pl.pallas_call(finish_body, grid_spec=pltpu.PrefetchScalarGridSpec(num_sc...  30.8 us
  transfers between devices with their start and end apart: 12, of which 5 were waited for; matrix products, arithmetic and copies ran while one was open for 4% of the time, Pallas kernels for 14%

profile of v1, /device:TPU:0, one launch (start us, length us, event | category | flops | bytes accessed | tf_op | source)
XLA Modules:
  0.0 665.5 jit_solution(2167957336273296962)
XLA Ops:
  0.0 3.4 collective-permute-start.2
  3.4 1.5 collective-permute-start
  6.4 2.9 collective-permute-start.6
  13.6 171.1 %collective-permute-done.2.z_ref = bf16[64,512,128]{2,1,0:T(8,128)(2,1)} collective-permute-done((bf16[64,512,128]{2,1,0:T(8,128)(2,1)}, bf16[64,512,128]{2,1,0:T(8,128)(2,1)}, u32[]{:S(2)}, u32[]{:S(2)}) %collective-permute-start.2) | collective-permute-done | bytes 8388640 | tf_op jit(solution)/shard_map/ppermute | solution.py:365
  184.7 2.6 slice.109
  187.3 2.0 collective-permute-start.5
  189.3 4.6 slice.108
  193.9 1.5 collective-permute-start.4
  196.9 23.6 %project.4 = (bf16[128,64,512]{2,1,0:T(8,128)(2,1)}, bf16[128,64,512]{2,1,0:T(8,128)(2,1)}, bf16[64,128,512]{2,1,0:T(8,128)(2,1)}, bf16[64,128,512]{2,1,0:T(8,128)(2,1)}) custom-call(bf16[64,512,128]{2,1,0:T(8,128)(2,1)} %z_ref.1, f32[64,512]{1,0:T(8,128)} %copy-done, bf16[512,144]{1,0:T(8,128)(2,1)} %bitcast.68, f32[128,128]{1,0:T(8,128)} %broadcast_in_dim.16.sc_ref, ...), custom_call_target="tpu_custom_call" | custom-call | flops 17179869184 | bytes 39321600 | tf_op jit(solution)/shard_map/project/pallas_call | solution.py:90
  221.1 23.6 %project.5 = (bf16[128,64,512]{2,1,0:T(8,128)(2,1)}, bf16[128,64,512]{2,1,0:T(8,128)(2,1)}, bf16[64,128,512]{2,1,0:T(8,128)(2,1)}, bf16[64,128,512]{2,1,0:T(8,128)(2,1)}) custom-call(bf16[64,512,128]{2,1,0:T(8,128)(2,1)} %collective-permute-done.z_ref, f32[64,512]{1,0:T(8,128)} %copy-done.3, bf16[512,144]{1,0:T(8,128)(2,1)} %bitcast.69, ...), custom_call_target="tpu_custom_call" | custom-call | flops 17179869184 | bytes 39321600 | tf_op jit(solution)/shard_map/project/pallas_call | solution.py:90
  245.4 23.6 %project.6 = (bf16[128,64,512]{2,1,0:T(8,128)(2,1)}, bf16[128,64,512]{2,1,0:T(8,128)(2,1)}, bf16[64,128,512]{2,1,0:T(8,128)(2,1)}, bf16[64,128,512]{2,1,0:T(8,128)(2,1)}) custom-call(bf16[64,512,128]{2,1,0:T(8,128)(2,1)} %collective-permute-done.2.z_ref, f32[64,512]{1,0:T(8,128)} %copy-done.2, bf16[512,144]{1,0:T(8,128)(2,1)} %bitcast.70, ...), custom_call_target="tpu_custom_call" | custom-call | flops 17179869184 | bytes 39321600 | tf_op jit(solution)/shard_map/project/pallas_call | solution.py:90
  269.0 11.8 %collective-permute-done.5 = bf16[32,512,128]{2,1,0:T(8,128)(2,1)} collective-permute-done((bf16[32,512,128]{2,1,0:T(8,128)(2,1)S(1)}, bf16[32,512,128]{2,1,0:T(8,128)(2,1)}, u32[]{:S(2)}, u32[]{:S(2)}) %collective-permute-start.5) | collective-permute-done | bytes 4194336 | tf_op jit(solution)/shard_map/ppermute | solution.py:365
  280.8 3.3 collective-permute-done.4
  284.1 7.5 %pad_maximum_fusion.z_ref = bf16[64,512,128]{2,1,0:T(8,128)(2,1)} fusion(bf16[32,512,128]{2,1,0:T(8,128)(2,1)} %collective-permute-done.5, bf16[32,512,128]{2,1,0:T(8,128)(2,1)} %collective-permute-done.4), kind=kLoop, calls=%fused_computation | loop fusion | flops 4194304 | bytes 16777216 | tf_op jit(solution)/shard_map/concatenate | solution.py:377
  292.2 23.7 %project.7 = (bf16[128,64,512]{2,1,0:T(8,128)(2,1)}, bf16[128,64,512]{2,1,0:T(8,128)(2,1)}, bf16[64,128,512]{2,1,0:T(8,128)(2,1)}, bf16[64,128,512]{2,1,0:T(8,128)(2,1)}) custom-call(bf16[64,512,128]{2,1,0:T(8,128)(2,1)} %pad_maximum_fusion.z_ref, f32[64,512]{1,0:T(8,128)} %copy-done.1, bf16[512,144]{1,0:T(8,128)(2,1)} %bitcast.71, ...), custom_call_target="tpu_custom_call" | custom-call | flops 17179869184 | bytes 39321600 | tf_op jit(solution)/shard_map/project/pallas_call | solution.py:90
  319.1 9.9 %collective-permute-done.10.refs_11_ = bf16[128,64,512]{2,1,0:T(8,128)(2,1)} collective-permute-done((bf16[128,64,512]{2,1,0:T(8,128)(2,1)}, bf16[128,64,512]{2,1,0:T(8,128)(2,1)}, u32[]{:S(2)}, u32[]{:S(2)}) %collective-permute-start.10) | collective-permute-done | bytes 8388640 | tf_op jit(solution)/shard_map/ppermute | solution.py:365
  329.0 67.8 %outgoing.1.o_ref = f32[128,256,512]{2,1,0:T(8,128)} custom-call(s32[1]{0:T(128)} %bitcast.1.h_ref, bf16[128,64,512]{2,1,0:T(8,128)(2,1)} %get-tuple-element.33.refs_0_, bf16[128,64,512]{2,1,0:T(8,128)(2,1)} %get-tuple-element.34.refs_1_, bf16[128,64,512]{2,1,0:T(8,128)(2,1)} %get-tuple-element.35.refs_2_, bf16[128,64,512]{2,1,0:T(8,128)(2,1)} %get-tuple-element.36.refs_3_, ...), custom_call_target="tpu_custom_call" | custom-call | flops 34359738368 | bytes 201326592 | tf_op jit(solution)/shard_map/outgoing/pallas_call | solution.py:125
  399.6 42.7 %finish_project.4 = (bf16[128,64,512]{2,1,0:T(8,128)(2,1)}, bf16[128,64,128]{2,1,0:T(8,128)(2,1)}, bf16[64,128,512]{2,1,0:T(8,128)(2,1)}, bf16[64,128,512]{2,1,0:T(8,128)(2,1)}) custom-call(s32[1]{0:T(128)} %bitcast.g_ref, f32[128,256,512]{2,1,0:T(8,128)} %outgoing.1.o_ref, bf16[64,128,512]{2,1,0:T(8,128)(2,1)} %get-tuple-element.41.zt_ref, ...), custom_call_target="tpu_custom_call" | custom-call | flops 17179869184 | bytes 52428800 | tf_op jit(solution)/shard_map/finish_project/pallas_call | solution.py:280
  442.4 42.1 %finish_project.5 = (bf16[128,64,512]{2,1,0:T(8,128)(2,1)}, bf16[128,64,128]{2,1,0:T(8,128)(2,1)}) custom-call(s32[1]{0:T(128)} %bitcast.g_ref, f32[128,256,512]{2,1,0:T(8,128)} %outgoing.1.o_ref, bf16[64,128,512]{2,1,0:T(8,128)(2,1)} %get-tuple-element.44.zt_ref, bf16[64,128,512]{2,1,0:T(8,128)(2,1)} %get-tuple-element.45.znt_ref, f32[64,512]{1,0:T(8,128)} %copy-done.3, ...), custom_call_target="tpu_custom_call" | custom-call | flops 17179869184 | bytes 52428800 | tf_op jit(solution)/shard_map/finish_project/pallas_call | solution.py:280
  484.5 42.1 %finish_project.6 = (bf16[128,64,512]{2,1,0:T(8,128)(2,1)}, bf16[128,64,128]{2,1,0:T(8,128)(2,1)}) custom-call(s32[1]{0:T(128)} %bitcast.g_ref, f32[128,256,512]{2,1,0:T(8,128)} %outgoing.1.o_ref, bf16[64,128,512]{2,1,0:T(8,128)(2,1)} %get-tuple-element.47.zt_ref, bf16[64,128,512]{2,1,0:T(8,128)(2,1)} %get-tuple-element.48.znt_ref, f32[64,512]{1,0:T(8,128)} %copy-done.2, ...), custom_call_target="tpu_custom_call" | custom-call | flops 17179869184 | bytes 52428800 | tf_op jit(solution)/shard_map/finish_project/pallas_call | solution.py:280
  526.6 42.1 %finish_project.7 = (bf16[128,64,512]{2,1,0:T(8,128)(2,1)}, bf16[128,64,128]{2,1,0:T(8,128)(2,1)}) custom-call(s32[1]{0:T(128)} %bitcast.g_ref, f32[128,256,512]{2,1,0:T(8,128)} %outgoing.1.o_ref, bf16[64,128,512]{2,1,0:T(8,128)(2,1)} %get-tuple-element.50.zt_ref, bf16[64,128,512]{2,1,0:T(8,128)(2,1)} %get-tuple-element.51.znt_ref, f32[64,512]{1,0:T(8,128)} %copy-done.1, ...), custom_call_target="tpu_custom_call" | custom-call | flops 17179869184 | bytes 52428800 | tf_op jit(solution)/shard_map/finish_project/pallas_call | solution.py:280
  568.7 39.5 %incoming.1 = (f32[128,64,512]{2,1,0:T(8,128)}, f32[128,64,512]{2,1,0:T(8,128)}) custom-call(s32[1]{0:T(128)} %bitcast.1.h_ref, bf16[128,64,128]{2,1,0:T(8,128)(2,1)} %get-tuple-element.43.refs_0_, bf16[128,64,128]{2,1,0:T(8,128)(2,1)} %get-tuple-element.46.refs_1_, bf16[128,64,128]{2,1,0:T(8,128)(2,1)} %get-tuple-element.49.refs_2_, ...), custom_call_target="tpu_custom_call" | custom-call | flops 4294967296 | bytes 83886080 | tf_op jit(solution)/shard_map/incoming/pallas_call | solution.py:155
  608.3 24.9 %collective-permute-done.11.r_ref = f32[128,64,512]{2,1,0:T(8,128)} collective-permute-done((f32[128,64,512]{2,1,0:T(8,128)}, f32[128,64,512]{2,1,0:T(8,128)}, u32[]{:S(2)}, u32[]{:S(2)}) %collective-permute-start.11) | collective-permute-done | bytes 16777248 | tf_op jit(solution)/shard_map/ppermute | solution.py:365
  634.7 30.8 %finish.1 = bf16[64,512,128]{2,1,0:T(8,128)(2,1)} custom-call(s32[1]{0:T(128)} %bitcast.g_ref, f32[128,64,512]{2,1,0:T(8,128)} %get-tuple-element.57.o_ref, f32[128,64,512]{2,1,0:T(8,128)} %collective-permute-done.11.r_ref, bf16[64,128,512]{2,1,0:T(8,128)(2,1)} %get-tuple-element.59.zt_ref, bf16[64,128,512]{2,1,0:T(8,128)(2,1)} %get-tuple-element.60.znt_ref, ...), custom_call_target="tpu_custom_call" | custom-call | flops 4294967296 | bytes 58982400 | tf_op jit(solution)/shard_map/finish/pallas_call | solution.py:329
  (71 shorter events, 16.5 us)
Async XLA Ops:
  0.0 184.7 %collective-permute-start.2 = (bf16[64,512,128]{2,1,0:T(8,128)(2,1)}, bf16[64,512,128]{2,1,0:T(8,128)(2,1)}, u32[]{:S(2)}, u32[]{:S(2)}) collective-permute-start(bf16[64,512,128]{2,1,0:T(8,128)(2,1)} %z_ref.1), channel_id=1, source_target_pairs={{0,4},{1,5},{2,6},{3,7},{4,0},{5,1},{6,2},{7,3}} | collective-permute-start | bytes 25165832 | tf_op jit(solution)/shard_map/ppermute | solution.py:365
  3.4 186.0 %collective-permute-start = (bf16[64,512,128]{2,1,0:T(8,128)(2,1)}, bf16[64,512,128]{2,1,0:T(8,128)(2,1)}, u32[]{:S(2)}, u32[]{:S(2)}) collective-permute-start(bf16[64,512,128]{2,1,0:T(8,128)(2,1)} %z_ref.1), channel_id=1, source_target_pairs={{0,2},{1,3},{2,0},{3,1},{4,6},{5,7},{6,4},{7,5}} | collective-permute-start | bytes 25165832 | tf_op jit(solution)/shard_map/ppermute | solution.py:365
  5.8 188.2 %copy-start = (f32[64,512]{1,0:T(8,128)}, f32[64,512]{1,0:T(8,128)S(1)}, u32[]{:S(2)}) copy-start(f32[64,512]{1,0:T(8,128)S(1)} %convert_element_type.83.m_ref) | copy-start | bytes 393220
  5.8 214.7 %collective-permute-start.1 = (f32[64,512]{1,0:T(8,128)S(1)}, f32[64,512]{1,0:T(8,128)S(1)}, u32[]{:S(2)}, u32[]{:S(2)}) collective-permute-start(f32[64,512]{1,0:T(8,128)S(1)} %convert_element_type.83.m_ref), channel_id=1, source_target_pairs={{0,2},{1,3},{2,0},{3,1},{4,6},{5,7},{6,4},{7,5}} | collective-permute-start | bytes 393224 | tf_op jit(solution)/shard_map/ppermute | solution.py:365
  6.3 238.4 %collective-permute-start.3 = (f32[64,512]{1,0:T(8,128)S(1)}, f32[64,512]{1,0:T(8,128)S(1)}, u32[]{:S(2)}, u32[]{:S(2)}) collective-permute-start(f32[64,512]{1,0:T(8,128)S(1)} %convert_element_type.83.m_ref), channel_id=1, source_target_pairs={{0,4},{1,5},{2,6},{3,7},{4,0},{5,1},{6,2},{7,3}} | collective-permute-start | bytes 393224 | tf_op jit(solution)/shard_map/ppermute | solution.py:365
  6.4 285.2 %collective-permute-start.6 = (f32[64,512]{1,0:T(8,128)S(1)}, f32[64,512]{1,0:T(8,128)S(1)}, u32[]{:S(2)}, u32[]{:S(2)}) collective-permute-start(f32[64,512]{1,0:T(8,128)S(1)} %convert_element_type.83.m_ref), channel_id=1, source_target_pairs={{0,6},{1,7},{2,4},{3,5},{4,2},{5,3},{6,0},{7,1}} | collective-permute-start | bytes 393224 | tf_op jit(solution)/shard_map/ppermute | solution.py:365
  187.3 93.5 %collective-permute-start.5 = (bf16[32,512,128]{2,1,0:T(8,128)(2,1)S(1)}, bf16[32,512,128]{2,1,0:T(8,128)(2,1)}, u32[]{:S(2)}, u32[]{:S(2)}) collective-permute-start(bf16[32,512,128]{2,1,0:T(8,128)(2,1)S(1)} %slice.109), channel_id=1, source_target_pairs={{0,2},{1,3},{2,0},{3,1},{4,6},{5,7},{6,4},{7,5}} | collective-permute-start | bytes 12582920 | tf_op jit(solution)/shard_map/ppermute | solution.py:365
  193.9 90.1 %collective-permute-start.4 = (bf16[32,512,128]{2,1,0:T(8,128)(2,1)}, bf16[32,512,128]{2,1,0:T(8,128)(2,1)}, u32[]{:S(2)}, u32[]{:S(2)}) collective-permute-start(bf16[32,512,128]{2,1,0:T(8,128)(2,1)} %slice.108), channel_id=1, source_target_pairs={{0,4},{1,5},{2,6},{3,7},{4,0},{5,1},{6,2},{7,3}} | collective-permute-start | bytes 12582920 | tf_op jit(solution)/shard_map/ppermute | solution.py:365
  220.5 0.7 copy-start.3
  220.5 98.6 %collective-permute-start.7 = (bf16[128,64,512]{2,1,0:T(8,128)(2,1)}, bf16[128,64,512]{2,1,0:T(8,128)(2,1)}, u32[]{:S(2)}, u32[]{:S(2)}) collective-permute-start(bf16[128,64,512]{2,1,0:T(8,128)(2,1)} %get-tuple-element.37.refs_4_), channel_id=1, source_target_pairs={{0,1},{1,0},{2,3},{3,2},{4,5},{5,4},{6,7},{7,6}} | collective-permute-start | bytes 25165832 | tf_op jit(solution)/shard_map/ppermute | solution.py:365
  244.7 0.7 copy-start.2
  244.7 74.4 %collective-permute-start.8 = (bf16[128,64,512]{2,1,0:T(8,128)(2,1)}, bf16[128,64,512]{2,1,0:T(8,128)(2,1)}, u32[]{:S(2)}, u32[]{:S(2)}) collective-permute-start(bf16[128,64,512]{2,1,0:T(8,128)(2,1)} %get-tuple-element.38.refs_5_), channel_id=1, source_target_pairs={{0,1},{1,0},{2,3},{3,2},{4,5},{5,4},{6,7},{7,6}} | collective-permute-start | bytes 25165832 | tf_op jit(solution)/shard_map/ppermute | solution.py:365
  280.8 38.3 %collective-permute-start.9 = (bf16[128,64,512]{2,1,0:T(8,128)(2,1)}, bf16[128,64,512]{2,1,0:T(8,128)(2,1)}, u32[]{:S(2)}, u32[]{:S(2)}) collective-permute-start(bf16[128,64,512]{2,1,0:T(8,128)(2,1)} %get-tuple-element.39.refs_6_), channel_id=1, source_target_pairs={{0,1},{1,0},{2,3},{3,2},{4,5},{5,4},{6,7},{7,6}} | collective-permute-start | bytes 25165832 | tf_op jit(solution)/shard_map/ppermute | solution.py:365
  291.6 24.4 %copy-start.9 = (bf16[2,128]{1,0:T(2,128)(2,1)S(1)}, bf16[2,128]{1,0:T(2,128)(2,1)}, u32[]{:S(2)}) copy-start(bf16[2,128]{1,0:T(2,128)(2,1)} %param.16) | copy-start | bytes 1540
  291.6 24.6 %copy-start.4 = (bf16[2,128,128]{2,1,0:T(8,128)(2,1)S(1)}, bf16[2,128,128]{2,1,0:T(8,128)(2,1)}, u32[]{:S(2)}) copy-start(bf16[2,128,128]{2,1,0:T(8,128)(2,1)} %param.15) | copy-start | bytes 196612
  291.6 24.9 %copy-start.10 = (bf16[2,128]{1,0:T(2,128)(2,1)S(1)}, bf16[2,128]{1,0:T(2,128)(2,1)}, u32[]{:S(2)}) copy-start(bf16[2,128]{1,0:T(2,128)(2,1)} %param.19) | copy-start | bytes 1540
  291.6 25.1 %copy-start.5 = (bf16[2,128,128]{2,1,0:T(8,128)(2,1)S(1)}, bf16[2,128,128]{2,1,0:T(8,128)(2,1)}, u32[]{:S(2)}) copy-start(bf16[2,128,128]{2,1,0:T(8,128)(2,1)} %param.18) | copy-start | bytes 196612
  291.6 26.2 %copy-start.6 = (bf16[2,2,128]{2,1,0:T(2,128)(2,1)S(1)}, bf16[2,2,128]{2,1,0:T(2,128)(2,1)}, u32[]{:S(2)}) copy-start(bf16[2,2,128]{2,1,0:T(2,128)(2,1)} %param.17) | copy-start | bytes 3076
  291.6 0.6 copy-start.1
  315.9 13.1 %collective-permute-start.10 = (bf16[128,64,512]{2,1,0:T(8,128)(2,1)}, bf16[128,64,512]{2,1,0:T(8,128)(2,1)}, u32[]{:S(2)}, u32[]{:S(2)}) collective-permute-start(bf16[128,64,512]{2,1,0:T(8,128)(2,1)} %get-tuple-element.40.refs_7_), channel_id=1, source_target_pairs={{0,1},{1,0},{2,3},{3,2},{4,5},{5,4},{6,7},{7,6}} | collective-permute-start | bytes 25165832 | tf_op jit(solution)/shard_map/ppermute | solution.py:365
  568.7 64.6 %copy-start.8 = (f32[128]{0:T(128)S(1)}, f32[128]{0:T(128)}, u32[]{:S(2)}) copy-start(f32[128]{0:T(128)} %get-tuple-element.72) | copy-start | bytes 1540
  568.7 65.3 %copy-start.7 = (f32[128]{0:T(128)S(1)}, f32[128]{0:T(128)}, u32[]{:S(2)}) copy-start(f32[128]{0:T(128)} %get-tuple-element.69) | copy-start | bytes 1540
  608.2 25.1 %collective-permute-start.11 = (f32[128,64,512]{2,1,0:T(8,128)}, f32[128,64,512]{2,1,0:T(8,128)}, u32[]{:S(2)}, u32[]{:S(2)}) collective-permute-start(f32[128,64,512]{2,1,0:T(8,128)} %get-tuple-element.58), channel_id=1, source_target_pairs={{0,1},{1,0},{2,3},{3,2},{4,5},{5,4},{6,7},{7,6}} | collective-permute-start | bytes 50331656 | tf_op jit(solution)/shard_map/ppermute | solution.py:365

commit v2 on v1

v2 whole, which is shorter than its diff:
```python
import functools

import jax
import jax.numpy as jnp
from jax import lax
from jax.experimental import pallas as pl
from jax.experimental.pallas import tpu as pltpu
from jax.sharding import PartitionSpec as P


f32, bf16 = jnp.float32, jnp.bfloat16
LN_EPS = 1e-5
CH = 128
EXT = CH + 16
ROWS = 16
PITCH = 24
ROW_PITCH = 136
VMEM = 56 * 2**20


def norm_columns(x, scale, offset):
    mean = jnp.sum(x, axis=0, keepdims=True) * (1.0 / CH)
    centred = x - mean
    var = jnp.sum(centred * centred, axis=0, keepdims=True) * (1.0 / CH)
    return centred * lax.rsqrt(var + LN_EPS) * scale + offset


def extend(columns, row):
    n = columns.shape[1]
    first = lax.broadcasted_iota(jnp.int32, (16, n), 0) == 0
    extra = jnp.where(first, jnp.broadcast_to(row, (16, n)), 0.0).astype(bf16)
    return jnp.concatenate([columns, extra], axis=0)


def twice(ref):
    return jnp.concatenate([ref[...]] * 2, axis=1)


def store_gated(proj, store):
    for q in range(proj.shape[0] // 16):
        value, gate = proj[16 * q:16 * q + 8], proj[16 * q + 8:16 * q + 16]
        side = (jnp.tanh(gate) + 1.0) * value
        for t in range(2):
            store(q, t, side[:, 128 * t:128 * t + 128])


def piece_start(chip, slot, piece):
    core, half = piece // 2, piece % 2
    middle = (slot == 1) | (slot == 2)
    other = jnp.where(middle, half + 1, slot)
    offset = jnp.where(middle, slot - 1, half)
    return pl.multiple_of((other ^ chip) * 128 + core * 64 + offset * 32, 32)


def project_body(g_ref, z_ref, m_ref, w_ref, sc_ref, of_ref, *refs):
    a_ref, zt_ref, znt_ref, b_ref, scr = refs[-5:]
    starts = [piece_start(g_ref[0], 2 * pl.program_id(1) + p // 4, p % 4) for p in range(8)]
    scale, offset = twice(sc_ref), twice(of_ref)

    def row(i, carry):
        zt = jnp.concatenate([z_ref[i, pl.ds(start, 32), :] for start in starts], axis=0).T
        zt_ref[i] = zt
        zn = norm_columns(zt.astype(f32), scale, offset).astype(bf16)
        znt_ref[i] = zn
        m = m_ref[pl.ds(i, 1), :]
        proj = jnp.dot(w_ref[...], extend(zn * m.astype(bf16), m), preferred_element_type=f32)

        def store(q, t, tile):
            scr[t, pl.ds(8 * q * PITCH + i, 8, stride=PITCH), :] = tile

        store_gated(proj, store)
        return carry

    lax.fori_loop(0, ROWS, row, 0, unroll=8)
    for side, out in ((0, a_ref), (1, b_ref)):
        def channel(q, carry):
            for u in range(16):
                c = q * 16 + u
                start = pl.multiple_of((side * CH + c) * PITCH, 8)
                for t in range(2):
                    out[c, :, 128 * t:128 * t + 128] = scr[t, pl.ds(start, ROWS), :].astype(bf16)
            return carry

        lax.fori_loop(0, CH // 16, channel, 0)


def whole(*shape):
    return pl.BlockSpec(shape, lambda *ids: (0,) * len(shape))


def params(n=1):
    return pltpu.CompilerParams(dimension_semantics=("arbitrary",) * n, vmem_limit_bytes=VMEM)


def cost(flops, nbytes):
    return pl.CostEstimate(flops=flops, bytes_accessed=nbytes, transcendentals=0)


ANY = pl.BlockSpec(memory_space=pl.ANY)


def project(chip, z, m, w, scale, offset, row, slot_rows, filled):
    rows, cols, _ = z.shape
    all_rows = m.shape[0]
    first, slot_first = row // ROWS, row % slot_rows // ROWS
    side = lambda at: pl.BlockSpec((CH, ROWS, 256), lambda i, k: (0, i + at, k))
    return pl.pallas_call(
        project_body,
        grid=(rows // ROWS, cols // 256),
        in_specs=[pl.BlockSpec(memory_space=pltpu.SMEM),
                  pl.BlockSpec((ROWS, cols, CH), lambda i, k: (i, 0, 0)),
                  pl.BlockSpec((ROWS, 256), lambda i, k: (i + first, k)),
                  whole(4 * CH, EXT), whole(CH, CH), whole(CH, CH)] + [ANY] * len(filled),
        out_specs=[side(first)] + [pl.BlockSpec((ROWS, CH, 256), lambda i, k: (i + first, 0, k))] * 2 + [side(slot_first)],
        out_shape=[jax.ShapeDtypeStruct((CH, all_rows, cols), bf16)]
        + [jax.ShapeDtypeStruct((all_rows, CH, cols), bf16)] * 2 + [jax.ShapeDtypeStruct((CH, slot_rows, cols), bf16)],
        input_output_aliases={6 + k: k for k in range(len(filled))},
        scratch_shapes=[pltpu.VMEM((2, 2 * CH * PITCH, 128), f32)],
        compiler_params=params(2),
        cost_estimate=cost(rows * cols * 2**19, rows * cols * 1200),
        name="project",
    )(chip, z, m, w, scale, offset, *filled)


def incoming_body(h_ref, a_ref, b_ref, keep_ref, send_ref, scr):
    at_mine, at_theirs = pl.multiple_of(64 * h_ref[0], 64), pl.multiple_of(64 - 64 * h_ref[0], 64)
    for c in range(keep_ref.shape[0]):
        scr[c] = lax.dot_general(a_ref[c], b_ref[c], (((0,), (0,)), ((), ())), preferred_element_type=f32)
        keep_ref[c] = scr[c, pl.ds(at_mine, 64), :]
        send_ref[c] = scr[c, pl.ds(at_theirs, 64), :]


def incoming(h, a, b, part, width):
    block = 16
    out = jax.ShapeDtypeStruct((CH, 64, width), f32)
    return pl.pallas_call(
        incoming_body,
        grid=(CH // block,),
        in_specs=[pl.BlockSpec(memory_space=pltpu.SMEM),
                  pl.BlockSpec((block,) + a.shape[1:], lambda c: (c, 0, 0)),
                  pl.BlockSpec((block, b.shape[1], width), lambda c: (c, 0, part))],
        out_specs=[pl.BlockSpec((block, 64, width), lambda c: (c, 0, 0))] * 2,
        out_shape=[out, out],
        scratch_shapes=[pltpu.VMEM((block, 128, width), f32)],
        compiler_params=params(),
        cost_estimate=cost(2**23 * width, 160 * 2**10 * width),
        name="incoming",
    )(h, a, b)


def normalize_rows(load, scr):
    groups = range(ROWS // 8)
    for gs in ([list(groups)] if 1 else [[g] for g in groups]):
        zeros = tuple(jnp.zeros((8, 128), f32) for _ in range(4 * len(gs)))

        def add(q, sums):
            sums = list(sums)
            for u in range(64):
                for n, g in enumerate(gs):
                    sums[4 * n + u % 4] += load(q * 64 + u, g)
            return tuple(sums)

        def total(s, n):
            s = list(s[4 * n:4 * n + 4])
            while len(s) > 1:
                s = [s[2 * k] + s[2 * k + 1] for k in range(len(s) // 2)]
            return s[0] * (1.0 / CH)

        s = lax.fori_loop(0, CH // 64, add, zeros)
        means = [total(s, n) for n in range(len(gs))]

        def add_square(q, sums):
            sums = list(sums)
            for u in range(64):
                for n, g in enumerate(gs):
                    centred = load(q * 64 + u, g) - means[n]
                    sums[4 * n + u % 4] += centred * centred
            return tuple(sums)

        s = lax.fori_loop(0, CH // 64, add_square, zeros)
        rstds = [lax.rsqrt(total(s, n) + LN_EPS) for n in range(len(gs))]

        def put(q, carry):
            for u in range(64):
                c = q * 64 + u
                for n, g in enumerate(gs):
                    scr[pl.ds(8 * g * ROW_PITCH + c, 8, stride=ROW_PITCH), :] = (load(c, g) - means[n]) * rstds[n]
            return carry

        lax.fori_loop(0, CH // 64, put, 0)


def pair_of(ref, p):
    return jnp.concatenate([ref[2 * p], ref[2 * p + 1]], axis=1)


def update_pair(p, scr, zt_ref, znt_ref, wo_ref, wg_ref, scale, offset, ones):
    start = pl.multiple_of(2 * p * ROW_PITCH, 8)
    normed = jnp.concatenate([scr[pl.ds(start, CH), :], scr[pl.ds(start + ROW_PITCH, CH), :]], axis=1)
    u = (normed * scale + offset).astype(bf16)
    update = jnp.dot(wo_ref[...], extend(u, ones), preferred_element_type=f32)
    gate = jnp.dot(wg_ref[...], extend(pair_of(znt_ref, p), ones), preferred_element_type=f32)
    return (pair_of(zt_ref, p).astype(f32) + (jnp.tanh(gate) + 1.0) * update).astype(bf16)


def block_body(n, with_left, with_pair, h_ref, a_ref, *refs):
    mine, theirs, refs = refs[:n], refs[n:2 * n], list(refs[2 * n:])
    sums, both = refs[-2:]
    step = pl.program_id(0)
    per_step = a_ref.shape[0]
    sum_steps = CH // per_step

    @pl.when(step < sum_steps)
    def _():
        at_mine, at_theirs = pl.multiple_of(64 * h_ref[0], 64), pl.multiple_of(64 - 64 * h_ref[0], 64)

        def channel(c, carry):
            for s in range(n):
                both[c, pl.ds(128 * s + at_mine, 64), :] = mine[s][c]
                both[c, pl.ds(128 * s + at_theirs, 64), :] = theirs[s][c]
            o = lax.dot_general(a_ref[c], both[c], (((1,), (1,)), ((), ())), preferred_element_type=f32)
            for s in range(n):
                sums[s, step * per_step + c] = o[:, 128 * s:128 * s + 128]
            return carry

        lax.fori_loop(0, per_step, channel, 0, unroll=4)

    @pl.when(step >= sum_steps)
    def _():
        at = step - sum_steps
        tile, row = at % n, pl.multiple_of(at // n * ROWS, ROWS)
        finish_project_body(with_left, with_pair, tile, lambda c, g: sums[tile, c, pl.ds(row + 8 * g, 8), :], *refs[:-2])


def finish_project_body(with_left, with_pair, tile, load, zt_ref, znt_ref, m_ref, wo_ref, wg_ref, so_ref, oo_ref,
                        w_ref, si_ref, oi_ref, *refs):
    refs = list(refs)[-(4 + with_left + 2 * with_pair):]
    b_ref = refs.pop(0)
    z1_ref, zn1_ref = (refs.pop(0), refs.pop(0)) if with_pair else (None, None)
    a_ref = refs.pop(0) if with_left else None
    scr, scr2, exts = refs
    normalize_rows(load, scr)
    scale_out, offset_out = twice(so_ref), twice(oo_ref)
    scale_in, offset_in = twice(si_ref), twice(oi_ref)
    ones = jnp.ones((1, 256), f32)

    def put(p):
        def store(q, t, tile):
            scr2[pl.ds(8 * q * PITCH + 2 * p + t, 8, stride=PITCH), :] = tile

        return store

    def pair(p, carry):
        z1 = update_pair(p, scr, zt_ref, znt_ref, wo_ref, wg_ref, scale_out, offset_out, ones)
        zn1 = norm_columns(z1.astype(f32), scale_in, offset_in).astype(bf16)
        if with_pair:
            for t in range(2):
                z1_ref[2 * p + t] = z1[:, 128 * t:128 * t + 128]
                zn1_ref[2 * p + t] = zn1[:, 128 * t:128 * t + 128]
        m = jnp.concatenate([m_ref[pl.ds(2 * p, 1), :], m_ref[pl.ds(2 * p + 1, 1), :]], axis=1)
        ext = extend(zn1 * m.astype(bf16), m)
        if with_left:
            exts[p] = ext
        store_gated(jnp.dot(w_ref[2 * CH:], ext, preferred_element_type=f32), put(p))
        return carry

    def emit(out):
        def channel(q, carry):
            for u in range(32):
                c = q * 32 + u
                out[c] = scr2[pl.ds(pl.multiple_of(c * PITCH, 8), ROWS), :].astype(bf16)
            return carry

        lax.fori_loop(0, CH // 32, channel, 0)

    lax.fori_loop(0, ROWS // 2, pair, 0, unroll=8)
    emit(b_ref)
    if with_left:
        @pl.when(tile == 0)
        def _():
            def left(p, carry):
                store_gated(jnp.dot(w_ref[:2 * CH], exts[p], preferred_element_type=f32), put(p))
                return carry

            lax.fori_loop(0, ROWS // 2, left, 0, unroll=8)
            emit(a_ref)


def block(core, a, mine, theirs, zt, znt, m, row, rows, first, ln_out, layer1, layer2, with_pair, filled):
    n, per_step = len(mine), 16
    all_rows, _, cols = zt.shape
    with_left = first == 0
    sum_steps, row_block = CH // per_step, row // ROWS

    def at(index):
        def block_index(t):
            f = jnp.maximum(t - sum_steps, 0)
            return index(row_block + f // n, first + f % n)

        return block_index

    def sides(rows, block):
        return pl.BlockSpec((per_step, rows, cols), lambda t: (jnp.minimum(t, sum_steps - 1), block, 0))

    positions = pl.BlockSpec((ROWS, CH, 128), at(lambda i, j: (i, 0, j)))
    out_specs = [pl.BlockSpec((CH, ROWS, 128), at(lambda i, j: (0, i, j)))]
    out_shape = [jax.ShapeDtypeStruct((CH, all_rows, cols), bf16)]
    if with_pair:
        out_specs += [positions] * 2
        out_shape += [jax.ShapeDtypeStruct((all_rows, CH, cols), bf16)] * 2
    if with_left:
        out_specs.append(pl.BlockSpec((CH, ROWS, 128), at(lambda i, j: (0, i, 0))))
        out_shape.append(jax.ShapeDtypeStruct((CH, all_rows, 128), bf16))
    return pl.pallas_call(
        functools.partial(block_body, n, with_left, with_pair),
        grid=(sum_steps + rows // ROWS * n,),
        in_specs=[pl.BlockSpec(memory_space=pltpu.SMEM), sides(rows, row // rows)] + [sides(64, 0)] * (2 * n)
        + [positions, positions, pl.BlockSpec((ROWS, 128), at(lambda i, j: (i, j))),
           whole(CH, EXT), whole(CH, EXT), whole(CH, CH), whole(CH, CH),
           whole(4 * CH, EXT), whole(CH, CH), whole(CH, CH)] + [ANY] * len(filled),
        out_specs=out_specs,
        out_shape=out_shape,
        scratch_shapes=[pltpu.VMEM((ROWS * ROW_PITCH, 128), f32), pltpu.VMEM((CH * PITCH, 128), f32),
                        pltpu.VMEM((ROWS // 2, EXT, 256), bf16),
                        pltpu.VMEM((n, CH, rows, 128), f32), pltpu.VMEM((per_step, 128 * n, cols), bf16)],
        input_output_aliases={12 + 2 * n + k: k for k in range(len(filled))},
        compiler_params=params(),
        cost_estimate=cost(rows * n * 128 * 2**19, rows * n * 128 * 1600),
        name="block",
    )(core, a, *mine, *theirs, zt, znt, m, layer1["w_out"], layer1["w_gate"], ln_out[0], ln_out[1],
      layer2["w_proj"], layer2["ln_in"][0], layer2["ln_in"][1], *filled)


def finish_body(slot0, g_ref, o_ref, r_ref, zt_ref, znt_ref, wo_ref, wg_ref, so_ref, oo_ref, *refs):
    out_ref, scr, total, rows_out, sems = refs[-5:]
    step, last = pl.program_id(0) * pl.num_programs(1) + pl.program_id(1), pl.num_programs(0) * pl.num_programs(1) - 1
    buffer = step % 2

    def copies(step):
        i, slot, buffer = step // pl.num_programs(1), slot0 + step % pl.num_programs(1), step % 2
        row = pl.multiple_of(i * ROWS, ROWS)
        return [pltpu.make_async_copy(rows_out.at[buffer, :, pl.ds(32 * p, 32), :],
                                      out_ref.at[pl.ds(row, ROWS), pl.ds(piece_start(g_ref[0], slot, p), 32), :],
                                      sems.at[buffer, p]) for p in range(4)]

    def add(q, carry):
        for u in range(8):
            total[q * 8 + u] = o_ref[q * 8 + u] + r_ref[q * 8 + u]
        return carry

    lax.fori_loop(0, CH // 8, add, 0)
    normalize_rows(lambda c, g: total[c, 8 * g:8 * g + 8, :], scr)
    scale, offset = twice(so_ref), twice(oo_ref)
    ones = jnp.ones((1, 256), f32)

    def pair(p, carry):
        z2 = update_pair(p, scr, zt_ref, znt_ref, wo_ref, wg_ref, scale, offset, ones).T
        for t in range(2):
            rows_out[buffer, 2 * p + t] = z2[128 * t:128 * t + 128]
        return carry

    lax.fori_loop(0, ROWS // 2, pair, 0, unroll=8)
    for copy in copies(step):
        copy.start()

    @pl.when(step > 0)
    def _():
        for copy in copies(step - 1):
            copy.wait()

    @pl.when(step == last)
    def _():
        for copy in copies(step):
            copy.wait()


def finish(chip, o, received, zt, znt, layer2, part, filled):
    _, rows, cols = o.shape
    n = cols // 128
    sums = pl.BlockSpec((CH, ROWS, 128), lambda i, j: (0, i, j))
    positions = pl.BlockSpec((ROWS, CH, 128), lambda i, j: (i, 0, j + n * part))
    return pl.pallas_call(
        functools.partial(finish_body, n * part),
        grid=(rows // ROWS, n),
        in_specs=[pl.BlockSpec(memory_space=pltpu.SMEM), sums, sums, positions, positions,
                  whole(CH, EXT), whole(CH, EXT), whole(CH, CH), whole(CH, CH)] + [ANY] * len(filled),
        out_specs=ANY,
        out_shape=jax.ShapeDtypeStruct((rows, zt.shape[2], CH), bf16),
        input_output_aliases={9 + k: k for k in range(len(filled))},
        scratch_shapes=[pltpu.VMEM((ROWS * ROW_PITCH, 128), f32), pltpu.VMEM((CH, ROWS, 128), f32),
                        pltpu.VMEM((2, ROWS, 128, CH), bf16), pltpu.SemaphoreType.DMA((2, 4))],
        compiler_params=params(2),
        cost_estimate=cost(rows * cols * 2**17, rows * cols * 1800),
        name="finish",
    )(chip, o, received, zt, znt, layer2["w_out"], layer2["w_gate"], layer2["ln_out"][0], layer2["ln_out"][1], *filled)


def in_slot_order(masks, chip):
    r = masks.reshape(-1, 2, 2, 2, 2, 32)
    r = jnp.where(chip % 2 == 1, r[:, :, ::-1], r)
    r = jnp.where(chip // 2 == 1, r[:, ::-1], r)
    near = jnp.stack([r[:, 0, 1], r[:, 1, 0]], axis=3)
    slots = [r[:, 0, 0], near[:, :, 0], near[:, :, 1], r[:, 1, 1]]
    return jnp.concatenate([slot.reshape(-1, 128) for slot in slots], axis=1)


def with_bias(w, b):
    n = w.shape[1]
    return jnp.concatenate([w.T, b[:, None], jnp.zeros((n, EXT - CH - 1), bf16)], axis=1) * jnp.asarray(0.5, bf16)


def layer_params(ln_in, w_proj, b_proj, w_gate, b_gate, ln_out, w_out, b_out):
    lanes = lambda v: jnp.broadcast_to(v.astype(f32)[:, None], (CH, CH))
    proj = with_bias(w_proj, b_proj).reshape(2, 2, CH // 8, 8, EXT).transpose(0, 2, 1, 3, 4).reshape(4 * CH, EXT)
    gate, out = with_bias(w_gate, b_gate), with_bias(w_out, b_out)
    return {"w_proj": proj, "w_gate": gate, "w_out": out,
            "ln_in": (lanes(ln_in[0]), lanes(ln_in[1])), "ln_out": (lanes(ln_out[0]), lanes(ln_out[1]))}


def solution(mesh):
    row_spec = P(("batch", "dap"), None, None)
    mask_spec = P(("batch", "dap"), None)
    n = mesh.shape["dap"]

    def swap(x, bits):
        return lax.ppermute(x, "dap", [(i, i ^ bits) for i in range(n)])

    def layers(pair, pair_mask, ln_in, w_proj, b_proj, w_gate, b_gate, ln_out, w_out, b_out):
        layer1, layer2 = (layer_params(ln_in[l], w_proj[l], b_proj[l], w_gate[l], b_gate[l], ln_out[l], w_out[l],
                                       b_out[l]) for l in range(2))
        me = lax.axis_index("dap")
        chip, core = (me // 2).reshape(1).astype(jnp.int32), (me % 2).reshape(1).astype(jnp.int32)
        rows = pair.shape[0]
        half = rows // 2

        mask = pair_mask.astype(f32)
        x_mask, y_mask = swap(mask, 2), swap(mask, 4)
        far_mask = swap(mask, 6)
        masks = in_slot_order(jnp.concatenate([mask, x_mask[:half], y_mask[:half], x_mask[half:], y_mask[half:], far_mask]),
                              chip[0])
        top, bottom = lax.optimization_barrier((pair[:half], pair[half:]))
        x_top, y_top = swap(top, 2), swap(top, 4)
        x_bottom, y_bottom = swap(bottom, 2), swap(bottom, 4)
        x_top_on, y_bottom_on, _, _ = lax.optimization_barrier((x_top, y_bottom, x_bottom, y_top))
        pieces = [[pair], [x_top, y_top], [x_bottom, y_bottom],
                  [swap(x_top_on, 4), swap(y_bottom_on, 2)]]

        step = [(top, bottom)]

        def next_step(small):
            return lax.optimization_barrier((small, step[0]))[0]

        def ran(outputs):
            step[0] = outputs[0]
            return outputs

        mine, theirs = [], []
        left = zt = znt = None
        b2 = a2 = None
        z1 = ()
        for s in range(4):
            made = ()
            for at, piece in enumerate(pieces[s]):
                scale, offset = layer1["ln_in"]
                filled = (left, zt, znt) + made if s or at else ()
                left, zt, znt, b = ran(project(chip, piece, masks, layer1["w_proj"], next_step(scale), offset,
                                               rows * s + half * at, rows, filled))
                made = (b,)
            mine.append(b)
            theirs.append(swap(b, 1))
            if s:
                b2, a2 = ran(block(core, left, mine[:s], theirs[:s], zt, znt, masks, rows * s, rows, 0,
                                   next_step(layer1["ln_out"]), layer1, layer2, False, (b2, a2)))
            out = ran(block(core, left, mine[s:], theirs[s:], zt, znt, masks, 0, rows * (s + 1), s,
                            next_step(layer1["ln_out"]), layer1, layer2, True, (b2, *z1) if s else ()))
            b2, z1 = out[0], out[1:3]
            if not s:
                a2 = out[3]

        parts, out = [], ()
        for part in range(2):
            keep, send = ran(incoming(next_step(core), a2, b2, part, 256))
            parts.append((keep, swap(send, 1)))
        for part, (keep, received) in enumerate(parts):
            out = (finish(chip, keep, received, *z1, layer2, part, out),)
        return out[0]

    return jax.shard_map(layers, mesh=mesh,
                         in_specs=(row_spec, mask_spec, P(), P(), P(), P(), P(), P(), P(), P()),
                         out_specs=row_spec, check_vma=False)
```

time: 667 us -> 583 us (0.87)
  waiting for transfers between devices: 221 us -> 103 us
  Pallas kernels: 402 us -> 437 us
  other arithmetic: 10.5 us -> 3.18 us
    ppermute x12 -> x15, waiting for transfers between devices: 221 us -> 103 us  [swap(): return lax.ppermute(x, 'dap', [(i, i ^ bits) for i in range(n)])]
    pallas_call x7 -> x11, Pallas kernels: 307 us -> 327 us  [the longest x7 263 us: block(): pl.pallas_call(functools.partial(block_body, n, with_left, with_pair), gr...]
    pallas_call x4 -> x7, Pallas kernels: 94.5 us -> 110 us  [project(): pl.pallas_call(project_body, grid=(rows // ROWS, cols // 256), in_specs=[...]
    ppermute x12 -> x15, starting transfers between devices: 12.1 us -> 15.1 us  [swap(): return lax.ppermute(x, 'dap', [(i, i ^ bits) for i in range(n)])]
  transfers between devices with their start and end apart: 12 -> 15, of which waited for: 5 -> 5; matrix products, arithmetic and copies ran while one was open for 4% -> 3% of each run, Pallas kernels for 14% -> 49%
where the time goes in v2:
time: 583 us; the launch traced here: 582 us
  Pallas kernels  437 us (75%)
  waiting for transfers between devices  103 us (18%)
  local copies, waits for them, and re-layouts  22.9 us (4%)
  starting transfers between devices  15.1 us (3%)
    pallas_call x7, Pallas kernels, block(): pl.pallas_call(functools.partial(block_body, n, with_left, with_pair), gr...  263 us
    pallas_call x7, Pallas kernels, project(): pl.pallas_call(project_body, grid=(rows // ROWS, cols // 256), in_specs=[...  110 us
    ppermute x15, waiting for transfers between devices, swap(): return lax.ppermute(x, 'dap', [(i, i ^ bits) for i in range(n)])  103 us
    pallas_call x2, Pallas kernels, incoming(): pl.pallas_call(incoming_body, grid=(CH // block,), in_specs=[pl.BlockSpec...  34.1 us
    pallas_call x2, Pallas kernels, finish(): pl.pallas_call(functools.partial(finish_body, n * part), grid=(rows // RO...  29.5 us
    ppermute x15, starting transfers between devices, swap(): return lax.ppermute(x, 'dap', [(i, i ^ bits) for i in range(n)])  15.1 us
  transfers between devices with their start and end apart: 15, of which 5 were waited for; matrix products, arithmetic and copies ran while one was open for 3% of the time, Pallas kernels for 49%

profile of v2, /device:TPU:0, one launch (start us, length us, event | category | flops | bytes accessed | tf_op | source)
XLA Modules:
  0.0 581.7 jit_solution(11554227031250233671)
XLA Ops:
  1.1 3.4 collective-permute-start.6
  6.7 6.0 %fusion.3 = (bf16[32,512,128]{2,1,0:T(8,128)(2,1)}, bf16[32,512,128]{2,1,0:T(8,128)(2,1)}) fusion(bf16[64,512,128]{2,1,0:T(8,128)(2,1)} %z_ref.1), kind=kLoop, calls=%fused_computation.31 | loop fusion | bytes 16777216 | tf_op jit(solution)/shard_map/slice | solution.py:441
  20.2 25.0 %project.7 = (bf16[128,256,512]{2,1,0:T(8,128)(2,1)}, bf16[256,128,512]{2,1,0:T(8,128)(2,1)}, bf16[256,128,512]{2,1,0:T(8,128)(2,1)}, bf16[128,64,512]{2,1,0:T(8,128)(2,1)}) custom-call(s32[1]{0:T(128)} %bitcast.g_ref, bf16[64,512,128]{2,1,0:T(8,128)(2,1)} %z_ref.1, f32[256,512]{1,0:T(8,128)} %pad_maximum_fusion.m_ref.refs_4_.refs_6_.refs_8_, ...), custom_call_target="tpu_custom_call" | custom-call | flops 17179869184 | bytes 39321600 | tf_op jit(solution)/shard_map/project/pallas_call | solution.py:107
  53.1 5.7 collective-permute-done.9.refs_1_.refs_2_.refs_3_
  60.1 25.2 %block.7 = (bf16[128,256,512]{2,1,0:T(8,128)(2,1)}, bf16[256,128,512]{2,1,0:T(8,128)(2,1)}, bf16[256,128,512]{2,1,0:T(8,128)(2,1)}, bf16[128,256,128]{2,1,0:T(8,128)(2,1)}) custom-call(s32[1]{0:T(128)} %bitcast.1.h_ref, bf16[128,256,512]{2,1,0:T(8,128)(2,1)} %get-tuple-element.88.a_ref.refs_0_, bf16[128,64,512]{2,1,0:T(8,128)(2,1)} %get-tuple-element.89.refs_0_, ...), custom_call_target="tpu_custom_call" | custom-call | flops 4294967296 | bytes 13107200 | tf_op jit(solution)/shard_map/block/pallas_call | solution.py:314
  85.3 53.2 %collective-permute-done.z_ref = bf16[32,512,128]{2,1,0:T(8,128)(2,1)} collective-permute-done((bf16[32,512,128]{2,1,0:T(8,128)(2,1)}, bf16[32,512,128]{2,1,0:T(8,128)(2,1)}, u32[]{:S(2)}, u32[]{:S(2)}) %collective-permute-start) | collective-permute-done | bytes 4194336 | tf_op jit(solution)/shard_map/ppermute | solution.py:426
  138.5 14.1 %project.8 = (bf16[128,256,512]{2,1,0:T(8,128)(2,1)}, bf16[256,128,512]{2,1,0:T(8,128)(2,1)}, bf16[256,128,512]{2,1,0:T(8,128)(2,1)}, bf16[128,64,512]{2,1,0:T(8,128)(2,1)}) custom-call(s32[1]{0:T(128)} %bitcast.g_ref, bf16[32,512,128]{2,1,0:T(8,128)(2,1)} %collective-permute-done.z_ref, ...), custom_call_target="tpu_custom_call", output_to_operand_aliasing={{0}: (6, {}), {1}: (7, {}), {2}: (8, {})} | custom-call | flops 8589934592 | bytes 19660800 | tf_op jit(solution)/shard_map/project/pallas_call | solution.py:107
  152.7 14.1 %project.9 = (bf16[128,256,512]{2,1,0:T(8,128)(2,1)}, bf16[256,128,512]{2,1,0:T(8,128)(2,1)}, bf16[256,128,512]{2,1,0:T(8,128)(2,1)}, bf16[128,64,512]{2,1,0:T(8,128)(2,1)}) custom-call(s32[1]{0:T(128)} %bitcast.g_ref, bf16[32,512,128]{2,1,0:T(8,128)(2,1)} %collective-permute-done.3.z_ref, ...), custom_call_target="tpu_custom_call", output_to_operand_aliasing={{0}: (6, {}), {1}: (7, {}), {2}: (8, {}), {3}: (9, {})} | custom-call | flops 8589934592 | bytes 19660800 | tf_op jit(solution)/shard_map/project/pallas_call | solution.py:107
  170.0 24.6 %block.8 = (bf16[128,256,512]{2,1,0:T(8,128)(2,1)}, bf16[128,256,128]{2,1,0:T(8,128)(2,1)}) custom-call(s32[1]{0:T(128)} %bitcast.1.h_ref, bf16[128,256,512]{2,1,0:T(8,128)(2,1)} %get-tuple-element.101.a_ref.refs_0_, bf16[128,64,512]{2,1,0:T(8,128)(2,1)} %get-tuple-element.89.refs_0_, ...), custom_call_target="tpu_custom_call", output_to_operand_aliasing={{0}: (14, {}), {1}: (15, {})} | custom-call | flops 4294967296 | bytes 13107200 | tf_op jit(solution)/shard_map/block/pallas_call | solution.py:314
  194.7 31.9 %block.9 = (bf16[128,256,512]{2,1,0:T(8,128)(2,1)}, bf16[256,128,512]{2,1,0:T(8,128)(2,1)}, bf16[256,128,512]{2,1,0:T(8,128)(2,1)}) custom-call(s32[1]{0:T(128)} %bitcast.1.h_ref, bf16[128,256,512]{2,1,0:T(8,128)(2,1)} %get-tuple-element.101.a_ref.refs_0_, ...), custom_call_target="tpu_custom_call", output_to_operand_aliasing={{0}: (14, {}), {1}: (15, {}), {2}: (16, {})} | custom-call | flops 8589934592 | bytes 26214400 | tf_op jit(solution)/shard_map/block/pallas_call | solution.py:314
  226.6 33.4 %collective-permute-done.2.z_ref = bf16[32,512,128]{2,1,0:T(8,128)(2,1)S(1)} collective-permute-done((bf16[32,512,128]{2,1,0:T(8,128)(2,1)}, bf16[32,512,128]{2,1,0:T(8,128)(2,1)S(1)}, u32[]{:S(2)}, u32[]{:S(2)}) %collective-permute-start.2) | collective-permute-done | bytes 4194336 | tf_op jit(solution)/shard_map/ppermute | solution.py:426
  262.0 14.1 %project.10 = (bf16[128,256,512]{2,1,0:T(8,128)(2,1)}, bf16[256,128,512]{2,1,0:T(8,128)(2,1)}, bf16[256,128,512]{2,1,0:T(8,128)(2,1)}, bf16[128,64,512]{2,1,0:T(8,128)(2,1)}) custom-call(s32[1]{0:T(128)} %bitcast.g_ref, bf16[32,512,128]{2,1,0:T(8,128)(2,1)} %copy-done.1, ...), custom_call_target="tpu_custom_call", output_to_operand_aliasing={{0}: (6, {}), {1}: (7, {}), {2}: (8, {})} | custom-call | flops 8589934592 | bytes 19660800 | tf_op jit(solution)/shard_map/project/pallas_call | solution.py:107
  276.1 14.2 %project.11 = (bf16[128,256,512]{2,1,0:T(8,128)(2,1)}, bf16[256,128,512]{2,1,0:T(8,128)(2,1)}, bf16[256,128,512]{2,1,0:T(8,128)(2,1)}, bf16[128,64,512]{2,1,0:T(8,128)(2,1)}) custom-call(s32[1]{0:T(128)} %bitcast.g_ref, bf16[32,512,128]{2,1,0:T(8,128)(2,1)} %collective-permute-done.1.z_ref, ...), custom_call_target="tpu_custom_call", output_to_operand_aliasing={{0}: (6, {}), {1}: (7, {}), {2}: (8, {}), {3}: (9, {})} | custom-call | flops 8589934592 | bytes 19660800 | tf_op jit(solution)/shard_map/project/pallas_call | solution.py:107
  293.5 37.8 %block.10 = (bf16[128,256,512]{2,1,0:T(8,128)(2,1)}, bf16[128,256,128]{2,1,0:T(8,128)(2,1)}) custom-call(s32[1]{0:T(128)} %bitcast.1.h_ref, bf16[128,256,512]{2,1,0:T(8,128)(2,1)} %get-tuple-element.120.a_ref.refs_0_, bf16[128,64,512]{2,1,0:T(8,128)(2,1)} %get-tuple-element.89.refs_0_, ...), custom_call_target="tpu_custom_call", output_to_operand_aliasing={{0}: (16, {}), {1}: (17, {})} | custom-call | flops 8589934592 | bytes 26214400 | tf_op jit(solution)/shard_map/block/pallas_call | solution.py:314
  331.3 41.4 %block.11 = (bf16[128,256,512]{2,1,0:T(8,128)(2,1)}, bf16[256,128,512]{2,1,0:T(8,128)(2,1)}, bf16[256,128,512]{2,1,0:T(8,128)(2,1)}) custom-call(s32[1]{0:T(128)} %bitcast.1.h_ref, bf16[128,256,512]{2,1,0:T(8,128)(2,1)} %get-tuple-element.120.a_ref.refs_0_, ...), custom_call_target="tpu_custom_call", output_to_operand_aliasing={{0}: (14, {}), {1}: (15, {}), {2}: (16, {})} | custom-call | flops 12884901888 | bytes 39321600 | tf_op jit(solution)/shard_map/block/pallas_call | solution.py:314
  372.7 10.7 %collective-permute-done.8.z_ref = bf16[32,512,128]{2,1,0:T(8,128)(2,1)S(1)} collective-permute-done((bf16[32,512,128]{2,1,0:T(8,128)(2,1)}, bf16[32,512,128]{2,1,0:T(8,128)(2,1)S(1)}, u32[]{:S(2)}, u32[]{:S(2)}) %collective-permute-start.8) | collective-permute-done | bytes 4194336 | tf_op jit(solution)/shard_map/ppermute | solution.py:426
  385.5 14.1 %project.12 = (bf16[128,256,512]{2,1,0:T(8,128)(2,1)}, bf16[256,128,512]{2,1,0:T(8,128)(2,1)}, bf16[256,128,512]{2,1,0:T(8,128)(2,1)}, bf16[128,64,512]{2,1,0:T(8,128)(2,1)}) custom-call(s32[1]{0:T(128)} %bitcast.g_ref, bf16[32,512,128]{2,1,0:T(8,128)(2,1)} %copy-done, ...), custom_call_target="tpu_custom_call", output_to_operand_aliasing={{0}: (6, {}), {1}: (7, {}), {2}: (8, {})} | custom-call | flops 8589934592 | bytes 19660800 | tf_op jit(solution)/shard_map/project/pallas_call | solution.py:107
  399.6 14.1 %project.13 = (bf16[128,256,512]{2,1,0:T(8,128)(2,1)}, bf16[256,128,512]{2,1,0:T(8,128)(2,1)}, bf16[256,128,512]{2,1,0:T(8,128)(2,1)}, bf16[128,64,512]{2,1,0:T(8,128)(2,1)}) custom-call(s32[1]{0:T(128)} %bitcast.g_ref, bf16[32,512,128]{2,1,0:T(8,128)(2,1)} %collective-permute-done.4.z_ref, ...), custom_call_target="tpu_custom_call", output_to_operand_aliasing={{0}: (6, {}), {1}: (7, {}), {2}: (8, {}), {3}: (9, {})} | custom-call | flops 8589934592 | bytes 19660800 | tf_op jit(solution)/shard_map/project/pallas_call | solution.py:107
  413.7 51.4 %block.12 = (bf16[128,256,512]{2,1,0:T(8,128)(2,1)}, bf16[128,256,128]{2,1,0:T(8,128)(2,1)}) custom-call(s32[1]{0:T(128)} %bitcast.1.h_ref, bf16[128,256,512]{2,1,0:T(8,128)(2,1)} %get-tuple-element.139.a_ref, bf16[128,64,512]{2,1,0:T(8,128)(2,1)} %get-tuple-element.89.refs_0_, ...), custom_call_target="tpu_custom_call", output_to_operand_aliasing={{0}: (18, {}), {1}: (19, {})} | custom-call | flops 12884901888 | bytes 39321600 | tf_op jit(solution)/shard_map/block/pallas_call | solution.py:314
  465.1 51.0 %block.13 = (bf16[128,256,512]{2,1,0:T(8,128)(2,1)}, bf16[256,128,512]{2,1,0:T(8,128)(2,1)}, bf16[256,128,512]{2,1,0:T(8,128)(2,1)}) custom-call(s32[1]{0:T(128)} %bitcast.1.h_ref, bf16[128,256,512]{2,1,0:T(8,128)(2,1)} %get-tuple-element.139.a_ref, ...), custom_call_target="tpu_custom_call", output_to_operand_aliasing={{0}: (14, {}), {1}: (15, {}), {2}: (16, {})} | custom-call | flops 17179869184 | bytes 52428800 | tf_op jit(solution)/shard_map/block/pallas_call | solution.py:314
  516.1 17.0 %incoming.2 = (f32[128,64,256]{2,1,0:T(8,128)}, f32[128,64,256]{2,1,0:T(8,128)}) custom-call(s32[1]{0:T(128)} %bitcast.1.h_ref, bf16[128,256,128]{2,1,0:T(8,128)(2,1)} %get-tuple-element.153.a_ref, bf16[128,256,512]{2,1,0:T(8,128)(2,1)} %get-tuple-element.151.b_ref), custom_call_target="tpu_custom_call" | custom-call | flops 2147483648 | bytes 41943040 | tf_op jit(solution)/shard_map/incoming/pallas_call | solution.py:136
  533.5 17.0 %incoming.3 = (f32[128,64,256]{2,1,0:T(8,128)}, f32[128,64,256]{2,1,0:T(8,128)}) custom-call(s32[1]{0:T(128)} %bitcast.1.h_ref, bf16[128,256,128]{2,1,0:T(8,128)(2,1)} %get-tuple-element.153.a_ref, bf16[128,256,512]{2,1,0:T(8,128)(2,1)} %get-tuple-element.151.b_ref), custom_call_target="tpu_custom_call" | custom-call | flops 2147483648 | bytes 41943040 | tf_op jit(solution)/shard_map/incoming/pallas_call | solution.py:136
  552.1 14.7 %finish.2.refs_0_ = bf16[64,512,128]{2,1,0:T(8,128)(2,1)} custom-call(s32[1]{0:T(128)} %bitcast.g_ref, f32[128,64,256]{2,1,0:T(8,128)} %get-tuple-element.154.o_ref, f32[128,64,256]{2,1,0:T(8,128)} %collective-permute-done.14.r_ref, bf16[256,128,512]{2,1,0:T(8,128)(2,1)} %get-tuple-element.158.zt_ref, bf16[256,128,512]{2,1,0:T(8,128)(2,1)} %get-tuple-element.159.znt_ref, ...), custom_call_target="tpu_custom_call" | custom-call | flops 2147483648 | bytes 29491200 | tf_op jit(solution)/shard_map/finish/pallas_call | solution.py:382
  566.8 14.7 %finish.3 = bf16[64,512,128]{2,1,0:T(8,128)(2,1)} custom-call(s32[1]{0:T(128)} %bitcast.g_ref, f32[128,64,256]{2,1,0:T(8,128)} %get-tuple-element.156.o_ref, f32[128,64,256]{2,1,0:T(8,128)} %collective-permute-done.13.r_ref, bf16[256,128,512]{2,1,0:T(8,128)(2,1)} %get-tuple-element.158.zt_ref, ...), custom_call_target="tpu_custom_call", output_to_operand_aliasing={{}: (9, {})} | custom-call | flops 2147483648 | bytes 29491200 | tf_op jit(solution)/shard_map/finish/pallas_call | solution.py:382
  (93 shorter events, 32.3 us)
Async XLA Ops:
  1.1 15.8 %collective-permute-start.6 = (f32[64,512]{0,1:T(8,128)S(1)}, f32[64,512]{0,1:T(8,128)S(1)}, u32[]{:S(2)}, u32[]{:S(2)}) collective-permute-start(f32[64,512]{0,1:T(8,128)S(1)} %convert_element_type.83), channel_id=1, source_target_pairs={{0,4},{1,5},{2,6},{3,7},{4,0},{5,1},{6,2},{7,3}} | collective-permute-start | bytes 393224 | tf_op jit(solution)/shard_map/ppermute | solution.py:426
  4.4 12.6 %collective-permute-start.5 = (f32[64,512]{0,1:T(8,128)S(1)}, f32[64,512]{0,1:T(8,128)S(1)}, u32[]{:S(2)}, u32[]{:S(2)}) collective-permute-start(f32[64,512]{0,1:T(8,128)S(1)} %convert_element_type.83), channel_id=1, source_target_pairs={{0,2},{1,3},{2,0},{3,1},{4,6},{5,7},{6,4},{7,5}} | collective-permute-start | bytes 393224 | tf_op jit(solution)/shard_map/ppermute | solution.py:426
  5.9 11.6 %collective-permute-start.7 = (f32[64,512]{0,1:T(8,128)S(1)}, f32[64,512]{0,1:T(8,128)S(1)}, u32[]{:S(2)}, u32[]{:S(2)}) collective-permute-start(f32[64,512]{0,1:T(8,128)S(1)} %convert_element_type.83), channel_id=1, source_target_pairs={{0,6},{1,7},{2,4},{3,5},{4,2},{5,3},{6,0},{7,1}} | collective-permute-start | bytes 393224 | tf_op jit(solution)/shard_map/ppermute | solution.py:426
  18.1 30.4 %copy-start.2 = (bf16[2,128,128]{2,1,0:T(8,128)(2,1)S(1)}, bf16[2,128,128]{2,1,0:T(8,128)(2,1)}, u32[]{:S(2)}) copy-start(bf16[2,128,128]{2,1,0:T(8,128)(2,1)} %param.18) | copy-start | bytes 196612
  18.1 30.5 %copy-start.3 = (bf16[2,128,128]{2,1,0:T(8,128)(2,1)S(1)}, bf16[2,128,128]{2,1,0:T(8,128)(2,1)}, u32[]{:S(2)}) copy-start(bf16[2,128,128]{2,1,0:T(8,128)(2,1)} %param.15) | copy-start | bytes 196612
  18.1 30.9 %copy-start.7 = (bf16[2,128]{1,0:T(2,128)(2,1)S(1)}, bf16[2,128]{1,0:T(2,128)(2,1)}, u32[]{:S(2)}) copy-start(bf16[2,128]{1,0:T(2,128)(2,1)} %param.19) | copy-start | bytes 1540
  18.2 31.0 %copy-start.8 = (bf16[2,128]{1,0:T(2,128)(2,1)S(1)}, bf16[2,128]{1,0:T(2,128)(2,1)}, u32[]{:S(2)}) copy-start(bf16[2,128]{1,0:T(2,128)(2,1)} %param.16) | copy-start | bytes 1540
  18.2 32.1 %copy-start.4 = (bf16[2,2,128]{2,1,0:T(2,128)(2,1)S(1)}, bf16[2,2,128]{2,1,0:T(2,128)(2,1)}, u32[]{:S(2)}) copy-start(bf16[2,2,128]{2,1,0:T(2,128)(2,1)} %param.17) | copy-start | bytes 3076
  45.2 13.5 %collective-permute-start.9 = (bf16[128,64,512]{2,1,0:T(8,128)(2,1)}, bf16[128,64,512]{2,1,0:T(8,128)(2,1)}, u32[]{:S(2)}, u32[]{:S(2)}) collective-permute-start(bf16[128,64,512]{2,1,0:T(8,128)(2,1)} %get-tuple-element.89.refs_0_), channel_id=1, source_target_pairs={{0,1},{1,0},{2,3},{3,2},{4,5},{5,4},{6,7},{7,6}} | collective-permute-start | bytes 25165832 | tf_op jit(solution)/shard_map/ppermute | solution.py:426
  45.2 93.3 %collective-permute-start = (bf16[32,512,128]{2,1,0:T(8,128)(2,1)}, bf16[32,512,128]{2,1,0:T(8,128)(2,1)}, u32[]{:S(2)}, u32[]{:S(2)}) collective-permute-start(bf16[32,512,128]{2,1,0:T(8,128)(2,1)} %get-tuple-element.83), channel_id=1, source_target_pairs={{0,2},{1,3},{2,0},{3,1},{4,6},{5,7},{6,4},{7,5}} | collective-permute-start | bytes 12582920 | tf_op jit(solution)/shard_map/ppermute | solution.py:426
  46.9 105.7 %collective-permute-start.3 = (bf16[32,512,128]{2,1,0:T(8,128)(2,1)}, bf16[32,512,128]{2,1,0:T(8,128)(2,1)}, u32[]{:S(2)}, u32[]{:S(2)}) collective-permute-start(bf16[32,512,128]{2,1,0:T(8,128)(2,1)} %get-tuple-element.83), channel_id=1, source_target_pairs={{0,4},{1,5},{2,6},{3,7},{4,0},{5,1},{6,2},{7,3}} | collective-permute-start | bytes 12582920 | tf_op jit(solution)/shard_map/ppermute | solution.py:426
  166.8 27.9 %collective-permute-start.10 = (bf16[128,64,512]{2,1,0:T(8,128)(2,1)}, bf16[128,64,512]{2,1,0:T(8,128)(2,1)}, u32[]{:S(2)}, u32[]{:S(2)}) collective-permute-start(bf16[128,64,512]{2,1,0:T(8,128)(2,1)} %get-tuple-element.102.refs_0_.refs_1_), channel_id=1, source_target_pairs={{0,1},{1,0},{2,3},{3,2},{4,5},{5,4},{6,7},{7,6}} | collective-permute-start | bytes 25165832 | tf_op jit(solution)/shard_map/ppermute | solution.py:426
  166.8 93.2 %collective-permute-start.2 = (bf16[32,512,128]{2,1,0:T(8,128)(2,1)}, bf16[32,512,128]{2,1,0:T(8,128)(2,1)S(1)}, u32[]{:S(2)}, u32[]{:S(2)}) collective-permute-start(bf16[32,512,128]{2,1,0:T(8,128)(2,1)} %get-tuple-element.84), channel_id=1, source_target_pairs={{0,2},{1,3},{2,0},{3,1},{4,6},{5,7},{6,4},{7,5}} | collective-permute-start | bytes 12582920 | tf_op jit(solution)/shard_map/ppermute | solution.py:426
  168.5 107.5 %collective-permute-start.1 = (bf16[32,512,128]{2,1,0:T(8,128)(2,1)}, bf16[32,512,128]{2,1,0:T(8,128)(2,1)}, u32[]{:S(2)}, u32[]{:S(2)}) collective-permute-start(bf16[32,512,128]{2,1,0:T(8,128)(2,1)} %get-tuple-element.84), channel_id=1, source_target_pairs={{0,4},{1,5},{2,6},{3,7},{4,0},{5,1},{6,2},{7,3}} | collective-permute-start | bytes 12582920 | tf_op jit(solution)/shard_map/ppermute | solution.py:426
  260.0 2.0 copy-start.1
  290.2 41.0 %collective-permute-start.11 = (bf16[128,64,512]{2,1,0:T(8,128)(2,1)}, bf16[128,64,512]{2,1,0:T(8,128)(2,1)}, u32[]{:S(2)}, u32[]{:S(2)}) collective-permute-start(bf16[128,64,512]{2,1,0:T(8,128)(2,1)} %get-tuple-element.121.refs_0_.refs_2_), channel_id=1, source_target_pairs={{0,1},{1,0},{2,3},{3,2},{4,5},{5,4},{6,7},{7,6}} | collective-permute-start | bytes 25165832 | tf_op jit(solution)/shard_map/ppermute | solution.py:426
  290.2 93.2 %collective-permute-start.8 = (bf16[32,512,128]{2,1,0:T(8,128)(2,1)}, bf16[32,512,128]{2,1,0:T(8,128)(2,1)S(1)}, u32[]{:S(2)}, u32[]{:S(2)}) collective-permute-start(bf16[32,512,128]{2,1,0:T(8,128)(2,1)} %collective-permute-done.z_ref), channel_id=1, source_target_pairs={{0,4},{1,5},{2,6},{3,7},{4,0},{5,1},{6,2},{7,3}} | collective-permute-start | bytes 12582920 | tf_op jit(solution)/shard_map/ppermute | solution.py:426
  292.0 107.6 %collective-permute-start.4 = (bf16[32,512,128]{2,1,0:T(8,128)(2,1)}, bf16[32,512,128]{2,1,0:T(8,128)(2,1)}, u32[]{:S(2)}, u32[]{:S(2)}) collective-permute-start(bf16[32,512,128]{2,1,0:T(8,128)(2,1)} %collective-permute-done.1.z_ref), channel_id=1, source_target_pairs={{0,2},{1,3},{2,0},{3,1},{4,6},{5,7},{6,4},{7,5}} | collective-permute-start | bytes 12582920 | tf_op jit(solution)/shard_map/ppermute | solution.py:426
  383.4 2.1 copy-start
  413.7 51.4 %collective-permute-start.12 = (bf16[128,64,512]{2,1,0:T(8,128)(2,1)}, bf16[128,64,512]{2,1,0:T(8,128)(2,1)}, u32[]{:S(2)}, u32[]{:S(2)}) collective-permute-start(bf16[128,64,512]{2,1,0:T(8,128)(2,1)} %get-tuple-element.140.refs_0_), channel_id=1, source_target_pairs={{0,1},{1,0},{2,3},{3,2},{4,5},{5,4},{6,7},{7,6}} | collective-permute-start | bytes 25165832 | tf_op jit(solution)/shard_map/ppermute | solution.py:426
  516.0 34.6 %copy-start.6 = (f32[128]{0:T(128)S(1)}, f32[128]{0:T(128)}, u32[]{:S(2)}) copy-start(f32[128]{0:T(128)} %get-tuple-element.184) | copy-start | bytes 1540
  516.1 35.3 %copy-start.5 = (f32[128]{0:T(128)S(1)}, f32[128]{0:T(128)}, u32[]{:S(2)}) copy-start(f32[128]{0:T(128)} %get-tuple-element.181) | copy-start | bytes 1540
  533.1 17.5 %collective-permute-start.14 = (f32[128,64,256]{2,1,0:T(8,128)}, f32[128,64,256]{2,1,0:T(8,128)}, u32[]{:S(2)}, u32[]{:S(2)}) collective-permute-start(f32[128,64,256]{2,1,0:T(8,128)} %get-tuple-element.160), channel_id=1, source_target_pairs={{0,1},{1,0},{2,3},{3,2},{4,5},{5,4},{6,7},{7,6}} | collective-permute-start | bytes 25165832 | tf_op jit(solution)/shard_map/ppermute | solution.py:426
  550.5 16.3 %collective-permute-start.13 = (f32[128,64,256]{2,1,0:T(8,128)}, f32[128,64,256]{2,1,0:T(8,128)}, u32[]{:S(2)}, u32[]{:S(2)}) collective-permute-start(f32[128,64,256]{2,1,0:T(8,128)} %get-tuple-element.157), channel_id=1, source_target_pairs={{0,1},{1,0},{2,3},{3,2},{4,5},{5,4},{6,7},{7,6}} | collective-permute-start | bytes 25165832 | tf_op jit(solution)/shard_map/ppermute | solution.py:426

commit v3 on v2

--- a/solution.py
+++ b/solution.py
@@ -59,9 +59,11 @@
 
     def row(i, carry):
         zt = jnp.concatenate([z_ref[i, pl.ds(start, 32), :] for start in starts], axis=0).T
-        zt_ref[i] = zt
+        for t in range(2):
+            zt_ref[t, i] = zt[:, 128 * t:128 * t + 128]
         zn = norm_columns(zt.astype(f32), scale, offset).astype(bf16)
-        znt_ref[i] = zn
+        for t in range(2):
+            znt_ref[t, i] = zn[:, 128 * t:128 * t + 128]
         m = m_ref[pl.ds(i, 1), :]
         proj = jnp.dot(w_ref[...], extend(zn * m.astype(bf16), m), preferred_element_type=f32)
 
@@ -71,7 +73,7 @@
         store_gated(proj, store)
         return carry
 
-    lax.fori_loop(0, ROWS, row, 0, unroll=8)
+    lax.fori_loop(0, ROWS, row, 0, unroll=16)
     for side, out in ((0, a_ref), (1, b_ref)):
         def channel(q, carry):
             for u in range(16):
@@ -111,9 +113,10 @@
                   pl.BlockSpec((ROWS, cols, CH), lambda i, k: (i, 0, 0)),
                   pl.BlockSpec((ROWS, 256), lambda i, k: (i + first, k)),
                   whole(4 * CH, EXT), whole(CH, CH), whole(CH, CH)] + [ANY] * len(filled),
-        out_specs=[side(first)] + [pl.BlockSpec((ROWS, CH, 256), lambda i, k: (i + first, 0, k))] * 2 + [side(slot_first)],
+        out_specs=[side(first)] + [pl.BlockSpec((2, ROWS, CH, 128), lambda i, k: (k, i + first, 0, 0))] * 2 + [side(slot_first)],
         out_shape=[jax.ShapeDtypeStruct((CH, all_rows, cols), bf16)]
-        + [jax.ShapeDtypeStruct((all_rows, CH, cols), bf16)] * 2 + [jax.ShapeDtypeStruct((CH, slot_rows, cols), bf16)],
+        + [jax.ShapeDtypeStruct((cols // 128, all_rows, CH, 128), bf16)] * 2
+        + [jax.ShapeDtypeStruct((CH, slot_rows, cols), bf16)],
         input_output_aliases={6 + k: k for k in range(len(filled))},
         scratch_shapes=[pltpu.VMEM((2, 2 * CH * PITCH, 128), f32)],
         compiler_params=params(2),
@@ -124,26 +127,28 @@
 
 def incoming_body(h_ref, a_ref, b_ref, keep_ref, send_ref, scr):
     at_mine, at_theirs = pl.multiple_of(64 * h_ref[0], 64), pl.multiple_of(64 - 64 * h_ref[0], 64)
-    for c in range(keep_ref.shape[0]):
-        scr[c] = lax.dot_general(a_ref[c], b_ref[c], (((0,), (0,)), ((), ())), preferred_element_type=f32)
-        keep_ref[c] = scr[c, pl.ds(at_mine, 64), :]
-        send_ref[c] = scr[c, pl.ds(at_theirs, 64), :]
-
-
-def incoming(h, a, b, part, width):
+    for c in range(keep_ref.shape[1]):
+        b = jnp.concatenate([b_ref[t, c] for t in range(b_ref.shape[0])], axis=1)
+        scr[c] = lax.dot_general(a_ref[c], b, (((0,), (0,)), ((), ())), preferred_element_type=f32)
+        for t in range(b_ref.shape[0]):
+            keep_ref[t, c] = scr[c, pl.ds(at_mine, 64), 128 * t:128 * t + 128]
+            send_ref[t, c] = scr[c, pl.ds(at_theirs, 64), 128 * t:128 * t + 128]
+
+
+def incoming(h, a, b, part, n):
     block = 16
-    out = jax.ShapeDtypeStruct((CH, 64, width), f32)
+    out = jax.ShapeDtypeStruct((n, CH, 64, 128), f32)
     return pl.pallas_call(
         incoming_body,
         grid=(CH // block,),
         in_specs=[pl.BlockSpec(memory_space=pltpu.SMEM),
                   pl.BlockSpec((block,) + a.shape[1:], lambda c: (c, 0, 0)),
-                  pl.BlockSpec((block, b.shape[1], width), lambda c: (c, 0, part))],
-        out_specs=[pl.BlockSpec((block, 64, width), lambda c: (c, 0, 0))] * 2,
+                  pl.BlockSpec((n, block, b.shape[2], 128), lambda c: (part, c, 0, 0))],
+        out_specs=[pl.BlockSpec((n, block, 64, 128), lambda c: (0, c, 0, 0))] * 2,
         out_shape=[out, out],
-        scratch_shapes=[pltpu.VMEM((block, 128, width), f32)],
+        scratch_shapes=[pltpu.VMEM((block, 128, 128 * n), f32)],
         compiler_params=params(),
-        cost_estimate=cost(2**23 * width, 160 * 2**10 * width),
+        cost_estimate=cost(2**30 * n, 20 * 2**20 * n),
         name="incoming",
     )(h, a, b)
 
@@ -194,10 +199,7 @@
     return jnp.concatenate([ref[2 * p], ref[2 * p + 1]], axis=1)
 
 
-def update_pair(p, scr, zt_ref, znt_ref, wo_ref, wg_ref, scale, offset, ones):
-    start = pl.multiple_of(2 * p * ROW_PITCH, 8)
-    normed = jnp.concatenate([scr[pl.ds(start, CH), :], scr[pl.ds(start + ROW_PITCH, CH), :]], axis=1)
-    u = (normed * scale + offset).astype(bf16)
+def update_pair(p, u, zt_ref, znt_ref, wo_ref, wg_ref, ones):
     update = jnp.dot(wo_ref[...], extend(u, ones), preferred_element_type=f32)
     gate = jnp.dot(wg_ref[...], extend(pair_of(znt_ref, p), ones), preferred_element_type=f32)
     return (pair_of(zt_ref, p).astype(f32) + (jnp.tanh(gate) + 1.0) * update).astype(bf16)
@@ -220,26 +222,32 @@
                 both[c, pl.ds(128 * s + at_theirs, 64), :] = theirs[s][c]
             o = lax.dot_general(a_ref[c], both[c], (((1,), (1,)), ((), ())), preferred_element_type=f32)
             for s in range(n):
-                sums[s, step * per_step + c] = o[:, 128 * s:128 * s + 128]
+                for r in range(0, o.shape[0], 8):
+                    to = pl.ds(r * ROW_PITCH + step * per_step + c, 8, stride=ROW_PITCH)
+                    sums[s, to, :] = o[r:r + 8, 128 * s:128 * s + 128]
             return carry
 
-        lax.fori_loop(0, per_step, channel, 0, unroll=4)
+        lax.fori_loop(0, per_step, channel, 0, unroll=8)
 
     @pl.when(step >= sum_steps)
     def _():
         at = step - sum_steps
         tile, row = at % n, pl.multiple_of(at // n * ROWS, ROWS)
-        finish_project_body(with_left, with_pair, tile, lambda c, g: sums[tile, c, pl.ds(row + 8 * g, 8), :], *refs[:-2])
+
+        def load(i):
+            return sums[tile, pl.ds(pl.multiple_of((row + i) * ROW_PITCH, 8), CH), :]
+
+        finish_project_body(with_left, with_pair, tile, load, *refs[:-2])
 
 
 def finish_project_body(with_left, with_pair, tile, load, zt_ref, znt_ref, m_ref, wo_ref, wg_ref, so_ref, oo_ref,
                         w_ref, si_ref, oi_ref, *refs):
-    refs = list(refs)[-(4 + with_left + 2 * with_pair):]
-    b_ref = refs.pop(0)
-    z1_ref, zn1_ref = (refs.pop(0), refs.pop(0)) if with_pair else (None, None)
+    refs = list(refs)[-(3 + with_left + 2 * with_pair):]
+    b_ref = refs.pop(0).at[0]
+    z1_ref, zn1_ref = (refs.pop(0).at[0], refs.pop(0).at[0]) if with_pair else (None, None)
+    zt_ref, znt_ref = zt_ref.at[0], znt_ref.at[0]
     a_ref = refs.pop(0) if with_left else None
-    scr, scr2, exts = refs
-    normalize_rows(load, scr)
+    scr2, exts = refs
     scale_out, offset_out = twice(so_ref), twice(oo_ref)
     scale_in, offset_in = twice(si_ref), twice(oi_ref)
     ones = jnp.ones((1, 256), f32)
@@ -251,7 +259,9 @@
         return store
 
     def pair(p, carry):
-        z1 = update_pair(p, scr, zt_ref, znt_ref, wo_ref, wg_ref, scale_out, offset_out, ones)
+        o = jnp.concatenate([load(2 * p), load(2 * p + 1)], axis=1)
+        u = norm_columns(o, scale_out, offset_out).astype(bf16)
+        z1 = update_pair(p, u, zt_ref, znt_ref, wo_ref, wg_ref, ones)
         zn1 = norm_columns(z1.astype(f32), scale_in, offset_in).astype(bf16)
         if with_pair:
             for t in range(2):
@@ -288,7 +298,8 @@
 
 def block(core, a, mine, theirs, zt, znt, m, row, rows, first, ln_out, layer1, layer2, with_pair, filled):
     n, per_step = len(mine), 16
-    all_rows, _, cols = zt.shape
+    slots, all_rows = zt.shape[:2]
+    cols = a.shape[2]
     with_left = first == 0
     sum_steps, row_block = CH // per_step, row // ROWS
 
@@ -302,12 +313,12 @@
     def sides(rows, block):
         return pl.BlockSpec((per_step, rows, cols), lambda t: (jnp.minimum(t, sum_steps - 1), block, 0))
 
-    positions = pl.BlockSpec((ROWS, CH, 128), at(lambda i, j: (i, 0, j)))
-    out_specs = [pl.BlockSpec((CH, ROWS, 128), at(lambda i, j: (0, i, j)))]
-    out_shape = [jax.ShapeDtypeStruct((CH, all_rows, cols), bf16)]
+    positions = pl.BlockSpec((1, ROWS, CH, 128), at(lambda i, j: (j, i, 0, 0)))
+    out_specs = [pl.BlockSpec((1, CH, ROWS, 128), at(lambda i, j: (j, 0, i, 0)))]
+    out_shape = [jax.ShapeDtypeStruct((slots, CH, all_rows, 128), bf16)]
     if with_pair:
         out_specs += [positions] * 2
-        out_shape += [jax.ShapeDtypeStruct((all_rows, CH, cols), bf16)] * 2
+        out_shape += [jax.ShapeDtypeStruct(zt.shape, bf16)] * 2
     if with_left:
         out_specs.append(pl.BlockSpec((CH, ROWS, 128), at(lambda i, j: (0, i, 0))))
         out_shape.append(jax.ShapeDtypeStruct((CH, all_rows, 128), bf16))
@@ -320,9 +331,8 @@
            whole(4 * CH, EXT), whole(CH, CH), whole(CH, CH)] + [ANY] * len(filled),
         out_specs=out_specs,
         out_shape=out_shape,
-        scratch_shapes=[pltpu.VMEM((ROWS * ROW_PITCH, 128), f32), pltpu.VMEM((CH * PITCH, 128), f32),
-                        pltpu.VMEM((ROWS // 2, EXT, 256), bf16),
-                        pltpu.VMEM((n, CH, rows, 128), f32), pltpu.VMEM((per_step, 128 * n, cols), bf16)],
+        scratch_shapes=[pltpu.VMEM((CH * PITCH, 128), f32), pltpu.VMEM((ROWS // 2, EXT, 256), bf16),
+                        pltpu.VMEM((n, rows * ROW_PITCH, 128), f32), pltpu.VMEM((per_step, 128 * n, cols), bf16)],
         input_output_aliases={12 + 2 * n + k: k for k in range(len(filled))},
         compiler_params=params(),
         cost_estimate=cost(rows * n * 128 * 2**19, rows * n * 128 * 1600),
@@ -333,6 +343,7 @@
 
 def finish_body(slot0, g_ref, o_ref, r_ref, zt_ref, znt_ref, wo_ref, wg_ref, so_ref, oo_ref, *refs):
     out_ref, scr, total, rows_out, sems = refs[-5:]
+    zt_ref, znt_ref = zt_ref.at[0], znt_ref.at[0]
     step, last = pl.program_id(0) * pl.num_programs(1) + pl.program_id(1), pl.num_programs(0) * pl.num_programs(1) - 1
     buffer = step % 2
 
@@ -345,7 +356,7 @@
 
     def add(q, carry):
         for u in range(8):
-            total[q * 8 + u] = o_ref[q * 8 + u] + r_ref[q * 8 + u]
+            total[q * 8 + u] = o_ref[0, q * 8 + u] + r_ref[0, q * 8 + u]
         return carry
 
     lax.fori_loop(0, CH // 8, add, 0)
@@ -354,7 +365,10 @@
     ones = jnp.ones((1, 256), f32)
 
     def pair(p, carry):
-        z2 = update_pair(p, scr, zt_ref, znt_ref, wo_ref, wg_ref, scale, offset, ones).T
+        start = pl.multiple_of(2 * p * ROW_PITCH, 8)
+        normed = jnp.concatenate([scr[pl.ds(start, CH), :], scr[pl.ds(start + ROW_PITCH, CH), :]], axis=1)
+        u = (normed * scale + offset).astype(bf16)
+        z2 = update_pair(p, u, zt_ref, znt_ref, wo_ref, wg_ref, ones).T
         for t in range(2):
             rows_out[buffer, 2 * p + t] = z2[128 * t:128 * t + 128]
         return carry
@@ -375,17 +389,17 @@
 
 
 def finish(chip, o, received, zt, znt, layer2, part, filled):
-    _, rows, cols = o.shape
-    n = cols // 128
-    sums = pl.BlockSpec((CH, ROWS, 128), lambda i, j: (0, i, j))
-    positions = pl.BlockSpec((ROWS, CH, 128), lambda i, j: (i, 0, j + n * part))
+    n, _, rows, _ = o.shape
+    cols = 128 * n
+    sums = pl.BlockSpec((1, CH, ROWS, 128), lambda i, j: (j, 0, i, 0))
+    positions = pl.BlockSpec((1, ROWS, CH, 128), lambda i, j: (j + n * part, i, 0, 0))
     return pl.pallas_call(
         functools.partial(finish_body, n * part),
         grid=(rows // ROWS, n),
         in_specs=[pl.BlockSpec(memory_space=pltpu.SMEM), sums, sums, positions, positions,
                   whole(CH, EXT), whole(CH, EXT), whole(CH, CH), whole(CH, CH)] + [ANY] * len(filled),
         out_specs=ANY,
-        out_shape=jax.ShapeDtypeStruct((rows, zt.shape[2], CH), bf16),
+        out_shape=jax.ShapeDtypeStruct((rows, 128 * zt.shape[0], CH), bf16),
         input_output_aliases={9 + k: k for k in range(len(filled))},
         scratch_shapes=[pltpu.VMEM((ROWS * ROW_PITCH, 128), f32), pltpu.VMEM((CH, ROWS, 128), f32),
                         pltpu.VMEM((2, ROWS, 128, CH), bf16), pltpu.SemaphoreType.DMA((2, 4))],
@@ -433,12 +447,13 @@
         rows = pair.shape[0]
         half = rows // 2
 
-        mask = pair_mask.astype(f32)
+        mask = pair_mask.astype(bf16)
         x_mask, y_mask = swap(mask, 2), swap(mask, 4)
         far_mask = swap(mask, 6)
-        masks = in_slot_order(jnp.concatenate([mask, x_mask[:half], y_mask[:half], x_mask[half:], y_mask[half:], far_mask]),
-                              chip[0])
-        top, bottom = lax.optimization_barrier((pair[:half], pair[half:]))
+        masks = in_slot_order(jnp.concatenate([mask, x_mask[:half], y_mask[:half], x_mask[half:], y_mask[half:], far_mask])
+                              .astype(f32), chip[0])
+        top = pair[:half]
+        bottom, _ = lax.optimization_barrier((pair[half:], top))
         x_top, y_top = swap(top, 2), swap(top, 4)
         x_bottom, y_bottom = swap(bottom, 2), swap(bottom, 4)
         x_top_on, y_bottom_on, _, _ = lax.optimization_barrier((x_top, y_bottom, x_bottom, y_top))
@@ -479,7 +494,7 @@
 
         parts, out = [], ()
         for part in range(2):
-            keep, send = ran(incoming(next_step(core), a2, b2, part, 256))
+            keep, send = ran(incoming(next_step(core), a2, b2, part, 2))
             parts.append((keep, swap(send, 1)))
         for part, (keep, received) in enumerate(parts):
             out = (finish(chip, keep, received, *z1, layer2, part, out),)

time: 583 us -> 570 us (0.978)
  Pallas kernels: 437 us -> 409 us
  waiting for transfers between devices: 103 us -> 117 us
    pallas_call x7, Pallas kernels: 263 us -> 241 us  [block(): pl.pallas_call(functools.partial(block_body, n, with_left, with_pair), gr...]
    ppermute x15, waiting for transfers between devices: 103 us -> 117 us  [swap(): return lax.ppermute(x, 'dap', [(i, i ^ bits) for i in range(n)])]
    pallas_call x7, Pallas kernels: 110 us -> 104 us  [project(): pl.pallas_call(project_body, grid=(rows // ROWS, cols // 256), in_specs=[...]
  transfers between devices with their start and end apart: 15 -> 15, of which waited for: 5 -> 4; matrix products, arithmetic and copies ran while one was open for 3% -> 3% of each run, Pallas kernels for 49% -> 47%
where the time goes in v3:
time: 570 us; the launch traced here: 567 us
  Pallas kernels  409 us (72%)
  waiting for transfers between devices  117 us (21%)
  local copies, waits for them, and re-layouts  22.7 us (4%)
  starting transfers between devices  15.4 us (3%)
    pallas_call x7, Pallas kernels, block(): pl.pallas_call(functools.partial(block_body, n, with_left, with_pair), gr...  241 us
    ppermute x15, waiting for transfers between devices, swap(): return lax.ppermute(x, 'dap', [(i, i ^ bits) for i in range(n)])  117 us
    pallas_call x7, Pallas kernels, project(): pl.pallas_call(project_body, grid=(rows // ROWS, cols // 256), in_specs=[...  104 us
    pallas_call x2, Pallas kernels, incoming(): pl.pallas_call(incoming_body, grid=(CH // block,), in_specs=[pl.BlockSpec...  34.6 us
    pallas_call x2, Pallas kernels, finish(): pl.pallas_call(functools.partial(finish_body, n * part), grid=(rows // RO...  29.1 us
    ppermute x15, starting transfers between devices, swap(): return lax.ppermute(x, 'dap', [(i, i ^ bits) for i in range(n)])  15.4 us
  transfers between devices with their start and end apart: 15, of which 4 were waited for; matrix products, arithmetic and copies ran while one was open for 3% of the time, Pallas kernels for 47%

profile of v3, /device:TPU:0, one launch (start us, length us, event | category | flops | bytes accessed | tf_op | source)
XLA Modules:
  0.0 567.4 jit_solution(17537016740277568634)
XLA Ops:
  1.1 3.3 collective-permute-start.5
  5.9 6.0 %fusion.3 = (bf16[32,512,128]{2,1,0:T(8,128)(2,1)}, bf16[32,512,128]{2,1,0:T(8,128)(2,1)}) fusion(bf16[64,512,128]{2,1,0:T(8,128)(2,1)} %z_ref.1), kind=kLoop, calls=%fused_computation.31 | loop fusion | bytes 16777216 | tf_op jit(solution)/shard_map/slice | solution.py:456
  19.7 23.8 %project.7 = (bf16[128,256,512]{2,1,0:T(8,128)(2,1)}, bf16[4,256,128,128]{3,2,1,0:T(8,128)(2,1)}, bf16[4,256,128,128]{3,2,1,0:T(8,128)(2,1)}, bf16[128,64,512]{2,1,0:T(8,128)(2,1)}) custom-call(s32[1]{0:T(128)} %bitcast.g_ref, bf16[64,512,128]{2,1,0:T(8,128)(2,1)} %z_ref.1, f32[256,512]{1,0:T(8,128)} %pad_maximum_fusion.m_ref.refs_4_.refs_6_.refs_8_, ...), custom_call_target="tpu_custom_call" | custom-call | flops 17179869184 | bytes 39321600 | tf_op jit(solution)/shard_map/project/pallas_call | solution.py:109
  51.5 5.4 collective-permute-done.9.refs_1_.refs_2_.refs_3_
  58.3 22.7 %block.7 = (bf16[4,128,256,128]{3,2,1,0:T(8,128)(2,1)}, bf16[4,256,128,128]{3,2,1,0:T(8,128)(2,1)}, bf16[4,256,128,128]{3,2,1,0:T(8,128)(2,1)}, bf16[128,256,128]{2,1,0:T(8,128)(2,1)}) custom-call(s32[1]{0:T(128)} %bitcast.1.h_ref, bf16[128,256,512]{2,1,0:T(8,128)(2,1)} %get-tuple-element.86.a_ref.refs_0_, bf16[128,64,512]{2,1,0:T(8,128)(2,1)} %get-tuple-element.87.refs_0_, ...), custom_call_target="tpu_custom_call" | custom-call | flops 4294967296 | bytes 13107200 | tf_op jit(solution)/shard_map/block/pallas_call | solution.py:325
  81.0 55.9 %collective-permute-done.z_ref = bf16[32,512,128]{2,1,0:T(8,128)(2,1)} collective-permute-done((bf16[32,512,128]{2,1,0:T(8,128)(2,1)}, bf16[32,512,128]{2,1,0:T(8,128)(2,1)}, u32[]{:S(2)}, u32[]{:S(2)}) %collective-permute-start) | collective-permute-done | bytes 4194336 | tf_op jit(solution)/shard_map/ppermute | solution.py:440
  136.9 13.3 %project.8 = (bf16[128,256,512]{2,1,0:T(8,128)(2,1)}, bf16[4,256,128,128]{3,2,1,0:T(8,128)(2,1)}, bf16[4,256,128,128]{3,2,1,0:T(8,128)(2,1)}, bf16[128,64,512]{2,1,0:T(8,128)(2,1)}) custom-call(s32[1]{0:T(128)} %bitcast.g_ref, bf16[32,512,128]{2,1,0:T(8,128)(2,1)} %collective-permute-done.z_ref, ...), custom_call_target="tpu_custom_call", output_to_operand_aliasing={{0}: (6, {}), {1}: (7, {}), {2}: (8, {})} | custom-call | flops 8589934592 | bytes 19660800 | tf_op jit(solution)/shard_map/project/pallas_call | solution.py:109
  150.2 13.3 %project.9 = (bf16[128,256,512]{2,1,0:T(8,128)(2,1)}, bf16[4,256,128,128]{3,2,1,0:T(8,128)(2,1)}, bf16[4,256,128,128]{3,2,1,0:T(8,128)(2,1)}, bf16[128,64,512]{2,1,0:T(8,128)(2,1)}) custom-call(s32[1]{0:T(128)} %bitcast.g_ref, ...), custom_call_target="tpu_custom_call", output_to_operand_aliasing={{0}: (6, {}), {1}: (7, {}), {2}: (8, {}), {3}: (9, {})} | custom-call | flops 8589934592 | bytes 19660800 | tf_op jit(solution)/shard_map/project/pallas_call | solution.py:109
  166.8 22.6 %block.8 = (bf16[4,128,256,128]{3,2,1,0:T(8,128)(2,1)}, bf16[128,256,128]{2,1,0:T(8,128)(2,1)}) custom-call(s32[1]{0:T(128)} %bitcast.1.h_ref, bf16[128,256,512]{2,1,0:T(8,128)(2,1)} %get-tuple-element.99.a_ref.refs_0_, bf16[128,64,512]{2,1,0:T(8,128)(2,1)} %get-tuple-element.87.refs_0_, ...), custom_call_target="tpu_custom_call", output_to_operand_aliasing={{0}: (14, {}), {1}: (15, {})} | custom-call | flops 4294967296 | bytes 13107200 | tf_op jit(solution)/shard_map/block/pallas_call | solution.py:325
  189.4 28.9 %block.9 = (bf16[4,128,256,128]{3,2,1,0:T(8,128)(2,1)}, bf16[4,256,128,128]{3,2,1,0:T(8,128)(2,1)}, bf16[4,256,128,128]{3,2,1,0:T(8,128)(2,1)}) custom-call(s32[1]{0:T(128)} %bitcast.1.h_ref, bf16[128,256,512]{2,1,0:T(8,128)(2,1)} %get-tuple-element.99.a_ref.refs_0_, ...), custom_call_target="tpu_custom_call", output_to_operand_aliasing={{0}: (14, {}), {1}: (15, {}), {2}: (16, {})} | custom-call | flops 8589934592 | bytes 26214400 | tf_op jit(solution)/shard_map/block/pallas_call | solution.py:325
  218.3 38.4 %collective-permute-done.2.z_ref = bf16[32,512,128]{2,1,0:T(8,128)(2,1)S(1)} collective-permute-done((bf16[32,512,128]{2,1,0:T(8,128)(2,1)}, bf16[32,512,128]{2,1,0:T(8,128)(2,1)S(1)}, u32[]{:S(2)}, u32[]{:S(2)}) %collective-permute-start.2) | collective-permute-done | bytes 4194336 | tf_op jit(solution)/shard_map/ppermute | solution.py:440
  258.7 13.2 %project.10 = (bf16[128,256,512]{2,1,0:T(8,128)(2,1)}, bf16[4,256,128,128]{3,2,1,0:T(8,128)(2,1)}, bf16[4,256,128,128]{3,2,1,0:T(8,128)(2,1)}, bf16[128,64,512]{2,1,0:T(8,128)(2,1)}) custom-call(s32[1]{0:T(128)} %bitcast.g_ref, bf16[32,512,128]{2,1,0:T(8,128)(2,1)} %copy-done.1, ...), custom_call_target="tpu_custom_call", output_to_operand_aliasing={{0}: (6, {}), {1}: (7, {}), {2}: (8, {})} | custom-call | flops 8589934592 | bytes 19660800 | tf_op jit(solution)/shard_map/project/pallas_call | solution.py:109
  272.0 13.3 %project.11 = (bf16[128,256,512]{2,1,0:T(8,128)(2,1)}, bf16[4,256,128,128]{3,2,1,0:T(8,128)(2,1)}, bf16[4,256,128,128]{3,2,1,0:T(8,128)(2,1)}, bf16[128,64,512]{2,1,0:T(8,128)(2,1)}) custom-call(s32[1]{0:T(128)} %bitcast.g_ref, ...), custom_call_target="tpu_custom_call", output_to_operand_aliasing={{0}: (6, {}), {1}: (7, {}), {2}: (8, {}), {3}: (9, {})} | custom-call | flops 8589934592 | bytes 19660800 | tf_op jit(solution)/shard_map/project/pallas_call | solution.py:109
  288.6 34.6 %block.10 = (bf16[4,128,256,128]{3,2,1,0:T(8,128)(2,1)}, bf16[128,256,128]{2,1,0:T(8,128)(2,1)}) custom-call(s32[1]{0:T(128)} %bitcast.1.h_ref, bf16[128,256,512]{2,1,0:T(8,128)(2,1)} %get-tuple-element.118.a_ref.refs_0_, bf16[128,64,512]{2,1,0:T(8,128)(2,1)} %get-tuple-element.87.refs_0_, ...), custom_call_target="tpu_custom_call", output_to_operand_aliasing={{0}: (16, {}), {1}: (17, {})} | custom-call | flops 8589934592 | bytes 26214400 | tf_op jit(solution)/shard_map/block/pallas_call | solution.py:325
  323.2 38.2 %block.11 = (bf16[4,128,256,128]{3,2,1,0:T(8,128)(2,1)}, bf16[4,256,128,128]{3,2,1,0:T(8,128)(2,1)}, bf16[4,256,128,128]{3,2,1,0:T(8,128)(2,1)}) custom-call(s32[1]{0:T(128)} %bitcast.1.h_ref, bf16[128,256,512]{2,1,0:T(8,128)(2,1)} %get-tuple-element.118.a_ref.refs_0_, ...), custom_call_target="tpu_custom_call", output_to_operand_aliasing={{0}: (14, {}), {1}: (15, {}), {2}: (16, {})} | custom-call | flops 12884901888 | bytes 39321600 | tf_op jit(solution)/shard_map/block/pallas_call | solution.py:325
  361.4 17.1 %collective-permute-done.8.z_ref = bf16[32,512,128]{2,1,0:T(8,128)(2,1)S(1)} collective-permute-done((bf16[32,512,128]{2,1,0:T(8,128)(2,1)}, bf16[32,512,128]{2,1,0:T(8,128)(2,1)S(1)}, u32[]{:S(2)}, u32[]{:S(2)}) %collective-permute-start.8) | collective-permute-done | bytes 4194336 | tf_op jit(solution)/shard_map/ppermute | solution.py:440
  380.6 13.3 %project.12 = (bf16[128,256,512]{2,1,0:T(8,128)(2,1)}, bf16[4,256,128,128]{3,2,1,0:T(8,128)(2,1)}, bf16[4,256,128,128]{3,2,1,0:T(8,128)(2,1)}, bf16[128,64,512]{2,1,0:T(8,128)(2,1)}) custom-call(s32[1]{0:T(128)} %bitcast.g_ref, bf16[32,512,128]{2,1,0:T(8,128)(2,1)} %copy-done, ...), custom_call_target="tpu_custom_call", output_to_operand_aliasing={{0}: (6, {}), {1}: (7, {}), {2}: (8, {})} | custom-call | flops 8589934592 | bytes 19660800 | tf_op jit(solution)/shard_map/project/pallas_call | solution.py:109
  393.9 13.3 %project.13 = (bf16[128,256,512]{2,1,0:T(8,128)(2,1)}, bf16[4,256,128,128]{3,2,1,0:T(8,128)(2,1)}, bf16[4,256,128,128]{3,2,1,0:T(8,128)(2,1)}, bf16[128,64,512]{2,1,0:T(8,128)(2,1)}) custom-call(s32[1]{0:T(128)} %bitcast.g_ref, ...), custom_call_target="tpu_custom_call", output_to_operand_aliasing={{0}: (6, {}), {1}: (7, {}), {2}: (8, {}), {3}: (9, {})} | custom-call | flops 8589934592 | bytes 19660800 | tf_op jit(solution)/shard_map/project/pallas_call | solution.py:109
  407.2 47.2 %block.12 = (bf16[4,128,256,128]{3,2,1,0:T(8,128)(2,1)}, bf16[128,256,128]{2,1,0:T(8,128)(2,1)}) custom-call(s32[1]{0:T(128)} %bitcast.1.h_ref, bf16[128,256,512]{2,1,0:T(8,128)(2,1)} %get-tuple-element.137.a_ref, bf16[128,64,512]{2,1,0:T(8,128)(2,1)} %get-tuple-element.87.refs_0_, ...), custom_call_target="tpu_custom_call", output_to_operand_aliasing={{0}: (18, {}), {1}: (19, {})} | custom-call | flops 12884901888 | bytes 39321600 | tf_op jit(solution)/shard_map/block/pallas_call | solution.py:325
  454.5 47.1 %block.13 = (bf16[4,128,256,128]{3,2,1,0:T(8,128)(2,1)}, bf16[4,256,128,128]{3,2,1,0:T(8,128)(2,1)}, bf16[4,256,128,128]{3,2,1,0:T(8,128)(2,1)}) custom-call(s32[1]{0:T(128)} %bitcast.1.h_ref, bf16[128,256,512]{2,1,0:T(8,128)(2,1)} %get-tuple-element.137.a_ref, ...), custom_call_target="tpu_custom_call", output_to_operand_aliasing={{0}: (14, {}), {1}: (15, {}), {2}: (16, {})} | custom-call | flops 17179869184 | bytes 52428800 | tf_op jit(solution)/shard_map/block/pallas_call | solution.py:325
  501.6 17.3 %incoming.2 = (f32[2,128,64,128]{3,2,1,0:T(8,128)}, f32[2,128,64,128]{3,2,1,0:T(8,128)}) custom-call(s32[1]{0:T(128)} %bitcast.1.h_ref, bf16[128,256,128]{2,1,0:T(8,128)(2,1)} %get-tuple-element.151.a_ref, bf16[4,128,256,128]{3,2,1,0:T(8,128)(2,1)} %get-tuple-element.149.b_ref), custom_call_target="tpu_custom_call" | custom-call | flops 2147483648 | bytes 41943040 | tf_op jit(solution)/shard_map/incoming/pallas_call | solution.py:141
  519.3 17.3 %incoming.3 = (f32[2,128,64,128]{3,2,1,0:T(8,128)}, f32[2,128,64,128]{3,2,1,0:T(8,128)}) custom-call(s32[1]{0:T(128)} %bitcast.1.h_ref, bf16[128,256,128]{2,1,0:T(8,128)(2,1)} %get-tuple-element.151.a_ref, bf16[4,128,256,128]{3,2,1,0:T(8,128)(2,1)} %get-tuple-element.149.b_ref), custom_call_target="tpu_custom_call" | custom-call | flops 2147483648 | bytes 41943040 | tf_op jit(solution)/shard_map/incoming/pallas_call | solution.py:141
  538.1 14.5 %finish.2.refs_0_ = bf16[64,512,128]{2,1,0:T(8,128)(2,1)} custom-call(s32[1]{0:T(128)} %bitcast.g_ref, f32[2,128,64,128]{3,2,1,0:T(8,128)} %get-tuple-element.152.o_ref, f32[2,128,64,128]{3,2,1,0:T(8,128)} %collective-permute-done.14.r_ref, bf16[4,256,128,128]{3,2,1,0:T(8,128)(2,1)} %get-tuple-element.156.zt_ref, ...), custom_call_target="tpu_custom_call" | custom-call | flops 2147483648 | bytes 29491200 | tf_op jit(solution)/shard_map/finish/pallas_call | solution.py:396
  552.7 14.6 %finish.3 = bf16[64,512,128]{2,1,0:T(8,128)(2,1)} custom-call(s32[1]{0:T(128)} %bitcast.g_ref, f32[2,128,64,128]{3,2,1,0:T(8,128)} %get-tuple-element.154.o_ref, f32[2,128,64,128]{3,2,1,0:T(8,128)} %collective-permute-done.13.r_ref, bf16[4,256,128,128]{3,2,1,0:T(8,128)(2,1)} %get-tuple-element.156.zt_ref, ...), custom_call_target="tpu_custom_call", output_to_operand_aliasing={{}: (9, {})} | custom-call | flops 2147483648 | bytes 29491200 | tf_op jit(solution)/shard_map/finish/pallas_call | solution.py:396
  (94 shorter events, 32.1 us)
Async XLA Ops:
  1.1 15.8 %collective-permute-start.5 = (bf16[64,512]{0,1:T(8,128)(2,1)S(1)}, bf16[64,512]{0,1:T(8,128)(2,1)S(1)}, u32[]{:S(2)}, u32[]{:S(2)}) collective-permute-start(bf16[64,512]{0,1:T(8,128)(2,1)S(1)} %convert_element_type.87), channel_id=1, source_target_pairs={{0,2},{1,3},{2,0},{3,1},{4,6},{5,7},{6,4},{7,5}} | collective-permute-start | bytes 196616 | tf_op jit(solution)/shard_map/ppermute | solution.py:440
  4.4 12.6 %collective-permute-start.6 = (bf16[64,512]{0,1:T(8,128)(2,1)S(1)}, bf16[64,512]{0,1:T(8,128)(2,1)S(1)}, u32[]{:S(2)}, u32[]{:S(2)}) collective-permute-start(bf16[64,512]{0,1:T(8,128)(2,1)S(1)} %convert_element_type.87), channel_id=1, source_target_pairs={{0,4},{1,5},{2,6},{3,7},{4,0},{5,1},{6,2},{7,3}} | collective-permute-start | bytes 196616 | tf_op jit(solution)/shard_map/ppermute | solution.py:440
  5.9 11.2 %collective-permute-start.7 = (bf16[64,512]{0,1:T(8,128)(2,1)S(1)}, bf16[64,512]{0,1:T(8,128)(2,1)S(1)}, u32[]{:S(2)}, u32[]{:S(2)}) collective-permute-start(bf16[64,512]{0,1:T(8,128)(2,1)S(1)} %convert_element_type.87), channel_id=1, source_target_pairs={{0,6},{1,7},{2,4},{3,5},{4,2},{5,3},{6,0},{7,1}} | collective-permute-start | bytes 196616 | tf_op jit(solution)/shard_map/ppermute | solution.py:440
  17.6 29.3 %copy-start.2 = (bf16[2,128,128]{2,1,0:T(8,128)(2,1)S(1)}, bf16[2,128,128]{2,1,0:T(8,128)(2,1)}, u32[]{:S(2)}) copy-start(bf16[2,128,128]{2,1,0:T(8,128)(2,1)} %param.18) | copy-start | bytes 196612
  17.6 29.5 %copy-start.3 = (bf16[2,128,128]{2,1,0:T(8,128)(2,1)S(1)}, bf16[2,128,128]{2,1,0:T(8,128)(2,1)}, u32[]{:S(2)}) copy-start(bf16[2,128,128]{2,1,0:T(8,128)(2,1)} %param.15) | copy-start | bytes 196612
  17.6 29.8 %copy-start.7 = (bf16[2,128]{1,0:T(2,128)(2,1)S(1)}, bf16[2,128]{1,0:T(2,128)(2,1)}, u32[]{:S(2)}) copy-start(bf16[2,128]{1,0:T(2,128)(2,1)} %param.19) | copy-start | bytes 1540
  17.6 30.0 %copy-start.8 = (bf16[2,128]{1,0:T(2,128)(2,1)S(1)}, bf16[2,128]{1,0:T(2,128)(2,1)}, u32[]{:S(2)}) copy-start(bf16[2,128]{1,0:T(2,128)(2,1)} %param.16) | copy-start | bytes 1540
  17.7 31.1 %copy-start.4 = (bf16[2,2,128]{2,1,0:T(2,128)(2,1)S(1)}, bf16[2,2,128]{2,1,0:T(2,128)(2,1)}, u32[]{:S(2)}) copy-start(bf16[2,2,128]{2,1,0:T(2,128)(2,1)} %param.17) | copy-start | bytes 3076
  43.4 13.5 %collective-permute-start.9 = (bf16[128,64,512]{2,1,0:T(8,128)(2,1)}, bf16[128,64,512]{2,1,0:T(8,128)(2,1)}, u32[]{:S(2)}, u32[]{:S(2)}) collective-permute-start(bf16[128,64,512]{2,1,0:T(8,128)(2,1)} %get-tuple-element.87.refs_0_), channel_id=1, source_target_pairs={{0,1},{1,0},{2,3},{3,2},{4,5},{5,4},{6,7},{7,6}} | collective-permute-start | bytes 25165832 | tf_op jit(solution)/shard_map/ppermute | solution.py:440
  43.4 93.5 %collective-permute-start = (bf16[32,512,128]{2,1,0:T(8,128)(2,1)}, bf16[32,512,128]{2,1,0:T(8,128)(2,1)}, u32[]{:S(2)}, u32[]{:S(2)}) collective-permute-start(bf16[32,512,128]{2,1,0:T(8,128)(2,1)} %get-tuple-element.162), channel_id=1, source_target_pairs={{0,2},{1,3},{2,0},{3,1},{4,6},{5,7},{6,4},{7,5}} | collective-permute-start | bytes 12582920 | tf_op jit(solution)/shard_map/ppermute | solution.py:440
  45.4 104.8 %collective-permute-start.3 = (bf16[32,512,128]{2,1,0:T(8,128)(2,1)}, bf16[32,512,128]{2,1,0:T(8,128)(2,1)}, u32[]{:S(2)}, u32[]{:S(2)}) collective-permute-start(bf16[32,512,128]{2,1,0:T(8,128)(2,1)} %get-tuple-element.162), channel_id=1, source_target_pairs={{0,4},{1,5},{2,6},{3,7},{4,0},{5,1},{6,2},{7,3}} | collective-permute-start | bytes 12582920 | tf_op jit(solution)/shard_map/ppermute | solution.py:440
  163.5 25.9 %collective-permute-start.10 = (bf16[128,64,512]{2,1,0:T(8,128)(2,1)}, bf16[128,64,512]{2,1,0:T(8,128)(2,1)}, u32[]{:S(2)}, u32[]{:S(2)}) collective-permute-start(bf16[128,64,512]{2,1,0:T(8,128)(2,1)} %get-tuple-element.100.refs_0_.refs_1_), channel_id=1, source_target_pairs={{0,1},{1,0},{2,3},{3,2},{4,5},{5,4},{6,7},{7,6}} | collective-permute-start | bytes 25165832 | tf_op jit(solution)/shard_map/ppermute | solution.py:440
  163.6 93.2 %collective-permute-start.2 = (bf16[32,512,128]{2,1,0:T(8,128)(2,1)}, bf16[32,512,128]{2,1,0:T(8,128)(2,1)S(1)}, u32[]{:S(2)}, u32[]{:S(2)}) collective-permute-start(bf16[32,512,128]{2,1,0:T(8,128)(2,1)} %get-tuple-element.82), channel_id=1, source_target_pairs={{0,2},{1,3},{2,0},{3,1},{4,6},{5,7},{6,4},{7,5}} | collective-permute-start | bytes 12582920 | tf_op jit(solution)/shard_map/ppermute | solution.py:440
  165.3 106.7 %collective-permute-start.1 = (bf16[32,512,128]{2,1,0:T(8,128)(2,1)}, bf16[32,512,128]{2,1,0:T(8,128)(2,1)}, u32[]{:S(2)}, u32[]{:S(2)}) collective-permute-start(bf16[32,512,128]{2,1,0:T(8,128)(2,1)} %get-tuple-element.82), channel_id=1, source_target_pairs={{0,4},{1,5},{2,6},{3,7},{4,0},{5,1},{6,2},{7,3}} | collective-permute-start | bytes 12582920 | tf_op jit(solution)/shard_map/ppermute | solution.py:440
  256.7 2.0 copy-start.1
  285.3 37.9 %collective-permute-start.11 = (bf16[128,64,512]{2,1,0:T(8,128)(2,1)}, bf16[128,64,512]{2,1,0:T(8,128)(2,1)}, u32[]{:S(2)}, u32[]{:S(2)}) collective-permute-start(bf16[128,64,512]{2,1,0:T(8,128)(2,1)} %get-tuple-element.119.refs_0_.refs_2_), channel_id=1, source_target_pairs={{0,1},{1,0},{2,3},{3,2},{4,5},{5,4},{6,7},{7,6}} | collective-permute-start | bytes 25165832 | tf_op jit(solution)/shard_map/ppermute | solution.py:440
  285.3 93.2 %collective-permute-start.8 = (bf16[32,512,128]{2,1,0:T(8,128)(2,1)}, bf16[32,512,128]{2,1,0:T(8,128)(2,1)S(1)}, u32[]{:S(2)}, u32[]{:S(2)}) collective-permute-start(bf16[32,512,128]{2,1,0:T(8,128)(2,1)} %collective-permute-done.z_ref), channel_id=1, source_target_pairs={{0,4},{1,5},{2,6},{3,7},{4,0},{5,1},{6,2},{7,3}} | collective-permute-start | bytes 12582920 | tf_op jit(solution)/shard_map/ppermute | solution.py:440
  287.1 106.8 %collective-permute-start.4 = (bf16[32,512,128]{2,1,0:T(8,128)(2,1)}, bf16[32,512,128]{2,1,0:T(8,128)(2,1)}, u32[]{:S(2)}, u32[]{:S(2)}) collective-permute-start(bf16[32,512,128]{2,1,0:T(8,128)(2,1)} %collective-permute-done.1.z_ref), channel_id=1, source_target_pairs={{0,2},{1,3},{2,0},{3,1},{4,6},{5,7},{6,4},{7,5}} | collective-permute-start | bytes 12582920 | tf_op jit(solution)/shard_map/ppermute | solution.py:440
  378.5 2.1 copy-start
  407.2 47.3 %collective-permute-start.12 = (bf16[128,64,512]{2,1,0:T(8,128)(2,1)}, bf16[128,64,512]{2,1,0:T(8,128)(2,1)}, u32[]{:S(2)}, u32[]{:S(2)}) collective-permute-start(bf16[128,64,512]{2,1,0:T(8,128)(2,1)} %get-tuple-element.138.refs_0_), channel_id=1, source_target_pairs={{0,1},{1,0},{2,3},{3,2},{4,5},{5,4},{6,7},{7,6}} | collective-permute-start | bytes 25165832 | tf_op jit(solution)/shard_map/ppermute | solution.py:440
  501.6 35.1 %copy-start.6 = (f32[128]{0:T(128)S(1)}, f32[128]{0:T(128)}, u32[]{:S(2)}) copy-start(f32[128]{0:T(128)} %get-tuple-element.182) | copy-start | bytes 1540
  501.6 35.8 %copy-start.5 = (f32[128]{0:T(128)S(1)}, f32[128]{0:T(128)}, u32[]{:S(2)}) copy-start(f32[128]{0:T(128)} %get-tuple-element.179) | copy-start | bytes 1540
  518.9 17.8 %collective-permute-start.14 = (f32[2,128,64,128]{3,2,1,0:T(8,128)}, f32[2,128,64,128]{3,2,1,0:T(8,128)}, u32[]{:S(2)}, u32[]{:S(2)}) collective-permute-start(f32[2,128,64,128]{3,2,1,0:T(8,128)} %get-tuple-element.158), channel_id=1, source_target_pairs={{0,1},{1,0},{2,3},{3,2},{4,5},{5,4},{6,7},{7,6}} | collective-permute-start | bytes 25165832 | tf_op jit(solution)/shard_map/ppermute | solution.py:440
  536.6 16.0 %collective-permute-start.13 = (f32[2,128,64,128]{3,2,1,0:T(8,128)}, f32[2,128,64,128]{3,2,1,0:T(8,128)}, u32[]{:S(2)}, u32[]{:S(2)}) collective-permute-start(f32[2,128,64,128]{3,2,1,0:T(8,128)} %get-tuple-element.155), channel_id=1, source_target_pairs={{0,1},{1,0},{2,3},{3,2},{4,5},{5,4},{6,7},{7,6}} | collective-permute-start | bytes 25165832 | tf_op jit(solution)/shard_map/ppermute | solution.py:440

commit v4 on v3

--- a/solution.py
+++ b/solution.py
@@ -101,9 +101,8 @@
 ANY = pl.BlockSpec(memory_space=pl.ANY)
 
 
-def project(chip, z, m, w, scale, offset, row, slot_rows, filled):
+def project(chip, z, m, w, scale, offset, row, slot_rows, all_rows, filled):
     rows, cols, _ = z.shape
-    all_rows = m.shape[0]
     first, slot_first = row // ROWS, row % slot_rows // ROWS
     side = lambda at: pl.BlockSpec((CH, ROWS, 256), lambda i, k: (0, i + at, k))
     return pl.pallas_call(
@@ -153,7 +152,7 @@
     )(h, a, b)
 
 
-def normalize_rows(load, scr):
+def normalize_rows(first_load, load, scr):
     groups = range(ROWS // 8)
     for gs in ([list(groups)] if 1 else [[g] for g in groups]):
         zeros = tuple(jnp.zeros((8, 128), f32) for _ in range(4 * len(gs)))
@@ -162,7 +161,7 @@
             sums = list(sums)
             for u in range(64):
                 for n, g in enumerate(gs):
-                    sums[4 * n + u % 4] += load(q * 64 + u, g)
+                    sums[4 * n + u % 4] += first_load(q * 64 + u, g)
             return tuple(sums)
 
         def total(s, n):
@@ -242,12 +241,12 @@
 
 def finish_project_body(with_left, with_pair, tile, load, zt_ref, znt_ref, m_ref, wo_ref, wg_ref, so_ref, oo_ref,
                         w_ref, si_ref, oi_ref, *refs):
-    refs = list(refs)[-(3 + with_left + 2 * with_pair):]
+    refs = list(refs)[-(4 + with_left + 2 * with_pair):]
     b_ref = refs.pop(0).at[0]
     z1_ref, zn1_ref = (refs.pop(0).at[0], refs.pop(0).at[0]) if with_pair else (None, None)
     zt_ref, znt_ref = zt_ref.at[0], znt_ref.at[0]
     a_ref = refs.pop(0) if with_left else None
-    scr2, exts = refs
+    scr2, exts, z1s = refs
     scale_out, offset_out = twice(so_ref), twice(oo_ref)
     scale_in, offset_in = twice(si_ref), twice(oi_ref)
     ones = jnp.ones((1, 256), f32)
@@ -261,7 +260,11 @@
     def pair(p, carry):
         o = jnp.concatenate([load(2 * p), load(2 * p + 1)], axis=1)
         u = norm_columns(o, scale_out, offset_out).astype(bf16)
-        z1 = update_pair(p, u, zt_ref, znt_ref, wo_ref, wg_ref, ones)
+        z1s[p] = update_pair(p, u, zt_ref, znt_ref, wo_ref, wg_ref, ones)
+        return carry
+
+    def project_pair(p, carry):
+        z1 = z1s[p]
         zn1 = norm_columns(z1.astype(f32), scale_in, offset_in).astype(bf16)
         if with_pair:
             for t in range(2):
@@ -276,14 +279,15 @@
 
     def emit(out):
         def channel(q, carry):
-            for u in range(32):
-                c = q * 32 + u
+            for u in range(16):
+                c = q * 16 + u
                 out[c] = scr2[pl.ds(pl.multiple_of(c * PITCH, 8), ROWS), :].astype(bf16)
             return carry
 
-        lax.fori_loop(0, CH // 32, channel, 0)
+        lax.fori_loop(0, CH // 16, channel, 0)
 
     lax.fori_loop(0, ROWS // 2, pair, 0, unroll=8)
+    lax.fori_loop(0, ROWS // 2, project_pair, 0, unroll=8)
     emit(b_ref)
     if with_left:
         @pl.when(tile == 0)
@@ -317,8 +321,8 @@
     out_specs = [pl.BlockSpec((1, CH, ROWS, 128), at(lambda i, j: (j, 0, i, 0)))]
     out_shape = [jax.ShapeDtypeStruct((slots, CH, all_rows, 128), bf16)]
     if with_pair:
-        out_specs += [positions] * 2
-        out_shape += [jax.ShapeDtypeStruct(zt.shape, bf16)] * 2
+        out_specs += [pl.BlockSpec((1, ROWS, CH, 128), at(lambda i, j: (j, jnp.minimum(i, 64 // ROWS), 0, 0)))] * 2
+        out_shape += [jax.ShapeDtypeStruct((slots, 64 + ROWS, CH, 128), bf16)] * 2
     if with_left:
         out_specs.append(pl.BlockSpec((CH, ROWS, 128), at(lambda i, j: (0, i, 0))))
         out_shape.append(jax.ShapeDtypeStruct((CH, all_rows, 128), bf16))
@@ -332,6 +336,7 @@
         out_specs=out_specs,
         out_shape=out_shape,
         scratch_shapes=[pltpu.VMEM((CH * PITCH, 128), f32), pltpu.VMEM((ROWS // 2, EXT, 256), bf16),
+                        pltpu.VMEM((ROWS // 2, CH, 256), bf16),
                         pltpu.VMEM((n, rows * ROW_PITCH, 128), f32), pltpu.VMEM((per_step, 128 * n, cols), bf16)],
         input_output_aliases={12 + 2 * n + k: k for k in range(len(filled))},
         compiler_params=params(),
@@ -354,13 +359,12 @@
                                       out_ref.at[pl.ds(row, ROWS), pl.ds(piece_start(g_ref[0], slot, p), 32), :],
                                       sems.at[buffer, p]) for p in range(4)]
 
-    def add(q, carry):
-        for u in range(8):
-            total[q * 8 + u] = o_ref[0, q * 8 + u] + r_ref[0, q * 8 + u]
-        return carry
-
-    lax.fori_loop(0, CH // 8, add, 0)
-    normalize_rows(lambda c, g: total[c, 8 * g:8 * g + 8, :], scr)
+    def add(c, g):
+        both = o_ref[0, c, 8 * g:8 * g + 8, :] + r_ref[0, c, 8 * g:8 * g + 8, :]
+        total[c, 8 * g:8 * g + 8, :] = both
+        return both
+
+    normalize_rows(add, lambda c, g: total[c, 8 * g:8 * g + 8, :], scr)
     scale, offset = twice(so_ref), twice(oo_ref)
     ones = jnp.ones((1, 256), f32)
 
@@ -450,10 +454,11 @@
         mask = pair_mask.astype(bf16)
         x_mask, y_mask = swap(mask, 2), swap(mask, 4)
         far_mask = swap(mask, 6)
+        own_masks = in_slot_order(mask.astype(f32), chip[0])
         masks = in_slot_order(jnp.concatenate([mask, x_mask[:half], y_mask[:half], x_mask[half:], y_mask[half:], far_mask])
                               .astype(f32), chip[0])
         top = pair[:half]
-        bottom, _ = lax.optimization_barrier((pair[half:], top))
+        bottom = lax.optimization_barrier((pair, top))[0][half:]
         x_top, y_top = swap(top, 2), swap(top, 4)
         x_bottom, y_bottom = swap(bottom, 2), swap(bottom, 4)
         x_top_on, y_bottom_on, _, _ = lax.optimization_barrier((x_top, y_bottom, x_bottom, y_top))
@@ -478,15 +483,15 @@
             for at, piece in enumerate(pieces[s]):
                 scale, offset = layer1["ln_in"]
                 filled = (left, zt, znt) + made if s or at else ()
-                left, zt, znt, b = ran(project(chip, piece, masks, layer1["w_proj"], next_step(scale), offset,
-                                               rows * s + half * at, rows, filled))
+                left, zt, znt, b = ran(project(chip, piece, masks if s else own_masks, layer1["w_proj"], next_step(scale), offset,
+                                               rows * s + half * at, rows, 4 * rows, filled))
                 made = (b,)
             mine.append(b)
             theirs.append(swap(b, 1))
             if s:
                 b2, a2 = ran(block(core, left, mine[:s], theirs[:s], zt, znt, masks, rows * s, rows, 0,
                                    next_step(layer1["ln_out"]), layer1, layer2, False, (b2, a2)))
-            out = ran(block(core, left, mine[s:], theirs[s:], zt, znt, masks, 0, rows * (s + 1), s,
+            out = ran(block(core, left, mine[s:], theirs[s:], zt, znt, masks if s else own_masks, 0, rows * (s + 1), s,
                             next_step(layer1["ln_out"]), layer1, layer2, True, (b2, *z1) if s else ()))
             b2, z1 = out[0], out[1:3]
             if not s:

time: 570 us -> 596 us (1.046)
  waiting for transfers between devices: 117 us -> 149 us
    ppermute x15, waiting for transfers between devices: 117 us -> 149 us  [swap(): return lax.ppermute(x, 'dap', [(i, i ^ bits) for i in range(n)])]
  transfers between devices with their start and end apart: 15 -> 15, of which waited for: 4 -> 4; matrix products, arithmetic and copies ran while one was open for 3% -> 2% of each run, Pallas kernels for 47% -> 44%
where the time goes in v4:
time: 596 us; the launch traced here: 595 us
  Pallas kernels  404 us (68%)
  waiting for transfers between devices  149 us (25%)
  local copies, waits for them, and re-layouts  22.4 us (4%)
  starting transfers between devices  14.6 us (2%)
    pallas_call x7, Pallas kernels, block(): pl.pallas_call(functools.partial(block_body, n, with_left, with_pair), gr...  238 us
    ppermute x15, waiting for transfers between devices, swap(): return lax.ppermute(x, 'dap', [(i, i ^ bits) for i in range(n)])  149 us
    pallas_call x7, Pallas kernels, project(): pl.pallas_call(project_body, grid=(rows // ROWS, cols // 256), in_specs=[...  104 us
    pallas_call x2, Pallas kernels, incoming(): pl.pallas_call(incoming_body, grid=(CH // block,), in_specs=[pl.BlockSpec...  34.5 us
    pallas_call x2, Pallas kernels, finish(): pl.pallas_call(functools.partial(finish_body, n * part), grid=(rows // RO...  28.4 us
    ppermute x15, starting transfers between devices, swap(): return lax.ppermute(x, 'dap', [(i, i ^ bits) for i in range(n)])  14.6 us
  transfers between devices with their start and end apart: 15, of which 4 were waited for; matrix products, arithmetic and copies ran while one was open for 2% of the time, Pallas kernels for 44%

profile of v4, /device:TPU:0, one launch (start us, length us, event | category | flops | bytes accessed | tf_op | source)
XLA Modules:
  0.0 594.9 jit_solution(3051978820984767805)
XLA Ops:
  2.5 4.7 slice.134
  13.5 23.8 %project.7 = (bf16[128,256,512]{2,1,0:T(8,128)(2,1)}, bf16[4,256,128,128]{3,2,1,0:T(8,128)(2,1)}, bf16[4,256,128,128]{3,2,1,0:T(8,128)(2,1)}, bf16[128,64,512]{2,1,0:T(8,128)(2,1)}) custom-call(s32[1]{0:T(128)} %bitcast.g_ref, bf16[64,512,128]{2,1,0:T(8,128)(2,1)} %z_ref.1, f32[64,512]{1,0:T(8,128)} %pad_maximum_fusion.2.m_ref.refs_4_, ...), custom_call_target="tpu_custom_call" | custom-call | flops 17179869184 | bytes 39321600 | tf_op jit(solution)/shard_map/project/pallas_call | solution.py:108
  47.2 87.7 %collective-permute-done.5 = bf16[64,512]{0,1:T(8,128)(2,1)S(1)} collective-permute-done((bf16[64,512]{0,1:T(8,128)(2,1)S(1)}, bf16[64,512]{0,1:T(8,128)(2,1)S(1)}, u32[]{:S(2)}, u32[]{:S(2)}) %collective-permute-start.5) | collective-permute-done | bytes 65568 | tf_op jit(solution)/shard_map/ppermute | solution.py:444
  134.9 2.7 collective-permute-start.7
  137.8 3.3 collective-permute-done.7
  144.3 22.8 %block.7 = (bf16[4,128,256,128]{3,2,1,0:T(8,128)(2,1)}, bf16[4,80,128,128]{3,2,1,0:T(8,128)(2,1)}, bf16[4,80,128,128]{3,2,1,0:T(8,128)(2,1)}, bf16[128,256,128]{2,1,0:T(8,128)(2,1)}) custom-call(s32[1]{0:T(128)} %bitcast.1.h_ref, bf16[128,256,512]{2,1,0:T(8,128)(2,1)} %get-tuple-element.86.a_ref.refs_0_, bf16[128,64,512]{2,1,0:T(8,128)(2,1)} %get-tuple-element.87.refs_0_, ...), custom_call_target="tpu_custom_call" | custom-call | flops 4294967296 | bytes 13107200 | tf_op jit(solution)/shard_map/block/pallas_call | solution.py:329
  167.1 13.3 %project.8 = (bf16[128,256,512]{2,1,0:T(8,128)(2,1)}, bf16[4,256,128,128]{3,2,1,0:T(8,128)(2,1)}, bf16[4,256,128,128]{3,2,1,0:T(8,128)(2,1)}, bf16[128,64,512]{2,1,0:T(8,128)(2,1)}) custom-call(s32[1]{0:T(128)} %bitcast.g_ref, bf16[32,512,128]{2,1,0:T(8,128)(2,1)} %collective-permute-done.z_ref, ...), custom_call_target="tpu_custom_call", output_to_operand_aliasing={{0}: (6, {}), {1}: (7, {}), {2}: (8, {})} | custom-call | flops 8589934592 | bytes 19660800 | tf_op jit(solution)/shard_map/project/pallas_call | solution.py:108
  180.4 13.3 %project.9 = (bf16[128,256,512]{2,1,0:T(8,128)(2,1)}, bf16[4,256,128,128]{3,2,1,0:T(8,128)(2,1)}, bf16[4,256,128,128]{3,2,1,0:T(8,128)(2,1)}, bf16[128,64,512]{2,1,0:T(8,128)(2,1)}) custom-call(s32[1]{0:T(128)} %bitcast.g_ref, ...), custom_call_target="tpu_custom_call", output_to_operand_aliasing={{0}: (6, {}), {1}: (7, {}), {2}: (8, {}), {3}: (9, {})} | custom-call | flops 8589934592 | bytes 19660800 | tf_op jit(solution)/shard_map/project/pallas_call | solution.py:108
  196.7 22.1 %block.8 = (bf16[4,128,256,128]{3,2,1,0:T(8,128)(2,1)}, bf16[128,256,128]{2,1,0:T(8,128)(2,1)}) custom-call(s32[1]{0:T(128)} %bitcast.1.h_ref, bf16[128,256,512]{2,1,0:T(8,128)(2,1)} %get-tuple-element.99.a_ref.refs_0_, bf16[128,64,512]{2,1,0:T(8,128)(2,1)} %get-tuple-element.87.refs_0_, ...), custom_call_target="tpu_custom_call", output_to_operand_aliasing={{0}: (14, {}), {1}: (15, {})} | custom-call | flops 4294967296 | bytes 13107200 | tf_op jit(solution)/shard_map/block/pallas_call | solution.py:329
  218.9 28.8 %block.9 = (bf16[4,128,256,128]{3,2,1,0:T(8,128)(2,1)}, bf16[4,80,128,128]{3,2,1,0:T(8,128)(2,1)}, bf16[4,80,128,128]{3,2,1,0:T(8,128)(2,1)}) custom-call(s32[1]{0:T(128)} %bitcast.1.h_ref, bf16[128,256,512]{2,1,0:T(8,128)(2,1)} %get-tuple-element.99.a_ref.refs_0_, ...), custom_call_target="tpu_custom_call", output_to_operand_aliasing={{0}: (14, {}), {1}: (15, {}), {2}: (16, {})} | custom-call | flops 8589934592 | bytes 26214400 | tf_op jit(solution)/shard_map/block/pallas_call | solution.py:329
  247.7 39.3 %collective-permute-done.2.z_ref = bf16[32,512,128]{2,1,0:T(8,128)(2,1)S(1)} collective-permute-done((bf16[32,512,128]{2,1,0:T(8,128)(2,1)}, bf16[32,512,128]{2,1,0:T(8,128)(2,1)S(1)}, u32[]{:S(2)}, u32[]{:S(2)}) %collective-permute-start.2) | collective-permute-done | bytes 4194336 | tf_op jit(solution)/shard_map/ppermute | solution.py:444
  288.9 13.3 %project.10 = (bf16[128,256,512]{2,1,0:T(8,128)(2,1)}, bf16[4,256,128,128]{3,2,1,0:T(8,128)(2,1)}, bf16[4,256,128,128]{3,2,1,0:T(8,128)(2,1)}, bf16[128,64,512]{2,1,0:T(8,128)(2,1)}) custom-call(s32[1]{0:T(128)} %bitcast.g_ref, bf16[32,512,128]{2,1,0:T(8,128)(2,1)} %copy-done.2, ...), custom_call_target="tpu_custom_call", output_to_operand_aliasing={{0}: (6, {}), {1}: (7, {}), {2}: (8, {})} | custom-call | flops 8589934592 | bytes 19660800 | tf_op jit(solution)/shard_map/project/pallas_call | solution.py:108
  302.3 13.3 %project.11 = (bf16[128,256,512]{2,1,0:T(8,128)(2,1)}, bf16[4,256,128,128]{3,2,1,0:T(8,128)(2,1)}, bf16[4,256,128,128]{3,2,1,0:T(8,128)(2,1)}, bf16[128,64,512]{2,1,0:T(8,128)(2,1)}) custom-call(s32[1]{0:T(128)} %bitcast.g_ref, ...), custom_call_target="tpu_custom_call", output_to_operand_aliasing={{0}: (6, {}), {1}: (7, {}), {2}: (8, {}), {3}: (9, {})} | custom-call | flops 8589934592 | bytes 19660800 | tf_op jit(solution)/shard_map/project/pallas_call | solution.py:108
  318.5 34.1 %block.10 = (bf16[4,128,256,128]{3,2,1,0:T(8,128)(2,1)}, bf16[128,256,128]{2,1,0:T(8,128)(2,1)}) custom-call(s32[1]{0:T(128)} %bitcast.1.h_ref, bf16[128,256,512]{2,1,0:T(8,128)(2,1)} %get-tuple-element.118.a_ref.refs_0_, bf16[128,64,512]{2,1,0:T(8,128)(2,1)} %get-tuple-element.87.refs_0_, ...), custom_call_target="tpu_custom_call", output_to_operand_aliasing={{0}: (16, {}), {1}: (17, {})} | custom-call | flops 8589934592 | bytes 26214400 | tf_op jit(solution)/shard_map/block/pallas_call | solution.py:329
  352.7 37.3 %block.11 = (bf16[4,128,256,128]{3,2,1,0:T(8,128)(2,1)}, bf16[4,80,128,128]{3,2,1,0:T(8,128)(2,1)}, bf16[4,80,128,128]{3,2,1,0:T(8,128)(2,1)}) custom-call(s32[1]{0:T(128)} %bitcast.1.h_ref, bf16[128,256,512]{2,1,0:T(8,128)(2,1)} %get-tuple-element.118.a_ref.refs_0_, ...), custom_call_target="tpu_custom_call", output_to_operand_aliasing={{0}: (14, {}), {1}: (15, {}), {2}: (16, {})} | custom-call | flops 12884901888 | bytes 39321600 | tf_op jit(solution)/shard_map/block/pallas_call | solution.py:329
  390.0 18.7 %collective-permute-done.8.z_ref = bf16[32,512,128]{2,1,0:T(8,128)(2,1)S(1)} collective-permute-done((bf16[32,512,128]{2,1,0:T(8,128)(2,1)}, bf16[32,512,128]{2,1,0:T(8,128)(2,1)S(1)}, u32[]{:S(2)}, u32[]{:S(2)}) %collective-permute-start.8) | collective-permute-done | bytes 4194336 | tf_op jit(solution)/shard_map/ppermute | solution.py:444
  410.7 13.2 %project.12 = (bf16[128,256,512]{2,1,0:T(8,128)(2,1)}, bf16[4,256,128,128]{3,2,1,0:T(8,128)(2,1)}, bf16[4,256,128,128]{3,2,1,0:T(8,128)(2,1)}, bf16[128,64,512]{2,1,0:T(8,128)(2,1)}) custom-call(s32[1]{0:T(128)} %bitcast.g_ref, bf16[32,512,128]{2,1,0:T(8,128)(2,1)} %copy-done.1, ...), custom_call_target="tpu_custom_call", output_to_operand_aliasing={{0}: (6, {}), {1}: (7, {}), {2}: (8, {})} | custom-call | flops 8589934592 | bytes 19660800 | tf_op jit(solution)/shard_map/project/pallas_call | solution.py:108
  423.9 13.3 %project.13 = (bf16[128,256,512]{2,1,0:T(8,128)(2,1)}, bf16[4,256,128,128]{3,2,1,0:T(8,128)(2,1)}, bf16[4,256,128,128]{3,2,1,0:T(8,128)(2,1)}, bf16[128,64,512]{2,1,0:T(8,128)(2,1)}) custom-call(s32[1]{0:T(128)} %bitcast.g_ref, ...), custom_call_target="tpu_custom_call", output_to_operand_aliasing={{0}: (6, {}), {1}: (7, {}), {2}: (8, {}), {3}: (9, {})} | custom-call | flops 8589934592 | bytes 19660800 | tf_op jit(solution)/shard_map/project/pallas_call | solution.py:108
  437.3 46.7 %block.12 = (bf16[4,128,256,128]{3,2,1,0:T(8,128)(2,1)}, bf16[128,256,128]{2,1,0:T(8,128)(2,1)}) custom-call(s32[1]{0:T(128)} %bitcast.1.h_ref, bf16[128,256,512]{2,1,0:T(8,128)(2,1)} %get-tuple-element.137.a_ref, bf16[128,64,512]{2,1,0:T(8,128)(2,1)} %get-tuple-element.87.refs_0_, ...), custom_call_target="tpu_custom_call", output_to_operand_aliasing={{0}: (18, {}), {1}: (19, {})} | custom-call | flops 12884901888 | bytes 39321600 | tf_op jit(solution)/shard_map/block/pallas_call | solution.py:329
  484.0 45.9 %block.13 = (bf16[4,128,256,128]{3,2,1,0:T(8,128)(2,1)}, bf16[4,80,128,128]{3,2,1,0:T(8,128)(2,1)}, bf16[4,80,128,128]{3,2,1,0:T(8,128)(2,1)}) custom-call(s32[1]{0:T(128)} %bitcast.1.h_ref, bf16[128,256,512]{2,1,0:T(8,128)(2,1)} %get-tuple-element.137.a_ref, ...), custom_call_target="tpu_custom_call", output_to_operand_aliasing={{0}: (14, {}), {1}: (15, {}), {2}: (16, {})} | custom-call | flops 17179869184 | bytes 52428800 | tf_op jit(solution)/shard_map/block/pallas_call | solution.py:329
  529.9 17.3 %incoming.2 = (f32[2,128,64,128]{3,2,1,0:T(8,128)}, f32[2,128,64,128]{3,2,1,0:T(8,128)}) custom-call(s32[1]{0:T(128)} %bitcast.1.h_ref, bf16[128,256,128]{2,1,0:T(8,128)(2,1)} %get-tuple-element.151.a_ref, bf16[4,128,256,128]{3,2,1,0:T(8,128)(2,1)} %get-tuple-element.149.b_ref), custom_call_target="tpu_custom_call" | custom-call | flops 2147483648 | bytes 41943040 | tf_op jit(solution)/shard_map/incoming/pallas_call | solution.py:140
  547.5 17.2 %incoming.3 = (f32[2,128,64,128]{3,2,1,0:T(8,128)}, f32[2,128,64,128]{3,2,1,0:T(8,128)}) custom-call(s32[1]{0:T(128)} %bitcast.1.h_ref, bf16[128,256,128]{2,1,0:T(8,128)(2,1)} %get-tuple-element.151.a_ref, bf16[4,128,256,128]{3,2,1,0:T(8,128)(2,1)} %get-tuple-element.149.b_ref), custom_call_target="tpu_custom_call" | custom-call | flops 2147483648 | bytes 41943040 | tf_op jit(solution)/shard_map/incoming/pallas_call | solution.py:140
  566.3 14.2 %finish.2.refs_0_ = bf16[64,512,128]{2,1,0:T(8,128)(2,1)} custom-call(s32[1]{0:T(128)} %bitcast.g_ref, f32[2,128,64,128]{3,2,1,0:T(8,128)} %get-tuple-element.152.o_ref, f32[2,128,64,128]{3,2,1,0:T(8,128)} %collective-permute-done.14.r_ref, bf16[4,80,128,128]{3,2,1,0:T(8,128)(2,1)} %get-tuple-element.156.zt_ref, ...), custom_call_target="tpu_custom_call" | custom-call | flops 2147483648 | bytes 29491200 | tf_op jit(solution)/shard_map/finish/pallas_call | solution.py:400
  580.5 14.2 %finish.3 = bf16[64,512,128]{2,1,0:T(8,128)(2,1)} custom-call(s32[1]{0:T(128)} %bitcast.g_ref, f32[2,128,64,128]{3,2,1,0:T(8,128)} %get-tuple-element.154.o_ref, f32[2,128,64,128]{3,2,1,0:T(8,128)} %collective-permute-done.13.r_ref, bf16[4,80,128,128]{3,2,1,0:T(8,128)(2,1)} %get-tuple-element.156.zt_ref, ...), custom_call_target="tpu_custom_call", output_to_operand_aliasing={{}: (9, {})} | custom-call | flops 2147483648 | bytes 29491200 | tf_op jit(solution)/shard_map/finish/pallas_call | solution.py:400
  (113 shorter events, 33.6 us)
Async XLA Ops:
  0.0 10.3 %copy-start.3 = (bf16[2,128,512]{2,1,0:T(8,128)(2,1)S(1)}, bf16[2,128,512]{2,1,0:T(8,128)(2,1)}, u32[]{:S(2)}) copy-start(bf16[2,128,512]{2,1,0:T(8,128)(2,1)} %param.13) | copy-start | bytes 786436
  1.1 9.5 %copy-start.6 = (bf16[2,512]{1,0:T(2,128)(2,1)S(1)}, bf16[2,512]{1,0:T(2,128)(2,1)}, u32[]{:S(2)}) copy-start(bf16[2,512]{1,0:T(2,128)(2,1)} %param.14) | copy-start | bytes 6148
  13.5 29.3 %copy-start.4 = (bf16[2,128,128]{2,1,0:T(8,128)(2,1)S(1)}, bf16[2,128,128]{2,1,0:T(8,128)(2,1)}, u32[]{:S(2)}) copy-start(bf16[2,128,128]{2,1,0:T(8,128)(2,1)} %param.18) | copy-start | bytes 196612
  13.5 29.4 %copy-start.5 = (bf16[2,128,128]{2,1,0:T(8,128)(2,1)S(1)}, bf16[2,128,128]{2,1,0:T(8,128)(2,1)}, u32[]{:S(2)}) copy-start(bf16[2,128,128]{2,1,0:T(8,128)(2,1)} %param.15) | copy-start | bytes 196612
  13.5 29.8 %copy-start.10 = (bf16[2,128]{1,0:T(2,128)(2,1)S(1)}, bf16[2,128]{1,0:T(2,128)(2,1)}, u32[]{:S(2)}) copy-start(bf16[2,128]{1,0:T(2,128)(2,1)} %param.19) | copy-start | bytes 1540
  13.5 29.9 %copy-start.11 = (bf16[2,128]{1,0:T(2,128)(2,1)S(1)}, bf16[2,128]{1,0:T(2,128)(2,1)}, u32[]{:S(2)}) copy-start(bf16[2,128]{1,0:T(2,128)(2,1)} %param.16) | copy-start | bytes 1540
  13.5 31.1 %copy-start.7 = (bf16[2,2,128]{2,1,0:T(2,128)(2,1)S(1)}, bf16[2,2,128]{2,1,0:T(2,128)(2,1)}, u32[]{:S(2)}) copy-start(bf16[2,2,128]{2,1,0:T(2,128)(2,1)} %param.17) | copy-start | bytes 3076
  37.3 105.6 %collective-permute-start.9 = (bf16[128,64,512]{2,1,0:T(8,128)(2,1)}, bf16[128,64,512]{2,1,0:T(8,128)(2,1)}, u32[]{:S(2)}, u32[]{:S(2)}) collective-permute-start(bf16[128,64,512]{2,1,0:T(8,128)(2,1)} %get-tuple-element.87.refs_0_), channel_id=1, source_target_pairs={{0,1},{1,0},{2,3},{3,2},{4,5},{5,4},{6,7},{7,6}} | collective-permute-start | bytes 25165832 | tf_op jit(solution)/shard_map/ppermute | solution.py:444
  38.2 129.0 %collective-permute-start = (bf16[32,512,128]{2,1,0:T(8,128)(2,1)}, bf16[32,512,128]{2,1,0:T(8,128)(2,1)}, u32[]{:S(2)}, u32[]{:S(2)}) collective-permute-start(bf16[32,512,128]{2,1,0:T(8,128)(2,1)} %slice.134), channel_id=1, source_target_pairs={{0,2},{1,3},{2,0},{3,1},{4,6},{5,7},{6,4},{7,5}} | collective-permute-start | bytes 12582920 | tf_op jit(solution)/shard_map/ppermute | solution.py:444
  40.7 139.7 %collective-permute-start.3 = (bf16[32,512,128]{2,1,0:T(8,128)(2,1)}, bf16[32,512,128]{2,1,0:T(8,128)(2,1)}, u32[]{:S(2)}, u32[]{:S(2)}) collective-permute-start(bf16[32,512,128]{2,1,0:T(8,128)(2,1)} %slice.134), channel_id=1, source_target_pairs={{0,4},{1,5},{2,6},{3,7},{4,0},{5,1},{6,2},{7,3}} | collective-permute-start | bytes 12582920 | tf_op jit(solution)/shard_map/ppermute | solution.py:444
  42.2 92.7 %collective-permute-start.5 = (bf16[64,512]{0,1:T(8,128)(2,1)S(1)}, bf16[64,512]{0,1:T(8,128)(2,1)S(1)}, u32[]{:S(2)}, u32[]{:S(2)}) collective-permute-start(bf16[64,512]{0,1:T(8,128)(2,1)S(1)} %convert_element_type.88), channel_id=1, source_target_pairs={{0,2},{1,3},{2,0},{3,1},{4,6},{5,7},{6,4},{7,5}} | collective-permute-start | bytes 196616 | tf_op jit(solution)/shard_map/ppermute | solution.py:444
  42.7 95.0 %collective-permute-start.6 = (bf16[64,512]{0,1:T(8,128)(2,1)S(1)}, bf16[64,512]{0,1:T(8,128)(2,1)S(1)}, u32[]{:S(2)}, u32[]{:S(2)}) collective-permute-start(bf16[64,512]{0,1:T(8,128)(2,1)S(1)} %convert_element_type.88), channel_id=1, source_target_pairs={{0,4},{1,5},{2,6},{3,7},{4,0},{5,1},{6,2},{7,3}} | collective-permute-start | bytes 196616 | tf_op jit(solution)/shard_map/ppermute | solution.py:444
  134.9 6.2 %collective-permute-start.7 = (bf16[64,512]{0,1:T(8,128)(2,1)S(1)}, bf16[64,512]{0,1:T(8,128)(2,1)S(1)}, u32[]{:S(2)}, u32[]{:S(2)}) collective-permute-start(bf16[64,512]{0,1:T(8,128)(2,1)S(1)} %convert_element_type.88), channel_id=1, source_target_pairs={{0,6},{1,7},{2,4},{3,5},{4,2},{5,3},{6,0},{7,1}} | collective-permute-start | bytes 196616 | tf_op jit(solution)/shard_map/ppermute | solution.py:444
  193.7 25.1 %collective-permute-start.10 = (bf16[128,64,512]{2,1,0:T(8,128)(2,1)}, bf16[128,64,512]{2,1,0:T(8,128)(2,1)}, u32[]{:S(2)}, u32[]{:S(2)}) collective-permute-start(bf16[128,64,512]{2,1,0:T(8,128)(2,1)} %get-tuple-element.100.refs_0_.refs_1_), channel_id=1, source_target_pairs={{0,1},{1,0},{2,3},{3,2},{4,5},{5,4},{6,7},{7,6}} | collective-permute-start | bytes 25165832 | tf_op jit(solution)/shard_map/ppermute | solution.py:444
  193.7 93.2 %collective-permute-start.2 = (bf16[32,512,128]{2,1,0:T(8,128)(2,1)}, bf16[32,512,128]{2,1,0:T(8,128)(2,1)S(1)}, u32[]{:S(2)}, u32[]{:S(2)}) collective-permute-start(bf16[32,512,128]{2,1,0:T(8,128)(2,1)} %slice.135), channel_id=1, source_target_pairs={{0,2},{1,3},{2,0},{3,1},{4,6},{5,7},{6,4},{7,5}} | collective-permute-start | bytes 12582920 | tf_op jit(solution)/shard_map/ppermute | solution.py:444
  195.2 107.0 %collective-permute-start.1 = (bf16[32,512,128]{2,1,0:T(8,128)(2,1)}, bf16[32,512,128]{2,1,0:T(8,128)(2,1)}, u32[]{:S(2)}, u32[]{:S(2)}) collective-permute-start(bf16[32,512,128]{2,1,0:T(8,128)(2,1)} %slice.135), channel_id=1, source_target_pairs={{0,4},{1,5},{2,6},{3,7},{4,0},{5,1},{6,2},{7,3}} | collective-permute-start | bytes 12582920 | tf_op jit(solution)/shard_map/ppermute | solution.py:444
  315.5 37.2 %collective-permute-start.11 = (bf16[128,64,512]{2,1,0:T(8,128)(2,1)}, bf16[128,64,512]{2,1,0:T(8,128)(2,1)}, u32[]{:S(2)}, u32[]{:S(2)}) collective-permute-start(bf16[128,64,512]{2,1,0:T(8,128)(2,1)} %get-tuple-element.119.refs_0_.refs_2_), channel_id=1, source_target_pairs={{0,1},{1,0},{2,3},{3,2},{4,5},{5,4},{6,7},{7,6}} | collective-permute-start | bytes 25165832 | tf_op jit(solution)/shard_map/ppermute | solution.py:444
  315.5 93.2 %collective-permute-start.8 = (bf16[32,512,128]{2,1,0:T(8,128)(2,1)}, bf16[32,512,128]{2,1,0:T(8,128)(2,1)S(1)}, u32[]{:S(2)}, u32[]{:S(2)}) collective-permute-start(bf16[32,512,128]{2,1,0:T(8,128)(2,1)} %collective-permute-done.z_ref), channel_id=1, source_target_pairs={{0,4},{1,5},{2,6},{3,7},{4,0},{5,1},{6,2},{7,3}} | collective-permute-start | bytes 12582920 | tf_op jit(solution)/shard_map/ppermute | solution.py:444
  317.0 106.9 %collective-permute-start.4 = (bf16[32,512,128]{2,1,0:T(8,128)(2,1)}, bf16[32,512,128]{2,1,0:T(8,128)(2,1)}, u32[]{:S(2)}, u32[]{:S(2)}) collective-permute-start(bf16[32,512,128]{2,1,0:T(8,128)(2,1)} %collective-permute-done.1.z_ref), channel_id=1, source_target_pairs={{0,2},{1,3},{2,0},{3,1},{4,6},{5,7},{6,4},{7,5}} | collective-permute-start | bytes 12582920 | tf_op jit(solution)/shard_map/ppermute | solution.py:444
  437.3 46.7 %collective-permute-start.12 = (bf16[128,64,512]{2,1,0:T(8,128)(2,1)}, bf16[128,64,512]{2,1,0:T(8,128)(2,1)}, u32[]{:S(2)}, u32[]{:S(2)}) collective-permute-start(bf16[128,64,512]{2,1,0:T(8,128)(2,1)} %get-tuple-element.138.refs_0_), channel_id=1, source_target_pairs={{0,1},{1,0},{2,3},{3,2},{4,5},{5,4},{6,7},{7,6}} | collective-permute-start | bytes 25165832 | tf_op jit(solution)/shard_map/ppermute | solution.py:444
  547.1 17.8 %collective-permute-start.14 = (f32[2,128,64,128]{3,2,1,0:T(8,128)}, f32[2,128,64,128]{3,2,1,0:T(8,128)}, u32[]{:S(2)}, u32[]{:S(2)}) collective-permute-start(f32[2,128,64,128]{3,2,1,0:T(8,128)} %get-tuple-element.158), channel_id=1, source_target_pairs={{0,1},{1,0},{2,3},{3,2},{4,5},{5,4},{6,7},{7,6}} | collective-permute-start | bytes 25165832 | tf_op jit(solution)/shard_map/ppermute | solution.py:444
  547.5 17.4 %copy-start.9 = (f32[128]{0:T(128)S(1)}, f32[128]{0:T(128)}, u32[]{:S(2)}) copy-start(f32[128]{0:T(128)} %get-tuple-element.186) | copy-start | bytes 1540
  547.5 18.1 %copy-start.8 = (f32[128]{0:T(128)S(1)}, f32[128]{0:T(128)}, u32[]{:S(2)}) copy-start(f32[128]{0:T(128)} %get-tuple-element.183) | copy-start | bytes 1540
  564.8 15.7 %collective-permute-start.13 = (f32[2,128,64,128]{3,2,1,0:T(8,128)}, f32[2,128,64,128]{3,2,1,0:T(8,128)}, u32[]{:S(2)}, u32[]{:S(2)}) collective-permute-start(f32[2,128,64,128]{3,2,1,0:T(8,128)} %get-tuple-element.155), channel_id=1, source_target_pairs={{0,1},{1,0},{2,3},{3,2},{4,5},{5,4},{6,7},{7,6}} | collective-permute-start | bytes 25165832 | tf_op jit(solution)/shard_map/ppermute | solution.py:444
  (3 other events, 9.6 us)
